TPU v7x, 256 devices: a whole 4x4x8 slice. The times are simulated.
256 devices in a mesh: lat: 2 (over x_hi), lon: 2 (over x_lo), lev: 64 (over z, y, core).
Axes of the slice: x: 4 (x_hi: 2, x_lo: 2; x = x_hi * 2 + x_lo), y: 4, z: 8, core: 2. Of those that a mesh axis runs over, the one named last changes fastest.
Arguments:
- along_axis_flow: bfloat16 [640, 4, 32, 1440], P(('lat', 'lev'), None, None, 'lon'), may hold values from -6 to 6
- poleward_flow: bfloat16 [640, 4, 32, 1440], P(('lat', 'lev'), None, None, 'lon'), may hold values from -6 to 6
- warmth_departure: bfloat16 [640, 4, 32, 1440], P(('lat', 'lev'), None, None, 'lon'), may hold values from -6 to 6
- validity_indicator: int32 [640, 32, 1440], P(('lat', 'lev'), None, 'lon'), may hold values from 0 to 1
- layer_depth_span: float32 [32], replicated, may hold values from 0.3 to 3
- desired_circulation_norm: float32 [640, 4, 32], P(('lat', 'lev')), may hold values from -4 to 4
Outputs:
- psi_norm: float32 [640, 4, 32], P(('lat', 'lev'))
- heat_cospec: float32 [720, 640, 128], P('lon', ('lat', 'lev'))
- momentum_cospec: float32 [720, 640, 128], P('lon', ('lat', 'lev'))
- budget_penalty: float32 [], replicated
All inputs are finite; a program needn't handle non-finite values. Where the computation divides by a largest or mean magnitude, that divisor is 1e-20 or more.
Results may differ from a plain program's by a relative error of at most 0.0033.
Values may be sent and summed in bfloat16 or wider, within the bound.
No kernel may reach another device: no remote copies, remote signals or barrier semaphores. Data moves between devices by JAX's collectives and lax.ppermute only.
A program may use at most 64 MiB of HBM per device.

v0:
```python
import functools
import math

import jax
import jax.numpy as jnp
import numpy as np
from jax import lax
from jax.experimental import pallas as pl
from jax.experimental.pallas import tpu as pltpu
from jax.sharding import Mesh
from jax.sharding import PartitionSpec as P


MERIDIANS = 1440
ORDERS = 720
PADDED = 184
LAT_LEV = ("lat", "lev_0", "lev_1", "lev_2")
INNER = ("lev_1", "lev_2")
OUTER = "lev_0"
EPSILON = 1e-06
GROUPS = ((0,), (1, 2), (3, 4))
F32 = jnp.float32
BF16 = jnp.bfloat16
MIB = 1024 * 1024
CONTRACT = (((1,), (1,)), ((), ()))
SMEM = pl.BlockSpec(memory_space=pltpu.SMEM)
VMEM = pl.BlockSpec(memory_space=pltpu.VMEM)
HBM = pl.BlockSpec(memory_space=pltpu.HBM)
ANY = pl.BlockSpec(memory_space=pl.ANY)


def half_table(lon):
    order = np.arange(1, ORDERS + 1, dtype=np.int64)
    turns = (order[:, None] * np.arange(lon, dtype=np.int64)[None, :]) % MERIDIANS
    angle = turns.astype(np.float32) * np.float32(2.0 * math.pi / MERIDIANS)
    both = np.stack([np.cos(angle), np.sin(angle)]).reshape(2, 2, ORDERS // 4, 2, lon)
    rows = np.zeros((2, 2, 2, PADDED, lon), np.float32)
    rows[:, :, :, : ORDERS // 4] = both.transpose(1, 3, 0, 2, 4)
    return rows.reshape(2, 2, 2 * PADDED, lon)


def params(mib):
    return pltpu.CompilerParams(vmem_limit_bytes=mib * MIB)


def keep_of(mask):
    return mask.astype(F32).astype(BF16)


def first_kernel(half_ref, u_ref, v_ref, t_ref, m_ref, o_ref, sums_ref, us, vs, ts, masks, sems):
    rows, samples, levels, lon = vs.shape
    part = samples // 2
    size = part * levels
    far = 1 - half_ref[0]
    at = pl.ds(far * part, part)
    copies = []
    for j in range(rows):
        copies.append(
            [
                pltpu.make_async_copy(m_ref.at[j], masks.at[j], sems.at[j, 0]),
                pltpu.make_async_copy(v_ref.at[j], vs.at[j], sems.at[j, 1]),
            ]
        )
    extra = [
        pltpu.make_async_copy(u_ref.at[0, at], us, sems.at[0, 2]),
        pltpu.make_async_copy(t_ref.at[0, at], ts, sems.at[0, 3]),
    ]
    for group in (copies[0], extra, *copies[1:]):
        for c in group:
            c.start()
    ones = jnp.ones((8, lon), BF16)
    for j in range(rows):
        for c in copies[j]:
            c.wait()
        keep = keep_of(masks[j])
        v = (vs[j] * keep[None]).reshape(samples * levels, lon)
        sums_ref[j : j + 1, :] = lax.dot_general(ones, v, CONTRACT, preferred_element_type=F32)[0:1]
        full = jnp.broadcast_to(keep[None], (samples, levels, lon)).reshape(samples * levels, lon)
        sums_ref[rows + j : rows + j + 1, :] = lax.dot_general(
            ones, full, CONTRACT, preferred_element_type=F32
        )[0:1]
    for c in extra:
        c.wait()
    keep = keep_of(masks[0])[None]
    for f, field in enumerate((ts[...], us[...], vs[0, at])):
        o_ref[0, f * size : (f + 1) * size, :] = (field * keep).reshape(size, lon)


def first_part(half, u, v, t, mask):
    rows, samples, levels, lon = v.shape
    part = samples // 2
    return pl.pallas_call(
        first_kernel,
        out_shape=(
            jax.ShapeDtypeStruct((1, 3 * part * levels, lon), BF16),
            jax.ShapeDtypeStruct((2 * rows, samples * levels), F32),
        ),
        in_specs=[SMEM, HBM, HBM, HBM, HBM],
        out_specs=(VMEM, VMEM),
        scratch_shapes=[
            pltpu.VMEM((part, levels, lon), BF16),
            pltpu.VMEM((rows, samples, levels, lon), BF16),
            pltpu.VMEM((part, levels, lon), BF16),
            pltpu.VMEM((rows, levels, lon), jnp.int32),
            pltpu.SemaphoreType.DMA((rows, 4)),
        ],
        compiler_params=params(60),
        name="sums",
    )(half, u, v, t, mask)


def send_kernel(groups, half_ref, u_ref, v_ref, t_ref, m_ref, _, *rest):
    n = len(groups)
    far_refs, near_refs = rest[: n - 1], rest[n - 1 : 2 * n - 1]
    us, vs, ts, masks, fars, nears, sems, out_sems = rest[2 * n - 1 :]
    rows, samples, levels, lon = vs.shape
    part = samples // 2
    size = part * levels
    near = half_ref[0]
    far = 1 - near
    copies = []
    for j in range(rows):
        group = [
            pltpu.make_async_copy(m_ref.at[j], masks.at[j], sems.at[j, 0]),
            pltpu.make_async_copy(v_ref.at[j], vs.at[j], sems.at[j, 1]),
            pltpu.make_async_copy(u_ref.at[j], us.at[j], sems.at[j, 2]),
            pltpu.make_async_copy(t_ref.at[j], ts.at[j], sems.at[j, 3]),
        ]
        for c in group:
            c.start()
        copies.append(group)
    done = []
    for g, group in enumerate(groups):
        for i, j in enumerate(group):
            for c in copies[j]:
                c.wait()
            keep = keep_of(masks[j])
            for k, (where, box) in enumerate(((far, fars), (near, nears))):
                if k == 0 and g == 0:
                    continue
                ref = far_refs[g - 1] if k == 0 else near_refs[g]
                for f, field in enumerate((ts, us, vs)):
                    mine = field[j, pl.ds(where * part, part)] * keep[None]
                    box[j, f * size : (f + 1) * size, :] = mine.reshape(size, lon)
                c = pltpu.make_async_copy(box.at[j], ref.at[i], out_sems.at[j, k])
                c.start()
                done.append(c)
    for c in done:
        c.wait()


def send(half, u, v, t, mask, after, groups):
    rows, samples, levels, lon = v.shape
    part = samples // 2
    unit = 3 * part * levels
    n = len(groups)
    packed = [jax.ShapeDtypeStruct((len(g), unit, lon), BF16) for g in groups]
    return pl.pallas_call(
        lambda *refs: send_kernel(groups, *refs),
        out_shape=(
            *packed[1:],
            *packed,
        ),
        in_specs=[SMEM, HBM, HBM, HBM, HBM, ANY],
        out_specs=(HBM,) * (2 * n - 1),
        scratch_shapes=[
            pltpu.VMEM((rows, samples, levels, lon), BF16),
            pltpu.VMEM((rows, samples, levels, lon), BF16),
            pltpu.VMEM((rows, samples, levels, lon), BF16),
            pltpu.VMEM((rows, levels, lon), jnp.int32),
            pltpu.VMEM((rows, unit, lon), BF16),
            pltpu.VMEM((rows, unit, lon), BF16),
            pltpu.SemaphoreType.DMA((rows, 4)),
            pltpu.SemaphoreType.DMA((rows, 2)),
        ],
        compiler_params=params(60),
        name="send",
    )(half, u, v, t, mask, after)


def wave_kernel(half_ref, table_ref, own_ref, got_ref, _, *o_refs, flips):
    n = table_ref.shape[2] // 2
    scale = 2.0 / (MERIDIANS * MERIDIANS)
    for i in range(got_ref.shape[0]):
        own, got = own_ref[i].astype(F32), got_ref[i].astype(F32)
        for p, mixed in enumerate(((own - got).astype(BF16), (own + got).astype(BF16))):
            x = jnp.concatenate([mixed, mixed[2 * mixed.shape[0] // 3 :]])
            w = x.shape[0] // 2
            for flip, o_ref in zip(flips, o_refs):
                table = table_ref[1 - half_ref[0] if flip else half_ref[0], p]
                c = lax.dot_general(table, x, CONTRACT, preferred_element_type=F32)
                both = c[:n, :w] * c[:n, w:] + c[n:, :w] * c[n:, w:]
                o_ref[i, p] = (scale * both).astype(o_ref.dtype)


def waves(half, table, own, got, after, *flips):
    rows, cols, _ = got.shape
    shape = (rows, 2, PADDED, 2 * cols // 3)
    return pl.pallas_call(
        functools.partial(wave_kernel, flips=flips),
        out_shape=tuple(jax.ShapeDtypeStruct(shape, BF16 if f else F32) for f in flips),
        in_specs=[SMEM, VMEM, VMEM, VMEM, ANY],
        out_specs=(VMEM,) * len(flips),
        compiler_params=params(16),
        name="waves",
    )(half, table, own, got, after)


def join_kernel(first, parts, half_ref, *refs):
    own_refs, got_refs = refs[:parts], refs[parts : 2 * parts]
    heat_ref, mom_ref, heat, mom, sems = refs[-5:]
    copies = []
    at = 0
    for own_ref, got_ref in zip(own_refs, got_refs):
        for i in range(own_ref.shape[0]):
            zero = half_ref[0] == 0
            for p in range(2):
                own = own_ref[i, p]
                got = got_ref[i, p].astype(F32)
                a = jnp.where(zero, own, got)
                b = jnp.where(zero, got, own)
                w = own.shape[1] // 2
                low = lax.broadcasted_iota(jnp.int32, own.shape, 1) < w
                n = heat.shape[1] // 2
                every = pl.ds(p, n, stride=2)
                heat[at, every, :] = jnp.where(low, a, pltpu.roll(b, w, 1))[:n]
                mom[at, every, :] = jnp.where(low, pltpu.roll(a, w, 1), b)[:n]
            for k, (x, ref) in enumerate(((heat, heat_ref), (mom, mom_ref))):
                c = pltpu.make_async_copy(x.at[at], ref.at[first + at], sems.at[at, k])
                c.start()
                copies.append(c)
            at += 1
    for c in copies:
        c.wait()


def join(half, own, got, outs, rows, total):
    n, width = ORDERS // 2, own[0].shape[3]
    shape = jax.ShapeDtypeStruct((total, n, width), F32)
    parts = len(own)
    args = (half, *own, *got)
    specs = [SMEM] + [VMEM] * (2 * parts)
    extra = {}
    if outs is not None:
        extra = {"input_output_aliases": {len(args): 0, len(args) + 1: 1}}
        args += outs
        specs += [HBM, HBM]
    return pl.pallas_call(
        lambda *refs: join_kernel(rows[0], parts, *refs),
        out_shape=(shape, shape),
        in_specs=specs,
        out_specs=(HBM, HBM),
        scratch_shapes=[
            pltpu.VMEM((len(rows), n, width), F32),
            pltpu.VMEM((len(rows), n, width), F32),
            pltpu.SemaphoreType.DMA((len(rows), 2)),
        ],
        compiler_params=params(8),
        name="join",
        **extra,
    )(*args)


def cosines(first, rows, total):
    index = lax.broadcasted_iota(jnp.int32, (rows, 1), 0) + first
    return jnp.cos(((index.astype(F32) + 0.5) / total - 0.5) * math.pi)


def weight_of(first, rows, total):
    latitude = ((np.arange(first, first + rows) + 0.5) / total - 0.5) * math.pi
    return float(np.sum(np.cos(latitude)))


def weigh_kernel(total, place_ref, own_ref, lon_ref, depth_ref, d_ref, o_ref):
    rows, samples, levels = d_ref.shape
    band = place_ref[0] // 128 * 64 + place_ref[0] % 64
    depth = depth_ref[...]
    spread = jnp.concatenate([depth] * samples, axis=1)
    kept = own_ref[rows : 2 * rows] + lon_ref[rows : 2 * rows]
    mean = (own_ref[0:rows] + lon_ref[0:rows]) / jnp.maximum(kept, 1.0)
    weighted = mean * cosines(band * rows, rows, total) * spread
    for p in range(o_ref.shape[0]):
        o_ref[p, 0:rows, :] = weighted
        for b in range(samples):
            o_ref[p, 8 : 8 + rows, b * levels : (b + 1) * levels] = d_ref[:, b, :]


def band_kernel(total, rows, levels, place_ref, g_ref, mine_ref, s_ref, w_ref):
    peers, _, width = g_ref.shape
    span = peers * rows
    lane = lax.broadcasted_iota(jnp.int32, (1, width), 1) % levels
    so_far = jnp.zeros((1, width), F32)
    for p in range(peers):
        for r in range(rows):
            so_far = so_far + g_ref[p, r : r + 1, :]
            w_ref[p * rows + r : p * rows + r + 1, :] = so_far
            w_ref[span + p * rows + r : span + p * rows + r + 1, :] = g_ref[p, 8 + r : 9 + r, :]
    run = w_ref[0:span, :]
    step = 1
    while step < levels:
        run = run + jnp.where(lane >= step, pltpu.roll(run, step, 1), 0.0)
        step *= 2
    want = w_ref[span:, :]
    block = place_ref[0] // 128 * 8 + place_ref[0] % 64 // 8
    cosine = cosines(block * span, span, total)
    stats = (
        run[span - 1 : span],
        jnp.max(run, axis=0, keepdims=True),
        jnp.min(run, axis=0, keepdims=True),
        jnp.sum(cosine * run, axis=0, keepdims=True),
        jnp.sum(cosine * run * run, axis=0, keepdims=True),
        jnp.sum(cosine * want, axis=0, keepdims=True),
        jnp.sum(cosine * run * want, axis=0, keepdims=True),
        jnp.sum(cosine * want * want, axis=0, keepdims=True),
    )
    for p in range(s_ref.shape[0]):
        for i, stat in enumerate(stats):
            s_ref[p, i : i + 1, :] = stat
    w_ref[0:span, :] = run
    for p in range(peers):

        @pl.when(place_ref[0] % 8 == p)
        def _():
            mine_ref[...] = w_ref[p * rows : (p + 1) * rows, :]


def add_block(so_far, block, weight):
    s, hi, lo, run1, run2, want1, cross, want2 = block
    if so_far is None:
        return block
    off = so_far[0]
    return (
        off + s,
        jnp.maximum(so_far[1], off + hi),
        jnp.minimum(so_far[2], off + lo),
        so_far[3] + (run1 + off * weight),
        so_far[4] + (run2 + 2.0 * off * run1 + off * off * weight),
        so_far[5] + want1,
        so_far[6] + (cross + off * want1),
        so_far[7] + want2,
    )


def half_kernel(total, span, place_ref, mine_ref, s_ref, own_ref, half_ref):
    blocks = s_ref.shape[0]
    here = place_ref[0] % 64 // 8
    north = place_ref[0] // 128 == 1
    stats = None
    offset = jnp.zeros((1, s_ref.shape[2]), F32)
    for z in range(blocks):
        if z:
            offset = jnp.where(here == z, stats[0], offset)
        weights = [weight_of((h * blocks + z) * span, span, total) for h in range(2)]
        weight = jnp.where(north, weights[1], weights[0])
        stats = add_block(stats, [s_ref[z, i : i + 1, :] for i in range(8)], weight)
    own_ref[...] = mine_ref[...] + offset
    for i, stat in enumerate(stats):
        half_ref[i : i + 1, :] = stat


def finish_kernel(total, place_ref, own_ref, near_ref, far_ref, psi_ref, loss_ref):
    _, samples, levels = psi_ref.shape
    north = place_ref[0] // 128 == 1
    near = near_ref[...]
    far = far_ref[...]
    south_half = jnp.where(north, far, near)
    north_half = jnp.where(north, near, far)
    weight = weight_of(total // 2, total // 2, total)
    stats = add_block(
        [south_half[i : i + 1] for i in range(8)], [north_half[i : i + 1] for i in range(8)], weight
    )
    peak = jnp.max(jnp.maximum(jnp.abs(stats[1]), jnp.abs(stats[2])), axis=1, keepdims=True)
    scale = peak + EPSILON
    psi = (own_ref[...] + jnp.where(north, far[0:1], 0.0)) / scale
    for b in range(samples):
        psi_ref[:, b, :] = psi[:, b * levels : (b + 1) * levels]
    a, b, c = (jnp.sum(stats[i], axis=1, keepdims=True) for i in (4, 6, 7))
    loss = (a / scale / scale - 2.0 * (b / scale) + c) / (samples * levels * total)
    loss_ref[...] = jnp.broadcast_to(loss, loss_ref.shape)


def small(body, out_shape, *args, scratch=(), after=None):
    many = isinstance(out_shape, tuple)
    specs = [SMEM] + [VMEM] * (len(args) - 1)
    if after is not None:
        plain, count = body, len(args)
        body = lambda *refs: plain(*refs[:count], *refs[count + 1 :])
        args += (after,)
        specs.append(ANY)
    return pl.pallas_call(
        body,
        out_shape=out_shape,
        in_specs=specs,
        out_specs=(VMEM,) * len(out_shape) if many else VMEM,
        scratch_shapes=scratch,
        compiler_params=params(2),
    )(*args)


def all_of(x, axes):
    return lax.all_to_all(x, axes, split_axis=0, concat_axis=0, tiled=True)


def floats(*shape):
    return jax.ShapeDtypeStruct(shape, F32)


def per_device(u, v, t, mask, depth, desired):
    bands, samples, levels, lon = v.shape
    width = samples * levels
    total = bands * lax.axis_size(LAT_LEV)
    half = lax.axis_index("lon")[None].astype(jnp.int32)
    place = lax.axis_index(("lat", "lon", "lev_0", "lev_1", "lev_2"))[None].astype(jnp.int32)
    across = [(0, 1), (1, 0)]
    table = jnp.asarray(half_table(lon), BF16)

    def swap(x):
        return lax.ppermute(x, "lon", across)

    first, sums = first_part(half, u, v, t, mask)
    packed = send(half, u, v, t, mask, sums, GROUPS)
    rest, own = packed[: len(GROUPS) - 1], packed[len(GROUPS) - 1 :]
    got = [swap(first)]
    by_lon = swap(sums)
    got += [swap(x) for x in rest]

    peers = lax.axis_size(INNER)
    outer = lax.axis_size(OUTER)
    rows = small(
        lambda *refs: weigh_kernel(total, *refs),
        floats(peers, 16, width),
        place,
        sums,
        by_lon,
        depth[None],
        desired,
    )
    near_bands = all_of(rows, INNER)
    far0, near0 = waves(half, table, own[0], got[0], rows, True, False)
    span = bands * peers
    mine, stats = small(
        lambda *refs: band_kernel(total, bands, levels, *refs),
        (floats(bands, width), floats(outer, 8, width)),
        place,
        near_bands,
        scratch=[pltpu.VMEM((2 * span, width), F32)],
    )
    all_stats = all_of(stats, OUTER)
    mine, near_half = small(
        lambda *refs: half_kernel(total, span, *refs),
        (floats(bands, width), floats(8, width)),
        place,
        mine,
        all_stats,
    )
    far_half = lax.ppermute(near_half, ("lat", "lon"), [(i, 3 - i) for i in range(4)])
    far1, near1 = waves(half, table, own[1], got[1], stats, True, False)
    (far2,) = waves(half, table, own[2], got[2], near_half, True)
    (near2,) = waves(half, table, own[2], got[2], near_half, False)
    psi, loss = small(
        lambda *refs: finish_kernel(total, *refs),
        (floats(bands, samples, levels), floats(1, width)),
        place,
        mine,
        near_half,
        far_half,
        after=near2,
    )

    back = [swap(x) for x in (far0, far1, far2)]
    kept = [near0, near1, near2]
    outs = join(half, kept[:2], back[:2], None, GROUPS[0] + GROUPS[1], bands)
    outs = join(half, kept[2:], back[2:], outs, GROUPS[2], bands)
    heat, momentum = (jnp.transpose(x, (1, 0, 2)) for x in outs)
    return psi, heat, momentum, loss[0, 0]


def solution(mesh):
    torus = Mesh(
        mesh.devices.reshape(mesh.shape["lat"], mesh.shape["lon"], 8, 4, 2),
        ("lat", "lon", "lev_0", "lev_1", "lev_2"),
    )
    in_specs = (
        P(LAT_LEV, None, None, "lon"),
        P(LAT_LEV, None, None, "lon"),
        P(LAT_LEV, None, None, "lon"),
        P(LAT_LEV, None, "lon"),
        P(),
        P(LAT_LEV, None, None),
    )
    out_specs = (P(LAT_LEV, None, None), P("lon", LAT_LEV, None), P("lon", LAT_LEV, None), P())

    return jax.shard_map(
        per_device, mesh=torus, in_specs=in_specs, out_specs=out_specs, check_vma=False
    )
```

profile of v0, /device:TPU:6, one launch (start us, length us, event | category | flops | bytes accessed | tf_op | source)
XLA Modules:
  0.0 85.4 jit_solution(17463527828189194466)
XLA Ops:
  0.6 3.0 %sums.1 = (bf16[1,192,720]{2,1,0:T(8,128)(2,1)}, f32[10,128]{1,0:T(8,128)}) custom-call(s32[1]{0:T(128)} %bitcast.1.half_ref.refs_0_, bf16[5,4,32,720]{3,2,1,0:T(8,128)(2,1)} %refs_1_.1, bf16[5,4,32,720]{3,2,1,0:T(8,128)(2,1)} %refs_2_.1, bf16[5,4,32,720]{3,2,1,0:T(8,128)(2,1)} %refs_3_.1, s32[5,32,720]{2,1,0:T(8,128)} %refs_4_.3), custom_call_target="tpu_custom_call" | custom-call | tf_op jit(solution)/shard_map/sums/pallas_call | solution.py:92
  3.7 3.3 %send.1 = (bf16[2,192,720]{2,1,0:T(8,128)(2,1)}, bf16[2,192,720]{2,1,0:T(8,128)(2,1)}, bf16[1,192,720]{2,1,0:T(8,128)(2,1)}, bf16[2,192,720]{2,1,0:T(8,128)(2,1)}, bf16[2,192,720]{2,1,0:T(8,128)(2,1)}) custom-call(s32[1]{0:T(128)} %bitcast.1.half_ref.refs_0_, bf16[5,4,32,720]{3,2,1,0:T(8,128)(2,1)} %refs_1_.1, bf16[5,4,32,720]{3,2,1,0:T(8,128)(2,1)} %refs_2_.1, ...), custom_call_target="tpu_custom_call" | custom-call | tf_op jit(solution)/shard_map/send/pallas_call | solution.py:158
  7.0 0.9 %collective-permute-start.5 = (bf16[2,192,720]{2,1,0:T(8,128)(2,1)}, bf16[2,192,720]{2,1,0:T(8,128)(2,1)}, u32[]{:S(2)}, u32[]{:S(2)}) collective-permute-start(bf16[2,192,720]{2,1,0:T(8,128)(2,1)} %get-tuple-element.37), channel_id=1, source_target_pairs={{0,64},{64,0},{1,65},{65,1},{2,66},{66,2},{3,67},{67,3},{4,68},{68... | collective-permute-start | bytes 1658888 | tf_op jit(solution)/shard_map/ppermute | solution.py:418
  7.9 1.2 %collective-permute-start.2 = (bf16[2,192,720]{2,1,0:T(8,128)(2,1)}, bf16[2,192,720]{2,1,0:T(8,128)(2,1)S(1)}, u32[]{:S(2)}, u32[]{:S(2)}) collective-permute-start(bf16[2,192,720]{2,1,0:T(8,128)(2,1)} %get-tuple-element.31), channel_id=1, source_target_pairs={{0,64},{64,0},{1,65},{65,1},{2,66},{66,2},{3,67},{67,3},{4,68},{68... | collective-permute-start | bytes 1658888 | tf_op jit(solution)/shard_map/ppermute | solution.py:418
  9.1 0.8 collective-permute-start.4
  10.0 1.2 %collective-permute-start = (f32[10,128]{1,0:T(8,128)S(1)}, f32[10,128]{1,0:T(8,128)S(1)}, u32[]{:S(2)}, u32[]{:S(2)}) collective-permute-start(f32[10,128]{1,0:T(8,128)S(1)} %copy-done.4), channel_id=1, source_target_pairs={{0,64},{64,0},{1,65},{65,1},{2,66},{66,2},{3,67},{67,3},{4,68},{68... | collective-permute-start | bytes 15368 | tf_op jit(solution)/shard_map/ppermute | solution.py:418
  11.2 30.4 %collective-permute-done.refs_2_ = f32[10,128]{1,0:T(8,128)S(1)} collective-permute-done((f32[10,128]{1,0:T(8,128)S(1)}, f32[10,128]{1,0:T(8,128)S(1)}, u32[]{:S(2)}, u32[]{:S(2)}) %collective-permute-start) | collective-permute-done | bytes 5152 | tf_op jit(solution)/shard_map/ppermute | solution.py:418
  41.5 0.1 shard_map.102._
  41.6 9.9 %all_to_all.10.refs_1_ = f32[8,16,128]{2,1,0:T(8,128)S(1)} all-to-all(f32[8,16,128]{2,1,0:T(8,128)S(1)} %shard_map.102._), channel_id=1, replica_groups=mesh['lat'=2,'lon'=2,'lev_0'=8,'lev_1'=4,'lev_2'=2] {'lev_1','lev_2'}, dimensions={0} | all-to-all | bytes 131072 | tf_op jit(solution)/shard_map/all_to_all | solution.py:401
  51.5 0.5 shard_map.103
  52.0 16.3 %all_to_all.11.refs_2_ = f32[8,8,128]{2,1,0:T(8,128)S(1)} all-to-all(f32[8,8,128]{2,1,0:T(8,128)S(1)} %get-tuple-element.27._), channel_id=1, replica_groups=mesh['lat'=2,'lon'=2,'lev_0'=8,'lev_1'=4,'lev_2'=2] {'lev_0'}, dimensions={0} | all-to-all | bytes 65536 | tf_op jit(solution)/shard_map/all_to_all | solution.py:401
  68.4 1.1 %copy-done.2 = bf16[2,192,720]{2,1,0:T(8,128)(2,1)S(1)} copy-done((bf16[2,192,720]{2,1,0:T(8,128)(2,1)S(1)}, bf16[2,192,720]{2,1,0:T(8,128)(2,1)}, u32[]{:S(2)}) %copy-start.2) | copy-done | bytes 552984
  69.5 2.4 %waves.7 = (bf16[2,2,184,128]{3,2,1,0:T(8,128)(2,1)S(1)}, f32[2,2,184,128]{3,2,1,0:T(8,128)S(1)}) custom-call(s32[1]{0:T(128)} %bitcast.1.half_ref.refs_0_, bf16[2,2,368,720]{3,2,1,0:T(8,128)(2,1)S(1)} %copy-done, bf16[2,192,720]{2,1,0:T(8,128)(2,1)S(1)} %copy-done.2, bf16[2,192,720]{2,1,0:T(8,128)(2,1)} %collective-permute-done.5.got_ref, ...), custom_call_target="tpu_custom_call" | custom-call | tf_op jit(solution)/shard_map/waves/pallas_call | solution.py:199
  71.9 0.9 %collective-permute-start.7 = (bf16[2,2,184,128]{3,2,1,0:T(8,128)(2,1)S(1)}, bf16[2,2,184,128]{3,2,1,0:T(8,128)(2,1)S(1)}, u32[]{:S(2)}, u32[]{:S(2)}) collective-permute-start(bf16[2,2,184,128]{3,2,1,0:T(8,128)(2,1)S(1)} %get-tuple-element.40), channel_id=1, source_target_pairs={{0,64},{64,0},{1,65},{65,1},{2,66},{66,2},{3,67},{67,3},{4,68},{68... | collective-permute-start | bytes 565256 | tf_op jit(solution)/shard_map/ppermute | solution.py:418
  72.8 0.8 waves.5
  73.6 1.3 %collective-permute-start.3 = (bf16[2,2,184,128]{3,2,1,0:T(8,128)(2,1)S(1)}, bf16[2,2,184,128]{3,2,1,0:T(8,128)(2,1)S(1)}, u32[]{:S(2)}, u32[]{:S(2)}) collective-permute-start(bf16[2,2,184,128]{3,2,1,0:T(8,128)(2,1)S(1)} %waves.5), channel_id=1, source_target_pairs={{0,64},{64,0},{1,65},{65,1},{2,66},{66,2},{3,67},{67,3},{4,68},{68... | collective-permute-start | bytes 565256 | tf_op jit(solution)/shard_map/ppermute | solution.py:418
  74.9 1.7 %waves.6 = (bf16[1,2,184,128]{3,2,1,0:T(8,128)(2,1)S(1)}, f32[1,2,184,128]{3,2,1,0:T(8,128)S(1)}) custom-call(s32[1]{0:T(128)} %bitcast.1.half_ref.refs_0_, bf16[2,2,368,720]{3,2,1,0:T(8,128)(2,1)S(1)} %copy-done, bf16[1,192,720]{2,1,0:T(8,128)(2,1)S(1)} %copy-done.3, bf16[1,192,720]{2,1,0:T(8,128)(2,1)} %collective-permute-done.4.got_ref, ...), custom_call_target="tpu_custom_call" | custom-call | tf_op jit(solution)/shard_map/waves/pallas_call | solution.py:199
  76.7 0.9 %collective-permute-start.6 = (bf16[1,2,184,128]{3,2,1,0:T(8,128)(2,1)S(1)}, bf16[1,2,184,128]{3,2,1,0:T(8,128)(2,1)S(1)}, u32[]{:S(2)}, u32[]{:S(2)}) collective-permute-start(bf16[1,2,184,128]{3,2,1,0:T(8,128)(2,1)S(1)} %get-tuple-element.39), channel_id=1, source_target_pairs={{0,64},{64,0},{1,65},{65,1},{2,66},{66,2},{3,67},{67,3},{4,68},{68... | collective-permute-start | bytes 282632 | tf_op jit(solution)/shard_map/ppermute | solution.py:418
  77.6 1.1 %collective-permute-start.1 = (f32[8,128]{1,0:T(8,128)S(1)}, f32[8,128]{1,0:T(8,128)S(1)}, u32[]{:S(2)}, u32[]{:S(2)}) collective-permute-start(f32[8,128]{1,0:T(8,128)S(1)} %get-tuple-element.29._.refs_2_), channel_id=1, source_target_pairs={{0,192},{64,128},{128,64},{192,0},{1,193},{65,129},{129,65},{193,1... | collective-permute-start | bytes 12296 | tf_op jit(solution)/shard_map/ppermute | solution.py:456
  78.7 0.8 waves.4.refs_4_.refs_1_
  79.5 2.9 %collective-permute-done.1.refs_3_ = f32[8,128]{1,0:T(8,128)S(1)} collective-permute-done((f32[8,128]{1,0:T(8,128)S(1)}, f32[8,128]{1,0:T(8,128)S(1)}, u32[]{:S(2)}, u32[]{:S(2)}) %collective-permute-start.1) | collective-permute-done | bytes 4128 | tf_op jit(solution)/shard_map/ppermute | solution.py:456
  82.4 0.8 shard_map.105
  83.2 1.2 %join.2 = (f32[5,360,128]{2,1,0:T(8,128)}, f32[5,360,128]{2,1,0:T(8,128)}) custom-call(s32[1]{0:T(128)} %bitcast.1.half_ref.refs_0_, f32[1,2,184,128]{3,2,1,0:T(8,128)S(1)} %get-tuple-element.35.refs_1_, f32[2,2,184,128]{3,2,1,0:T(8,128)S(1)} %get-tuple-element.38.refs_2_, bf16[1,2,184,128]{3,2,1,0:T(8,128)(2,1)S(1)} %collective-permute-done.6.refs_3_, ...), custom_call_target="tpu_custom_call" | custom-call | tf_op jit(solution)/shard_map/join/pallas_call | solution.py:248
  84.4 1.0 %join.3 = (f32[5,360,128]{2,1,0:T(8,128)}, f32[5,360,128]{2,1,0:T(8,128)}) custom-call(s32[1]{0:T(128)} %bitcast.1.half_ref.refs_0_, f32[2,2,184,128]{3,2,1,0:T(8,128)S(1)} %waves.4.refs_4_.refs_1_, bf16[2,2,184,128]{3,2,1,0:T(8,128)(2,1)S(1)} %collective-permute-done.3.refs_2_, ...), custom_call_target="tpu_custom_call", output_to_operand_aliasing={{0}: (3, {}), {1}: (4, {})} | custom-call | tf_op jit(solution)/shard_map/join/pallas_call | solution.py:248
  (20 shorter events, 0.1 us)
Async XLA Ops:
  3.7 6.3 %copy-start.4 = (f32[10,128]{1,0:T(8,128)S(1)}, f32[10,128]{1,0:T(8,128)}, u32[]{:S(2)}) copy-start(f32[10,128]{1,0:T(8,128)} %get-tuple-element.25.refs_1_.refs_5_) | copy-start | bytes 15364
  3.7 37.8 %copy-start.5 = (f32[5,4,32]{2,1,0:T(4,128)S(1)}, f32[5,4,32]{2,1,0:T(4,128)}, u32[]{:S(2)}) copy-start(f32[5,4,32]{2,1,0:T(4,128)} %refs_4_.2) | copy-start | bytes 7684
  3.7 37.8 %copy-start.6 = (f32[32]{0:T(128)S(1)}, f32[32]{0:T(128)}, u32[]{:S(2)}) copy-start(f32[32]{0:T(128)} %param.11) | copy-start | bytes 388
  3.7 64.7 %copy-start = (bf16[2,2,368,720]{3,2,1,0:T(8,128)(2,1)S(1)}, bf16[2,2,368,720]{3,2,1,0:T(8,128)(2,1)}, u32[]{:S(2)}) copy-start(bf16[2,2,368,720]{3,2,1,0:T(8,128)(2,1)} %constant.29.clone.table_ref) | copy-start | bytes 6359044
  7.0 65.8 %copy-start.1 = (bf16[2,192,720]{2,1,0:T(8,128)(2,1)S(1)}, bf16[2,192,720]{2,1,0:T(8,128)(2,1)}, u32[]{:S(2)}) copy-start(bf16[2,192,720]{2,1,0:T(8,128)(2,1)} %get-tuple-element.30.own_ref) | copy-start | bytes 1658884
  7.0 61.3 %collective-permute-start.5 = (bf16[2,192,720]{2,1,0:T(8,128)(2,1)}, bf16[2,192,720]{2,1,0:T(8,128)(2,1)}, u32[]{:S(2)}, u32[]{:S(2)}) collective-permute-start(bf16[2,192,720]{2,1,0:T(8,128)(2,1)} %get-tuple-element.37), channel_id=1, source_target_pairs={{0,64},{64,0},{1,65},{65,1},{2,66},{66,2},{3,67},{67,3},{4,68},{68... | collective-permute-start | bytes 1658888 | tf_op jit(solution)/shard_map/ppermute | solution.py:418
  7.9 64.9 %collective-permute-start.2 = (bf16[2,192,720]{2,1,0:T(8,128)(2,1)}, bf16[2,192,720]{2,1,0:T(8,128)(2,1)S(1)}, u32[]{:S(2)}, u32[]{:S(2)}) collective-permute-start(bf16[2,192,720]{2,1,0:T(8,128)(2,1)} %get-tuple-element.31), channel_id=1, source_target_pairs={{0,64},{64,0},{1,65},{65,1},{2,66},{66,2},{3,67},{67,3},{4,68},{68... | collective-permute-start | bytes 1658888 | tf_op jit(solution)/shard_map/ppermute | solution.py:418
  9.1 65.8 %collective-permute-start.4 = (bf16[1,192,720]{2,1,0:T(8,128)(2,1)}, bf16[1,192,720]{2,1,0:T(8,128)(2,1)}, u32[]{:S(2)}, u32[]{:S(2)}) collective-permute-start(bf16[1,192,720]{2,1,0:T(8,128)(2,1)} %get-tuple-element.34), channel_id=1, source_target_pairs={{0,64},{64,0},{1,65},{65,1},{2,66},{66,2},{3,67},{67,3},{4,68},{68... | collective-permute-start | bytes 829448 | tf_op jit(solution)/shard_map/ppermute | solution.py:418
  10.0 31.6 %collective-permute-start = (f32[10,128]{1,0:T(8,128)S(1)}, f32[10,128]{1,0:T(8,128)S(1)}, u32[]{:S(2)}, u32[]{:S(2)}) collective-permute-start(f32[10,128]{1,0:T(8,128)S(1)} %copy-done.4), channel_id=1, source_target_pairs={{0,64},{64,0},{1,65},{65,1},{2,66},{66,2},{3,67},{67,3},{4,68},{68... | collective-permute-start | bytes 15368 | tf_op jit(solution)/shard_map/ppermute | solution.py:418
  68.4 1.1 %copy-start.2 = (bf16[2,192,720]{2,1,0:T(8,128)(2,1)S(1)}, bf16[2,192,720]{2,1,0:T(8,128)(2,1)}, u32[]{:S(2)}) copy-start(bf16[2,192,720]{2,1,0:T(8,128)(2,1)} %get-tuple-element.36.own_ref) | copy-start | bytes 1658884
  71.9 3.0 %copy-start.3 = (bf16[1,192,720]{2,1,0:T(8,128)(2,1)S(1)}, bf16[1,192,720]{2,1,0:T(8,128)(2,1)}, u32[]{:S(2)}) copy-start(bf16[1,192,720]{2,1,0:T(8,128)(2,1)} %get-tuple-element.33.own_ref) | copy-start | bytes 829444
  71.9 11.3 %collective-permute-start.7 = (bf16[2,2,184,128]{3,2,1,0:T(8,128)(2,1)S(1)}, bf16[2,2,184,128]{3,2,1,0:T(8,128)(2,1)S(1)}, u32[]{:S(2)}, u32[]{:S(2)}) collective-permute-start(bf16[2,2,184,128]{3,2,1,0:T(8,128)(2,1)S(1)} %get-tuple-element.40), channel_id=1, source_target_pairs={{0,64},{64,0},{1,65},{65,1},{2,66},{66,2},{3,67},{67,3},{4,68},{68... | collective-permute-start | bytes 565256 | tf_op jit(solution)/shard_map/ppermute | solution.py:418
  73.6 10.8 %collective-permute-start.3 = (bf16[2,2,184,128]{3,2,1,0:T(8,128)(2,1)S(1)}, bf16[2,2,184,128]{3,2,1,0:T(8,128)(2,1)S(1)}, u32[]{:S(2)}, u32[]{:S(2)}) collective-permute-start(bf16[2,2,184,128]{3,2,1,0:T(8,128)(2,1)S(1)} %waves.5), channel_id=1, source_target_pairs={{0,64},{64,0},{1,65},{65,1},{2,66},{66,2},{3,67},{67,3},{4,68},{68... | collective-permute-start | bytes 565256 | tf_op jit(solution)/shard_map/ppermute | solution.py:418
  76.7 6.5 %collective-permute-start.6 = (bf16[1,2,184,128]{3,2,1,0:T(8,128)(2,1)S(1)}, bf16[1,2,184,128]{3,2,1,0:T(8,128)(2,1)S(1)}, u32[]{:S(2)}, u32[]{:S(2)}) collective-permute-start(bf16[1,2,184,128]{3,2,1,0:T(8,128)(2,1)S(1)} %get-tuple-element.39), channel_id=1, source_target_pairs={{0,64},{64,0},{1,65},{65,1},{2,66},{66,2},{3,67},{67,3},{4,68},{68... | collective-permute-start | bytes 282632 | tf_op jit(solution)/shard_map/ppermute | solution.py:418
  77.6 4.8 %collective-permute-start.1 = (f32[8,128]{1,0:T(8,128)S(1)}, f32[8,128]{1,0:T(8,128)S(1)}, u32[]{:S(2)}, u32[]{:S(2)}) collective-permute-start(f32[8,128]{1,0:T(8,128)S(1)} %get-tuple-element.29._.refs_2_), channel_id=1, source_target_pairs={{0,192},{64,128},{128,64},{192,0},{1,193},{65,129},{129,65},{193,1... | collective-permute-start | bytes 12296 | tf_op jit(solution)/shard_map/ppermute | solution.py:456
where the time goes:
time: 85.7 us; the launch traced here: 85.4 us
  waiting for transfers between devices  33.3 us (39%)
  blocking collectives  26.2 us (31%)
  Pallas kernels  15.7 us (18%)
  starting transfers between devices  8.39 us (10%)
  local copies, waits for them, and re-layouts  1.09 us (1%)
    ppermute x7, waiting for transfers between devices, swap(): return lax.ppermute(x, 'lon', across)  30.4 us
    all_to_all x2, blocking collectives, all_of(): return lax.all_to_all(x, axes, split_axis=0, concat_axis=0, tiled=True)  26.2 us
    ppermute x7, starting transfers between devices, swap(): return lax.ppermute(x, 'lon', across)  7.25 us
    pallas_call x4, Pallas kernels, waves(): pl.pallas_call(functools.partial(wave_kernel, flips=flips), out_shape=tup...  5.76 us
    pallas_call x1, Pallas kernels, send(): pl.pallas_call(lambda *refs: send_kernel(groups, *refs), out_shape=(*pack...  3.27 us
    pallas_call x1, Pallas kernels, first_part(): pl.pallas_call(first_kernel, out_shape=(jax.ShapeDtypeStruct((1, 3 * part...  3.04 us
    ppermute x1, waiting for transfers between devices, per_device(): lax.ppermute(near_half, ('lat', 'lon'), [(i, 3 - i) for i in range(4)])  2.88 us
    pallas_call x2, Pallas kernels, join(): pl.pallas_call(lambda *refs: join_kernel(rows[0], parts, *refs), out_shap...  2.22 us
  transfers between devices with their start and end apart: 8, of which 2 were waited for; matrix products, arithmetic and copies ran while one was open for 0% of the time, Pallas kernels for 10%

commit v1 on v0

--- a/solution.py
+++ b/solution.py
@@ -47,25 +47,50 @@
     return mask.astype(F32).astype(BF16)
 
 
-def first_kernel(half_ref, u_ref, v_ref, t_ref, m_ref, o_ref, sums_ref, us, vs, ts, masks, sems):
+def pack_kernel(half_ref, u_ref, v_ref, t_ref, m_ref, o_ref, fields, mask, sems):
+    part = fields.shape[1]
+    at = pl.ds((1 - half_ref[0]) * part, part)
+    copies = [pltpu.make_async_copy(m_ref.at[0], mask, sems.at[3])]
+    for f, ref in enumerate((t_ref, u_ref, v_ref)):
+        copies.append(pltpu.make_async_copy(ref.at[0, at], fields.at[f], sems.at[f]))
+    for c in copies:
+        c.start()
+    for c in copies:
+        c.wait()
+    size = part * fields.shape[2]
+    keep = keep_of(mask[...])[None]
+    for f in range(3):
+        o_ref[0, f * size : (f + 1) * size, :] = (fields[f] * keep).reshape(size, -1)
+
+
+def pack(half, u, v, t, mask):
+    _, samples, levels, lon = u.shape
+    part = samples // 2
+    return pl.pallas_call(
+        pack_kernel,
+        out_shape=jax.ShapeDtypeStruct((1, 3 * part * levels, lon), BF16),
+        in_specs=[SMEM, HBM, HBM, HBM, HBM],
+        out_specs=VMEM,
+        scratch_shapes=[
+            pltpu.VMEM((3, part, levels, lon), BF16),
+            pltpu.VMEM((levels, lon), jnp.int32),
+            pltpu.SemaphoreType.DMA((4,)),
+        ],
+        compiler_params=params(60),
+        name="pack",
+    )(half, u, v, t, mask)
+
+
+def sums_kernel(v_ref, m_ref, _, sums_ref, vs, masks, sems):
     rows, samples, levels, lon = vs.shape
-    part = samples // 2
-    size = part * levels
-    far = 1 - half_ref[0]
-    at = pl.ds(far * part, part)
-    copies = []
-    for j in range(rows):
-        copies.append(
-            [
-                pltpu.make_async_copy(m_ref.at[j], masks.at[j], sems.at[j, 0]),
-                pltpu.make_async_copy(v_ref.at[j], vs.at[j], sems.at[j, 1]),
-            ]
+    copies = [
+        (
+            pltpu.make_async_copy(m_ref.at[j], masks.at[j], sems.at[j, 0]),
+            pltpu.make_async_copy(v_ref.at[j], vs.at[j], sems.at[j, 1]),
         )
-    extra = [
-        pltpu.make_async_copy(u_ref.at[0, at], us, sems.at[0, 2]),
-        pltpu.make_async_copy(t_ref.at[0, at], ts, sems.at[0, 3]),
+        for j in range(rows)
     ]
-    for group in (copies[0], extra, *copies[1:]):
+    for group in copies:
         for c in group:
             c.start()
     ones = jnp.ones((8, lon), BF16)
@@ -75,38 +100,25 @@
         keep = keep_of(masks[j])
         v = (vs[j] * keep[None]).reshape(samples * levels, lon)
         sums_ref[j : j + 1, :] = lax.dot_general(ones, v, CONTRACT, preferred_element_type=F32)[0:1]
-        full = jnp.broadcast_to(keep[None], (samples, levels, lon)).reshape(samples * levels, lon)
-        sums_ref[rows + j : rows + j + 1, :] = lax.dot_general(
-            ones, full, CONTRACT, preferred_element_type=F32
-        )[0:1]
-    for c in extra:
-        c.wait()
-    keep = keep_of(masks[0])[None]
-    for f, field in enumerate((ts[...], us[...], vs[0, at])):
-        o_ref[0, f * size : (f + 1) * size, :] = (field * keep).reshape(size, lon)
-
-
-def first_part(half, u, v, t, mask):
+        kept = lax.dot_general(ones, keep, CONTRACT, preferred_element_type=F32)[0:1]
+        sums_ref[rows + j : rows + j + 1, :] = jnp.concatenate([kept] * samples, axis=1)
+
+
+def zonal(v, mask, after):
     rows, samples, levels, lon = v.shape
-    part = samples // 2
     return pl.pallas_call(
-        first_kernel,
-        out_shape=(
-            jax.ShapeDtypeStruct((1, 3 * part * levels, lon), BF16),
-            jax.ShapeDtypeStruct((2 * rows, samples * levels), F32),
-        ),
-        in_specs=[SMEM, HBM, HBM, HBM, HBM],
-        out_specs=(VMEM, VMEM),
+        sums_kernel,
+        out_shape=jax.ShapeDtypeStruct((2 * rows, samples * levels), F32),
+        in_specs=[HBM, HBM, ANY],
+        out_specs=VMEM,
         scratch_shapes=[
-            pltpu.VMEM((part, levels, lon), BF16),
             pltpu.VMEM((rows, samples, levels, lon), BF16),
-            pltpu.VMEM((part, levels, lon), BF16),
             pltpu.VMEM((rows, levels, lon), jnp.int32),
-            pltpu.SemaphoreType.DMA((rows, 4)),
+            pltpu.SemaphoreType.DMA((rows, 2)),
         ],
         compiler_params=params(60),
         name="sums",
-    )(half, u, v, t, mask)
+    )(v, mask, after)
 
 
 def send_kernel(groups, half_ref, u_ref, v_ref, t_ref, m_ref, _, *rest):
@@ -417,7 +429,8 @@
     def swap(x):
         return lax.ppermute(x, "lon", across)
 
-    first, sums = first_part(half, u, v, t, mask)
+    first = pack(half, u, v, t, mask)
+    sums = zonal(v, mask, first)
     packed = send(half, u, v, t, mask, sums, GROUPS)
     rest, own = packed[: len(GROUPS) - 1], packed[len(GROUPS) - 1 :]
     got = [swap(first)]

time: 85.7 us -> 87.4 us (1.020)
  Pallas kernels: 15.7 us -> 17.3 us
    pallas_call x1 -> x2, Pallas kernels: 3.04 us -> 4.65 us  [the longest x1 2.81 us: zonal(): pl.pallas_call(sums_kernel, out_shape=jax.ShapeDtypeStruct((2 * rows, sam...]
where the time goes in v1:
time: 87.4 us; the launch traced here: 87 us
  waiting for transfers between devices  33.3 us (38%)
  blocking collectives  26.2 us (30%)
  Pallas kernels  17.3 us (20%)
  starting transfers between devices  8.39 us (10%)
  local copies, waits for them, and re-layouts  1.09 us (1%)
    ppermute x7, waiting for transfers between devices, swap(): return lax.ppermute(x, 'lon', across)  30.4 us
    all_to_all x2, blocking collectives, all_of(): return lax.all_to_all(x, axes, split_axis=0, concat_axis=0, tiled=True)  26.2 us
    ppermute x7, starting transfers between devices, swap(): return lax.ppermute(x, 'lon', across)  7.25 us
    pallas_call x4, Pallas kernels, waves(): pl.pallas_call(functools.partial(wave_kernel, flips=flips), out_shape=tup...  5.76 us
    pallas_call x1, Pallas kernels, send(): pl.pallas_call(lambda *refs: send_kernel(groups, *refs), out_shape=(*pack...  3.27 us
    ppermute x1, waiting for transfers between devices, per_device(): lax.ppermute(near_half, ('lat', 'lon'), [(i, 3 - i) for i in range(4)])  2.88 us
    pallas_call x1, Pallas kernels, zonal(): pl.pallas_call(sums_kernel, out_shape=jax.ShapeDtypeStruct((2 * rows, sam...  2.81 us
    pallas_call x2, Pallas kernels, join(): pl.pallas_call(lambda *refs: join_kernel(rows[0], parts, *refs), out_shap...  2.22 us
  transfers between devices with their start and end apart: 8, of which 2 were waited for; matrix products, arithmetic and copies ran while one was open for 0% of the time, Pallas kernels for 10%

profile of v1, /device:TPU:6, one launch (start us, length us, event | category | flops | bytes accessed | tf_op | source)
XLA Modules:
  0.0 87.0 jit_solution(9893333195667905603)
XLA Ops:
  0.6 1.8 %pack.1._ = bf16[1,192,720]{2,1,0:T(8,128)(2,1)} custom-call(s32[1]{0:T(128)} %bitcast.1.half_ref.refs_0_, bf16[5,4,32,720]{3,2,1,0:T(8,128)(2,1)} %refs_1_.1, bf16[5,4,32,720]{3,2,1,0:T(8,128)(2,1)} %refs_2_.1, bf16[5,4,32,720]{3,2,1,0:T(8,128)(2,1)} %refs_3_.1, s32[5,32,720]{2,1,0:T(8,128)} %refs_4_.3), custom_call_target="tpu_custom_call" | custom-call | tf_op jit(solution)/shard_map/pack/pallas_call | solution.py:69
  2.5 2.8 %sums.1.refs_1_.refs_5_ = f32[10,128]{1,0:T(8,128)} custom-call(bf16[5,4,32,720]{3,2,1,0:T(8,128)(2,1)} %refs_2_.1, s32[5,32,720]{2,1,0:T(8,128)} %refs_4_.3, bf16[1,192,720]{2,1,0:T(8,128)(2,1)} %pack.1._), custom_call_target="tpu_custom_call" | custom-call | tf_op jit(solution)/shard_map/sums/pallas_call | solution.py:109
  5.3 3.3 %send.1 = (bf16[2,192,720]{2,1,0:T(8,128)(2,1)}, bf16[2,192,720]{2,1,0:T(8,128)(2,1)}, bf16[1,192,720]{2,1,0:T(8,128)(2,1)}, bf16[2,192,720]{2,1,0:T(8,128)(2,1)}, bf16[2,192,720]{2,1,0:T(8,128)(2,1)}) custom-call(s32[1]{0:T(128)} %bitcast.1.half_ref.refs_0_, bf16[5,4,32,720]{3,2,1,0:T(8,128)(2,1)} %refs_1_.1, bf16[5,4,32,720]{3,2,1,0:T(8,128)(2,1)} %refs_2_.1, ...), custom_call_target="tpu_custom_call" | custom-call | tf_op jit(solution)/shard_map/send/pallas_call | solution.py:170
  8.6 0.9 %collective-permute-start.5 = (bf16[2,192,720]{2,1,0:T(8,128)(2,1)}, bf16[2,192,720]{2,1,0:T(8,128)(2,1)}, u32[]{:S(2)}, u32[]{:S(2)}) collective-permute-start(bf16[2,192,720]{2,1,0:T(8,128)(2,1)} %get-tuple-element.33), channel_id=1, source_target_pairs={{0,64},{64,0},{1,65},{65,1},{2,66},{66,2},{3,67},{67,3},{4,68},{68... | collective-permute-start | bytes 1658888 | tf_op jit(solution)/shard_map/ppermute | solution.py:430
  9.6 1.2 %collective-permute-start.2 = (bf16[2,192,720]{2,1,0:T(8,128)(2,1)}, bf16[2,192,720]{2,1,0:T(8,128)(2,1)S(1)}, u32[]{:S(2)}, u32[]{:S(2)}) collective-permute-start(bf16[2,192,720]{2,1,0:T(8,128)(2,1)} %get-tuple-element.28), channel_id=1, source_target_pairs={{0,64},{64,0},{1,65},{65,1},{2,66},{66,2},{3,67},{67,3},{4,68},{68... | collective-permute-start | bytes 1658888 | tf_op jit(solution)/shard_map/ppermute | solution.py:430
  10.7 0.8 collective-permute-start.4
  11.6 1.2 %collective-permute-start = (f32[10,128]{1,0:T(8,128)S(1)}, f32[10,128]{1,0:T(8,128)S(1)}, u32[]{:S(2)}, u32[]{:S(2)}) collective-permute-start(f32[10,128]{1,0:T(8,128)S(1)} %copy-done.4), channel_id=1, source_target_pairs={{0,64},{64,0},{1,65},{65,1},{2,66},{66,2},{3,67},{67,3},{4,68},{68... | collective-permute-start | bytes 15368 | tf_op jit(solution)/shard_map/ppermute | solution.py:430
  12.8 30.4 %collective-permute-done.refs_2_ = f32[10,128]{1,0:T(8,128)S(1)} collective-permute-done((f32[10,128]{1,0:T(8,128)S(1)}, f32[10,128]{1,0:T(8,128)S(1)}, u32[]{:S(2)}, u32[]{:S(2)}) %collective-permute-start) | collective-permute-done | bytes 5152 | tf_op jit(solution)/shard_map/ppermute | solution.py:430
  43.3 9.9 %all_to_all.10.refs_1_ = f32[8,16,128]{2,1,0:T(8,128)S(1)} all-to-all(f32[8,16,128]{2,1,0:T(8,128)S(1)} %shard_map.102._), channel_id=1, replica_groups=mesh['lat'=2,'lon'=2,'lev_0'=8,'lev_1'=4,'lev_2'=2] {'lev_1','lev_2'}, dimensions={0} | all-to-all | bytes 131072 | tf_op jit(solution)/shard_map/all_to_all | solution.py:413
  53.2 0.5 shard_map.103
  53.7 16.3 %all_to_all.11.refs_2_ = f32[8,8,128]{2,1,0:T(8,128)S(1)} all-to-all(f32[8,8,128]{2,1,0:T(8,128)S(1)} %get-tuple-element.24._), channel_id=1, replica_groups=mesh['lat'=2,'lon'=2,'lev_0'=8,'lev_1'=4,'lev_2'=2] {'lev_0'}, dimensions={0} | all-to-all | bytes 65536 | tf_op jit(solution)/shard_map/all_to_all | solution.py:413
  70.0 1.1 %copy-done.2 = bf16[2,192,720]{2,1,0:T(8,128)(2,1)S(1)} copy-done((bf16[2,192,720]{2,1,0:T(8,128)(2,1)S(1)}, bf16[2,192,720]{2,1,0:T(8,128)(2,1)}, u32[]{:S(2)}) %copy-start.2) | copy-done | bytes 552984
  71.1 2.4 %waves.7 = (bf16[2,2,184,128]{3,2,1,0:T(8,128)(2,1)S(1)}, f32[2,2,184,128]{3,2,1,0:T(8,128)S(1)}) custom-call(s32[1]{0:T(128)} %bitcast.1.half_ref.refs_0_, bf16[2,2,368,720]{3,2,1,0:T(8,128)(2,1)S(1)} %copy-done, bf16[2,192,720]{2,1,0:T(8,128)(2,1)S(1)} %copy-done.2, bf16[2,192,720]{2,1,0:T(8,128)(2,1)} %collective-permute-done.5.got_ref, ...), custom_call_target="tpu_custom_call" | custom-call | tf_op jit(solution)/shard_map/waves/pallas_call | solution.py:211
  73.5 0.9 %collective-permute-start.7 = (bf16[2,2,184,128]{3,2,1,0:T(8,128)(2,1)S(1)}, bf16[2,2,184,128]{3,2,1,0:T(8,128)(2,1)S(1)}, u32[]{:S(2)}, u32[]{:S(2)}) collective-permute-start(bf16[2,2,184,128]{3,2,1,0:T(8,128)(2,1)S(1)} %get-tuple-element.36), channel_id=1, source_target_pairs={{0,64},{64,0},{1,65},{65,1},{2,66},{66,2},{3,67},{67,3},{4,68},{68... | collective-permute-start | bytes 565256 | tf_op jit(solution)/shard_map/ppermute | solution.py:430
  74.4 0.8 waves.5
  75.2 1.3 %collective-permute-start.3 = (bf16[2,2,184,128]{3,2,1,0:T(8,128)(2,1)S(1)}, bf16[2,2,184,128]{3,2,1,0:T(8,128)(2,1)S(1)}, u32[]{:S(2)}, u32[]{:S(2)}) collective-permute-start(bf16[2,2,184,128]{3,2,1,0:T(8,128)(2,1)S(1)} %waves.5), channel_id=1, source_target_pairs={{0,64},{64,0},{1,65},{65,1},{2,66},{66,2},{3,67},{67,3},{4,68},{68... | collective-permute-start | bytes 565256 | tf_op jit(solution)/shard_map/ppermute | solution.py:430
  76.5 1.7 %waves.6 = (bf16[1,2,184,128]{3,2,1,0:T(8,128)(2,1)S(1)}, f32[1,2,184,128]{3,2,1,0:T(8,128)S(1)}) custom-call(s32[1]{0:T(128)} %bitcast.1.half_ref.refs_0_, bf16[2,2,368,720]{3,2,1,0:T(8,128)(2,1)S(1)} %copy-done, bf16[1,192,720]{2,1,0:T(8,128)(2,1)S(1)} %copy-done.3, bf16[1,192,720]{2,1,0:T(8,128)(2,1)} %collective-permute-done.4.got_ref, ...), custom_call_target="tpu_custom_call" | custom-call | tf_op jit(solution)/shard_map/waves/pallas_call | solution.py:211
  78.3 0.9 %collective-permute-start.6 = (bf16[1,2,184,128]{3,2,1,0:T(8,128)(2,1)S(1)}, bf16[1,2,184,128]{3,2,1,0:T(8,128)(2,1)S(1)}, u32[]{:S(2)}, u32[]{:S(2)}) collective-permute-start(bf16[1,2,184,128]{3,2,1,0:T(8,128)(2,1)S(1)} %get-tuple-element.35), channel_id=1, source_target_pairs={{0,64},{64,0},{1,65},{65,1},{2,66},{66,2},{3,67},{67,3},{4,68},{68... | collective-permute-start | bytes 282632 | tf_op jit(solution)/shard_map/ppermute | solution.py:430
  79.2 1.1 %collective-permute-start.1 = (f32[8,128]{1,0:T(8,128)S(1)}, f32[8,128]{1,0:T(8,128)S(1)}, u32[]{:S(2)}, u32[]{:S(2)}) collective-permute-start(f32[8,128]{1,0:T(8,128)S(1)} %get-tuple-element.26._.refs_2_), channel_id=1, source_target_pairs={{0,192},{64,128},{128,64},{192,0},{1,193},{65,129},{129,65},{193,1... | collective-permute-start | bytes 12296 | tf_op jit(solution)/shard_map/ppermute | solution.py:469
  80.3 0.8 waves.4.refs_4_.refs_1_
  81.1 2.9 %collective-permute-done.1.refs_3_ = f32[8,128]{1,0:T(8,128)S(1)} collective-permute-done((f32[8,128]{1,0:T(8,128)S(1)}, f32[8,128]{1,0:T(8,128)S(1)}, u32[]{:S(2)}, u32[]{:S(2)}) %collective-permute-start.1) | collective-permute-done | bytes 4128 | tf_op jit(solution)/shard_map/ppermute | solution.py:469
  84.0 0.8 shard_map.105
  84.8 1.2 %join.2 = (f32[5,360,128]{2,1,0:T(8,128)}, f32[5,360,128]{2,1,0:T(8,128)}) custom-call(s32[1]{0:T(128)} %bitcast.1.half_ref.refs_0_, f32[1,2,184,128]{3,2,1,0:T(8,128)S(1)} %get-tuple-element.31.refs_1_, f32[2,2,184,128]{3,2,1,0:T(8,128)S(1)} %get-tuple-element.34.refs_2_, bf16[1,2,184,128]{3,2,1,0:T(8,128)(2,1)S(1)} %collective-permute-done.6.refs_3_, ...), custom_call_target="tpu_custom_call" | custom-call | tf_op jit(solution)/shard_map/join/pallas_call | solution.py:260
  86.0 1.0 %join.3 = (f32[5,360,128]{2,1,0:T(8,128)}, f32[5,360,128]{2,1,0:T(8,128)}) custom-call(s32[1]{0:T(128)} %bitcast.1.half_ref.refs_0_, f32[2,2,184,128]{3,2,1,0:T(8,128)S(1)} %waves.4.refs_4_.refs_1_, bf16[2,2,184,128]{3,2,1,0:T(8,128)(2,1)S(1)} %collective-permute-done.3.refs_2_, ...), custom_call_target="tpu_custom_call", output_to_operand_aliasing={{0}: (3, {}), {1}: (4, {})} | custom-call | tf_op jit(solution)/shard_map/join/pallas_call | solution.py:260
  (21 shorter events, 0.2 us)
Async XLA Ops:
  2.5 40.7 %copy-start.5 = (f32[5,4,32]{2,1,0:T(4,128)S(1)}, f32[5,4,32]{2,1,0:T(4,128)}, u32[]{:S(2)}) copy-start(f32[5,4,32]{2,1,0:T(4,128)} %refs_4_.2) | copy-start | bytes 7684
  2.5 40.7 %copy-start.6 = (f32[32]{0:T(128)S(1)}, f32[32]{0:T(128)}, u32[]{:S(2)}) copy-start(f32[32]{0:T(128)} %param.11) | copy-start | bytes 388
  5.3 6.3 %copy-start.4 = (f32[10,128]{1,0:T(8,128)S(1)}, f32[10,128]{1,0:T(8,128)}, u32[]{:S(2)}) copy-start(f32[10,128]{1,0:T(8,128)} %sums.1.refs_1_.refs_5_) | copy-start | bytes 15364
  5.3 64.7 %copy-start = (bf16[2,2,368,720]{3,2,1,0:T(8,128)(2,1)S(1)}, bf16[2,2,368,720]{3,2,1,0:T(8,128)(2,1)}, u32[]{:S(2)}) copy-start(bf16[2,2,368,720]{3,2,1,0:T(8,128)(2,1)} %constant.29.clone.table_ref) | copy-start | bytes 6359044
  8.6 65.8 %copy-start.1 = (bf16[2,192,720]{2,1,0:T(8,128)(2,1)S(1)}, bf16[2,192,720]{2,1,0:T(8,128)(2,1)}, u32[]{:S(2)}) copy-start(bf16[2,192,720]{2,1,0:T(8,128)(2,1)} %get-tuple-element.27.own_ref) | copy-start | bytes 1658884
  8.6 61.3 %collective-permute-start.5 = (bf16[2,192,720]{2,1,0:T(8,128)(2,1)}, bf16[2,192,720]{2,1,0:T(8,128)(2,1)}, u32[]{:S(2)}, u32[]{:S(2)}) collective-permute-start(bf16[2,192,720]{2,1,0:T(8,128)(2,1)} %get-tuple-element.33), channel_id=1, source_target_pairs={{0,64},{64,0},{1,65},{65,1},{2,66},{66,2},{3,67},{67,3},{4,68},{68... | collective-permute-start | bytes 1658888 | tf_op jit(solution)/shard_map/ppermute | solution.py:430
  9.6 64.9 %collective-permute-start.2 = (bf16[2,192,720]{2,1,0:T(8,128)(2,1)}, bf16[2,192,720]{2,1,0:T(8,128)(2,1)S(1)}, u32[]{:S(2)}, u32[]{:S(2)}) collective-permute-start(bf16[2,192,720]{2,1,0:T(8,128)(2,1)} %get-tuple-element.28), channel_id=1, source_target_pairs={{0,64},{64,0},{1,65},{65,1},{2,66},{66,2},{3,67},{67,3},{4,68},{68... | collective-permute-start | bytes 1658888 | tf_op jit(solution)/shard_map/ppermute | solution.py:430
  10.7 65.8 %collective-permute-start.4 = (bf16[1,192,720]{2,1,0:T(8,128)(2,1)}, bf16[1,192,720]{2,1,0:T(8,128)(2,1)}, u32[]{:S(2)}, u32[]{:S(2)}) collective-permute-start(bf16[1,192,720]{2,1,0:T(8,128)(2,1)} %pack.1._), channel_id=1, source_target_pairs={{0,64},{64,0},{1,65},{65,1},{2,66},{66,2},{3,67},{67,3},{4,68},{68... | collective-permute-start | bytes 829448 | tf_op jit(solution)/shard_map/ppermute | solution.py:430
  11.6 31.6 %collective-permute-start = (f32[10,128]{1,0:T(8,128)S(1)}, f32[10,128]{1,0:T(8,128)S(1)}, u32[]{:S(2)}, u32[]{:S(2)}) collective-permute-start(f32[10,128]{1,0:T(8,128)S(1)} %copy-done.4), channel_id=1, source_target_pairs={{0,64},{64,0},{1,65},{65,1},{2,66},{66,2},{3,67},{67,3},{4,68},{68... | collective-permute-start | bytes 15368 | tf_op jit(solution)/shard_map/ppermute | solution.py:430
  70.0 1.1 %copy-start.2 = (bf16[2,192,720]{2,1,0:T(8,128)(2,1)S(1)}, bf16[2,192,720]{2,1,0:T(8,128)(2,1)}, u32[]{:S(2)}) copy-start(bf16[2,192,720]{2,1,0:T(8,128)(2,1)} %get-tuple-element.32.own_ref) | copy-start | bytes 1658884
  73.5 3.0 %copy-start.3 = (bf16[1,192,720]{2,1,0:T(8,128)(2,1)S(1)}, bf16[1,192,720]{2,1,0:T(8,128)(2,1)}, u32[]{:S(2)}) copy-start(bf16[1,192,720]{2,1,0:T(8,128)(2,1)} %get-tuple-element.30.own_ref) | copy-start | bytes 829444
  73.5 11.3 %collective-permute-start.7 = (bf16[2,2,184,128]{3,2,1,0:T(8,128)(2,1)S(1)}, bf16[2,2,184,128]{3,2,1,0:T(8,128)(2,1)S(1)}, u32[]{:S(2)}, u32[]{:S(2)}) collective-permute-start(bf16[2,2,184,128]{3,2,1,0:T(8,128)(2,1)S(1)} %get-tuple-element.36), channel_id=1, source_target_pairs={{0,64},{64,0},{1,65},{65,1},{2,66},{66,2},{3,67},{67,3},{4,68},{68... | collective-permute-start | bytes 565256 | tf_op jit(solution)/shard_map/ppermute | solution.py:430
  75.2 10.8 %collective-permute-start.3 = (bf16[2,2,184,128]{3,2,1,0:T(8,128)(2,1)S(1)}, bf16[2,2,184,128]{3,2,1,0:T(8,128)(2,1)S(1)}, u32[]{:S(2)}, u32[]{:S(2)}) collective-permute-start(bf16[2,2,184,128]{3,2,1,0:T(8,128)(2,1)S(1)} %waves.5), channel_id=1, source_target_pairs={{0,64},{64,0},{1,65},{65,1},{2,66},{66,2},{3,67},{67,3},{4,68},{68... | collective-permute-start | bytes 565256 | tf_op jit(solution)/shard_map/ppermute | solution.py:430
  78.3 6.5 %collective-permute-start.6 = (bf16[1,2,184,128]{3,2,1,0:T(8,128)(2,1)S(1)}, bf16[1,2,184,128]{3,2,1,0:T(8,128)(2,1)S(1)}, u32[]{:S(2)}, u32[]{:S(2)}) collective-permute-start(bf16[1,2,184,128]{3,2,1,0:T(8,128)(2,1)S(1)} %get-tuple-element.35), channel_id=1, source_target_pairs={{0,64},{64,0},{1,65},{65,1},{2,66},{66,2},{3,67},{67,3},{4,68},{68... | collective-permute-start | bytes 282632 | tf_op jit(solution)/shard_map/ppermute | solution.py:430
  79.2 4.8 %collective-permute-start.1 = (f32[8,128]{1,0:T(8,128)S(1)}, f32[8,128]{1,0:T(8,128)S(1)}, u32[]{:S(2)}, u32[]{:S(2)}) collective-permute-start(f32[8,128]{1,0:T(8,128)S(1)} %get-tuple-element.26._.refs_2_), channel_id=1, source_target_pairs={{0,192},{64,128},{128,64},{192,0},{1,193},{65,129},{129,65},{193,1... | collective-permute-start | bytes 12296 | tf_op jit(solution)/shard_map/ppermute | solution.py:469

commit v2 on v1

--- a/solution.py
+++ b/solution.py
@@ -18,7 +18,7 @@
 INNER = ("lev_1", "lev_2")
 OUTER = "lev_0"
 EPSILON = 1e-06
-GROUPS = ((0,), (1, 2), (3, 4))
+GROUPS = ((0,), (1, 2, 3), (4,))
 F32 = jnp.float32
 BF16 = jnp.bfloat16
 MIB = 1024 * 1024
@@ -482,8 +482,9 @@
 
     back = [swap(x) for x in (far0, far1, far2)]
     kept = [near0, near1, near2]
-    outs = join(half, kept[:2], back[:2], None, GROUPS[0] + GROUPS[1], bands)
-    outs = join(half, kept[2:], back[2:], outs, GROUPS[2], bands)
+    outs = None
+    for group, mine, far in zip(GROUPS, kept, back):
+        outs = join(half, [mine], [far], outs, group, bands)
     heat, momentum = (jnp.transpose(x, (1, 0, 2)) for x in outs)
     return psi, heat, momentum, loss[0, 0]
 

time: 87.4 us -> 89.3 us (1.022)
  blocking collectives: 26.2 us -> 9.89 us
  starting transfers between devices: 8.39 us -> 16.4 us
  Pallas kernels: 17.3 us -> 22 us
  waiting for transfers between devices: 33.3 us -> 37 us
  local copies, waits for them, and re-layouts: 1.09 us -> 2.83 us
    all_to_all x2 -> x1, blocking collectives: 26.2 us -> 9.89 us  [all_of(): return lax.all_to_all(x, axes, split_axis=0, concat_axis=0, tiled=True)]
    all_to_all x0 -> x1, starting transfers between devices: none -> 8.47 us  [all_of(): return lax.all_to_all(x, axes, split_axis=0, concat_axis=0, tiled=True)]
    all_to_all x0 -> x1, waiting for transfers between devices: none -> 2.79 us  [all_of(): return lax.all_to_all(x, axes, split_axis=0, concat_axis=0, tiled=True)]
    pallas_call x2 -> x3, Pallas kernels: 2.22 us -> 4.82 us  [join(): pl.pallas_call(lambda *refs: join_kernel(rows[0], parts, *refs), out_shap...]
    unnamed x14 -> x18, local copies, waits for them, and re-layouts: 1.09 us -> 2.83 us
    pallas_call x4, Pallas kernels: 5.76 us -> 7.25 us  [waves(): pl.pallas_call(functools.partial(wave_kernel, flips=flips), out_shape=tup...]
    ppermute x1, waiting for transfers between devices: 2.88 us -> 3.84 us  [per_device(): lax.ppermute(near_half, ('lat', 'lon'), [(i, 3 - i) for i in range(4)])]
  transfers between devices with their start and end apart: 8 -> 9, of which waited for: 2 -> 3; matrix products, arithmetic and copies ran while one was open for 0% -> 0% of each run, Pallas kernels for 10% -> 15%
where the time goes in v2:
time: 89.3 us; the launch traced here: 88.9 us
  waiting for transfers between devices  37 us (41%)
  Pallas kernels  22 us (25%)
  starting transfers between devices  16.4 us (18%)
  blocking collectives  9.89 us (11%)
  local copies, waits for them, and re-layouts  2.83 us (3%)
    ppermute x7, waiting for transfers between devices, swap(): return lax.ppermute(x, 'lon', across)  30.4 us
    all_to_all x1, blocking collectives, all_of(): return lax.all_to_all(x, axes, split_axis=0, concat_axis=0, tiled=True)  9.89 us
    all_to_all x1, starting transfers between devices, all_of(): return lax.all_to_all(x, axes, split_axis=0, concat_axis=0, tiled=True)  8.47 us
    ppermute x7, starting transfers between devices, swap(): return lax.ppermute(x, 'lon', across)  7.44 us
    pallas_call x4, Pallas kernels, waves(): pl.pallas_call(functools.partial(wave_kernel, flips=flips), out_shape=tup...  7.25 us
    pallas_call x3, Pallas kernels, join(): pl.pallas_call(lambda *refs: join_kernel(rows[0], parts, *refs), out_shap...  4.82 us
    ppermute x1, waiting for transfers between devices, per_device(): lax.ppermute(near_half, ('lat', 'lon'), [(i, 3 - i) for i in range(4)])  3.84 us
    pallas_call x1, Pallas kernels, send(): pl.pallas_call(lambda *refs: send_kernel(groups, *refs), out_shape=(*pack...  3.27 us
  transfers between devices with their start and end apart: 9, of which 3 were waited for; matrix products, arithmetic and copies ran while one was open for 0% of the time, Pallas kernels for 15%

profile of v2, /device:TPU:6, one launch (start us, length us, event | category | flops | bytes accessed | tf_op | source)
XLA Modules:
  0.0 88.9 jit_solution(11415324299250060285)
XLA Ops:
  0.6 1.8 %pack.1._ = bf16[1,192,720]{2,1,0:T(8,128)(2,1)} custom-call(s32[1]{0:T(128)} %bitcast.1.half_ref.refs_0_, bf16[5,4,32,720]{3,2,1,0:T(8,128)(2,1)} %refs_1_.1, bf16[5,4,32,720]{3,2,1,0:T(8,128)(2,1)} %refs_2_.1, bf16[5,4,32,720]{3,2,1,0:T(8,128)(2,1)} %refs_3_.1, s32[5,32,720]{2,1,0:T(8,128)} %refs_4_.3), custom_call_target="tpu_custom_call" | custom-call | tf_op jit(solution)/shard_map/pack/pallas_call | solution.py:69
  2.5 2.8 %sums.1.refs_1_.refs_5_ = f32[10,128]{1,0:T(8,128)} custom-call(bf16[5,4,32,720]{3,2,1,0:T(8,128)(2,1)} %refs_2_.1, s32[5,32,720]{2,1,0:T(8,128)} %refs_4_.3, bf16[1,192,720]{2,1,0:T(8,128)(2,1)} %pack.1._), custom_call_target="tpu_custom_call" | custom-call | tf_op jit(solution)/shard_map/sums/pallas_call | solution.py:109
  5.3 3.3 %send.1 = (bf16[3,192,720]{2,1,0:T(8,128)(2,1)}, bf16[1,192,720]{2,1,0:T(8,128)(2,1)}, bf16[1,192,720]{2,1,0:T(8,128)(2,1)}, bf16[3,192,720]{2,1,0:T(8,128)(2,1)}, bf16[1,192,720]{2,1,0:T(8,128)(2,1)}) custom-call(s32[1]{0:T(128)} %bitcast.1.half_ref.refs_0_, bf16[5,4,32,720]{3,2,1,0:T(8,128)(2,1)} %refs_1_.1, bf16[5,4,32,720]{3,2,1,0:T(8,128)(2,1)} %refs_2_.1, ...), custom_call_target="tpu_custom_call" | custom-call | tf_op jit(solution)/shard_map/send/pallas_call | solution.py:170
  8.6 0.9 %collective-permute-start.4 = (bf16[3,192,720]{2,1,0:T(8,128)(2,1)}, bf16[3,192,720]{2,1,0:T(8,128)(2,1)}, u32[]{:S(2)}, u32[]{:S(2)}) collective-permute-start(bf16[3,192,720]{2,1,0:T(8,128)(2,1)} %get-tuple-element.33), channel_id=1, source_target_pairs={{0,64},{64,0},{1,65},{65,1},{2,66},{66,2},{3,67},{67,3},{4,68},{68... | collective-permute-start | bytes 2488328 | tf_op jit(solution)/shard_map/ppermute | solution.py:430
  9.5 1.2 %collective-permute-start.6 = (bf16[1,192,720]{2,1,0:T(8,128)(2,1)}, bf16[1,192,720]{2,1,0:T(8,128)(2,1)}, u32[]{:S(2)}, u32[]{:S(2)}) collective-permute-start(bf16[1,192,720]{2,1,0:T(8,128)(2,1)} %pack.1._), channel_id=1, source_target_pairs={{0,64},{64,0},{1,65},{65,1},{2,66},{66,2},{3,67},{67,3},{4,68},{68... | collective-permute-start | bytes 829448 | tf_op jit(solution)/shard_map/ppermute | solution.py:430
  10.7 0.8 collective-permute-start.2
  11.5 1.2 %collective-permute-start = (f32[10,128]{1,0:T(8,128)S(1)}, f32[10,128]{1,0:T(8,128)S(1)}, u32[]{:S(2)}, u32[]{:S(2)}) collective-permute-start(f32[10,128]{1,0:T(8,128)S(1)} %copy-done.6), channel_id=1, source_target_pairs={{0,64},{64,0},{1,65},{65,1},{2,66},{66,2},{3,67},{67,3},{4,68},{68... | collective-permute-start | bytes 15368 | tf_op jit(solution)/shard_map/ppermute | solution.py:430
  12.7 30.4 %collective-permute-done.refs_2_ = f32[10,128]{1,0:T(8,128)S(1)} collective-permute-done((f32[10,128]{1,0:T(8,128)S(1)}, f32[10,128]{1,0:T(8,128)S(1)}, u32[]{:S(2)}, u32[]{:S(2)}) %collective-permute-start) | collective-permute-done | bytes 5152 | tf_op jit(solution)/shard_map/ppermute | solution.py:430
  43.2 9.9 %all_to_all.10.refs_1_ = f32[8,16,128]{2,1,0:T(8,128)S(1)} all-to-all(f32[8,16,128]{2,1,0:T(8,128)S(1)} %shard_map.102._), channel_id=1, replica_groups=mesh['lat'=2,'lon'=2,'lev_0'=8,'lev_1'=4,'lev_2'=2] {'lev_1','lev_2'}, dimensions={0} | all-to-all | bytes 131072 | tf_op jit(solution)/shard_map/all_to_all | solution.py:413
  53.1 1.1 %shard_map.103 = (f32[5,128]{1,0:T(8,128)S(1)}, f32[8,8,128]{2,1,0:T(8,128)}) custom-call(s32[1]{0:T(128)} %bitcast.refs_0_, f32[8,16,128]{2,1,0:T(8,128)S(1)} %all_to_all.10.refs_1_), custom_call_target="tpu_custom_call" | custom-call | tf_op jit(solution)/shard_map/pallas_call | solution.py:402
  54.2 1.2 %copy-done.2 = bf16[3,192,720]{2,1,0:T(8,128)(2,1)S(1)} copy-done((bf16[3,192,720]{2,1,0:T(8,128)(2,1)S(1)}, bf16[3,192,720]{2,1,0:T(8,128)(2,1)}, u32[]{:S(2)}) %copy-start.2) | copy-done | bytes 829464
  55.4 3.9 %waves.6 = (bf16[3,2,184,128]{3,2,1,0:T(8,128)(2,1)}, f32[3,2,184,128]{3,2,1,0:T(8,128)S(1)}) custom-call(s32[1]{0:T(128)} %bitcast.1.half_ref.refs_0_, bf16[2,2,368,720]{3,2,1,0:T(8,128)(2,1)S(1)} %copy-done, bf16[3,192,720]{2,1,0:T(8,128)(2,1)S(1)} %copy-done.2, bf16[3,192,720]{2,1,0:T(8,128)(2,1)} %collective-permute-done.4.got_ref, ...), custom_call_target="tpu_custom_call" | custom-call | tf_op jit(solution)/shard_map/waves/pallas_call | solution.py:211
  59.2 0.8 collective-permute-start.5
  60.1 8.5 %all-to-all-start.1 = ((f32[8,8,128]{2,1,0:T(8,128)}), f32[8,8,128]{2,1,0:T(8,128)S(1)}, u32[]{:S(2)}, u32[]{:S(2)}) async-start(f32[8,8,128]{2,1,0:T(8,128)} %get-tuple-element.26._), calls=%async_computation.1 | async-start | bytes 65536 | tf_op jit(solution)/shard_map/all_to_all | solution.py:413
  68.5 1.0 %copy-done.3 = bf16[1,192,720]{2,1,0:T(8,128)(2,1)S(1)} copy-done((bf16[1,192,720]{2,1,0:T(8,128)(2,1)S(1)}, bf16[1,192,720]{2,1,0:T(8,128)(2,1)}, u32[]{:S(2)}) %copy-start.3) | copy-done | bytes 276504
  69.5 2.4 %waves.7 = (bf16[1,2,184,128]{3,2,1,0:T(8,128)(2,1)}, f32[1,2,184,128]{3,2,1,0:T(8,128)S(1)}) custom-call(s32[1]{0:T(128)} %bitcast.1.half_ref.refs_0_, bf16[2,2,368,720]{3,2,1,0:T(8,128)(2,1)S(1)} %copy-done, bf16[1,192,720]{2,1,0:T(8,128)(2,1)S(1)} %copy-done.3, bf16[1,192,720]{2,1,0:T(8,128)(2,1)} %collective-permute-done.6.got_ref, ...), custom_call_target="tpu_custom_call" | custom-call | tf_op jit(solution)/shard_map/waves/pallas_call | solution.py:211
  72.6 1.2 %collective-permute-start.7 = (bf16[1,2,184,128]{3,2,1,0:T(8,128)(2,1)}, bf16[1,2,184,128]{3,2,1,0:T(8,128)(2,1)}, u32[]{:S(2)}, u32[]{:S(2)}) collective-permute-start(bf16[1,2,184,128]{3,2,1,0:T(8,128)(2,1)} %get-tuple-element.38), channel_id=1, source_target_pairs={{0,64},{64,0},{1,65},{65,1},{2,66},{66,2},{3,67},{67,3},{4,68},{68... | collective-permute-start | bytes 282632 | tf_op jit(solution)/shard_map/ppermute | solution.py:430
  73.8 2.8 %all-to-all-done.1.refs_2_ = f32[8,8,128]{2,1,0:T(8,128)S(1)} async-done(((f32[8,8,128]{2,1,0:T(8,128)}), f32[8,8,128]{2,1,0:T(8,128)S(1)}, u32[]{:S(2)}, u32[]{:S(2)}) %all-to-all-start.1) | async-done | bytes 32800 | tf_op jit(solution)/shard_map/all_to_all | solution.py:413
  77.1 1.3 %collective-permute-start.3 = (bf16[1,2,184,128]{3,2,1,0:T(8,128)(2,1)S(1)}, bf16[1,2,184,128]{3,2,1,0:T(8,128)(2,1)S(1)}, u32[]{:S(2)}, u32[]{:S(2)}) collective-permute-start(bf16[1,2,184,128]{3,2,1,0:T(8,128)(2,1)S(1)} %waves.5), channel_id=1, source_target_pairs={{0,64},{64,0},{1,65},{65,1},{2,66},{66,2},{3,67},{67,3},{4,68},{68... | collective-permute-start | bytes 282632 | tf_op jit(solution)/shard_map/ppermute | solution.py:430
  79.4 3.8 %collective-permute-done.1.refs_3_ = f32[8,128]{1,0:T(8,128)S(1)} collective-permute-done((f32[8,128]{1,0:T(8,128)S(1)}, f32[8,128]{1,0:T(8,128)S(1)}, u32[]{:S(2)}, u32[]{:S(2)}) %collective-permute-start.1) | collective-permute-done | bytes 4128 | tf_op jit(solution)/shard_map/ppermute | solution.py:469
  83.2 0.8 shard_map.105
  84.0 1.8 %join.3 = (f32[5,360,128]{2,1,0:T(8,128)}, f32[5,360,128]{2,1,0:T(8,128)}) custom-call(s32[1]{0:T(128)} %bitcast.1.half_ref.refs_0_, f32[1,2,184,128]{3,2,1,0:T(8,128)S(1)} %copy-done.5, bf16[1,2,184,128]{3,2,1,0:T(8,128)(2,1)} %collective-permute-done.7.refs_2_), custom_call_target="tpu_custom_call" | custom-call | tf_op jit(solution)/shard_map/join/pallas_call | solution.py:260
  85.8 2.1 %join.4 = (f32[5,360,128]{2,1,0:T(8,128)}, f32[5,360,128]{2,1,0:T(8,128)}) custom-call(s32[1]{0:T(128)} %bitcast.1.half_ref.refs_0_, f32[3,2,184,128]{3,2,1,0:T(8,128)S(1)} %get-tuple-element.34.refs_1_, bf16[3,2,184,128]{3,2,1,0:T(8,128)(2,1)} %collective-permute-done.5.refs_2_, ...), custom_call_target="tpu_custom_call", output_to_operand_aliasing={{0}: (3, {}), {1}: (4, {})} | custom-call | tf_op jit(solution)/shard_map/join/pallas_call | solution.py:260
  88.0 0.9 %join.5 = (f32[5,360,128]{2,1,0:T(8,128)}, f32[5,360,128]{2,1,0:T(8,128)}) custom-call(s32[1]{0:T(128)} %bitcast.1.half_ref.refs_0_, f32[1,2,184,128]{3,2,1,0:T(8,128)S(1)} %waves.4.refs_4_.refs_1_, bf16[1,2,184,128]{3,2,1,0:T(8,128)(2,1)S(1)} %collective-permute-done.3.refs_2_, ...), custom_call_target="tpu_custom_call", output_to_operand_aliasing={{0}: (3, {}), {1}: (4, {})} | custom-call | tf_op jit(solution)/shard_map/join/pallas_call | solution.py:260
  (27 shorter events, 2.3 us)
Async XLA Ops:
  2.4 40.6 %copy-start.7 = (f32[5,4,32]{2,1,0:T(4,128)S(1)}, f32[5,4,32]{2,1,0:T(4,128)}, u32[]{:S(2)}) copy-start(f32[5,4,32]{2,1,0:T(4,128)} %refs_4_.2) | copy-start | bytes 7684
  2.5 40.6 %copy-start.8 = (f32[32]{0:T(128)S(1)}, f32[32]{0:T(128)}, u32[]{:S(2)}) copy-start(f32[32]{0:T(128)} %param.11) | copy-start | bytes 388
  5.3 6.2 %copy-start.6 = (f32[10,128]{1,0:T(8,128)S(1)}, f32[10,128]{1,0:T(8,128)}, u32[]{:S(2)}) copy-start(f32[10,128]{1,0:T(8,128)} %sums.1.refs_1_.refs_5_) | copy-start | bytes 15364
  5.3 48.9 %copy-start = (bf16[2,2,368,720]{3,2,1,0:T(8,128)(2,1)S(1)}, bf16[2,2,368,720]{3,2,1,0:T(8,128)(2,1)}, u32[]{:S(2)}) copy-start(bf16[2,2,368,720]{3,2,1,0:T(8,128)(2,1)} %constant.29.clone.table_ref) | copy-start | bytes 6359044
  8.6 45.6 %collective-permute-start.4 = (bf16[3,192,720]{2,1,0:T(8,128)(2,1)}, bf16[3,192,720]{2,1,0:T(8,128)(2,1)}, u32[]{:S(2)}, u32[]{:S(2)}) collective-permute-start(bf16[3,192,720]{2,1,0:T(8,128)(2,1)} %get-tuple-element.33), channel_id=1, source_target_pairs={{0,64},{64,0},{1,65},{65,1},{2,66},{66,2},{3,67},{67,3},{4,68},{68... | collective-permute-start | bytes 2488328 | tf_op jit(solution)/shard_map/ppermute | solution.py:430
  9.5 59.0 %collective-permute-start.6 = (bf16[1,192,720]{2,1,0:T(8,128)(2,1)}, bf16[1,192,720]{2,1,0:T(8,128)(2,1)}, u32[]{:S(2)}, u32[]{:S(2)}) collective-permute-start(bf16[1,192,720]{2,1,0:T(8,128)(2,1)} %pack.1._), channel_id=1, source_target_pairs={{0,64},{64,0},{1,65},{65,1},{2,66},{66,2},{3,67},{67,3},{4,68},{68... | collective-permute-start | bytes 829448 | tf_op jit(solution)/shard_map/ppermute | solution.py:430
  10.7 65.9 %collective-permute-start.2 = (bf16[1,192,720]{2,1,0:T(8,128)(2,1)}, bf16[1,192,720]{2,1,0:T(8,128)(2,1)S(1)}, u32[]{:S(2)}, u32[]{:S(2)}) collective-permute-start(bf16[1,192,720]{2,1,0:T(8,128)(2,1)} %get-tuple-element.30), channel_id=1, source_target_pairs={{0,64},{64,0},{1,65},{65,1},{2,66},{66,2},{3,67},{67,3},{4,68},{68... | collective-permute-start | bytes 829448 | tf_op jit(solution)/shard_map/ppermute | solution.py:430
  11.5 31.6 %collective-permute-start = (f32[10,128]{1,0:T(8,128)S(1)}, f32[10,128]{1,0:T(8,128)S(1)}, u32[]{:S(2)}, u32[]{:S(2)}) collective-permute-start(f32[10,128]{1,0:T(8,128)S(1)} %copy-done.6), channel_id=1, source_target_pairs={{0,64},{64,0},{1,65},{65,1},{2,66},{66,2},{3,67},{67,3},{4,68},{68... | collective-permute-start | bytes 15368 | tf_op jit(solution)/shard_map/ppermute | solution.py:430
  54.2 1.2 %copy-start.2 = (bf16[3,192,720]{2,1,0:T(8,128)(2,1)S(1)}, bf16[3,192,720]{2,1,0:T(8,128)(2,1)}, u32[]{:S(2)}) copy-start(bf16[3,192,720]{2,1,0:T(8,128)(2,1)} %get-tuple-element.32.own_ref) | copy-start | bytes 2488324
  59.2 17.4 %copy-start.1 = (bf16[1,192,720]{2,1,0:T(8,128)(2,1)S(1)}, bf16[1,192,720]{2,1,0:T(8,128)(2,1)}, u32[]{:S(2)}) copy-start(bf16[1,192,720]{2,1,0:T(8,128)(2,1)} %get-tuple-element.29.own_ref) | copy-start | bytes 829444
  59.2 26.6 %collective-permute-start.5 = (bf16[3,2,184,128]{3,2,1,0:T(8,128)(2,1)}, bf16[3,2,184,128]{3,2,1,0:T(8,128)(2,1)}, u32[]{:S(2)}, u32[]{:S(2)}) collective-permute-start(bf16[3,2,184,128]{3,2,1,0:T(8,128)(2,1)} %get-tuple-element.35), channel_id=1, source_target_pairs={{0,64},{64,0},{1,65},{65,1},{2,66},{66,2},{3,67},{67,3},{4,68},{68... | collective-permute-start | bytes 847880 | tf_op jit(solution)/shard_map/ppermute | solution.py:430
  60.1 16.5 %all-to-all-start.1 = ((f32[8,8,128]{2,1,0:T(8,128)}), f32[8,8,128]{2,1,0:T(8,128)S(1)}, u32[]{:S(2)}, u32[]{:S(2)}) async-start(f32[8,8,128]{2,1,0:T(8,128)} %get-tuple-element.26._), calls=%async_computation.1 | async-start | bytes 65536 | tf_op jit(solution)/shard_map/all_to_all | solution.py:413
  68.5 1.0 %copy-start.3 = (bf16[1,192,720]{2,1,0:T(8,128)(2,1)S(1)}, bf16[1,192,720]{2,1,0:T(8,128)(2,1)}, u32[]{:S(2)}) copy-start(bf16[1,192,720]{2,1,0:T(8,128)(2,1)} %get-tuple-element.36.own_ref) | copy-start | bytes 829444
  71.9 0.7 copy-start.4
  72.6 11.4 %collective-permute-start.7 = (bf16[1,2,184,128]{3,2,1,0:T(8,128)(2,1)}, bf16[1,2,184,128]{3,2,1,0:T(8,128)(2,1)}, u32[]{:S(2)}, u32[]{:S(2)}) collective-permute-start(bf16[1,2,184,128]{3,2,1,0:T(8,128)(2,1)} %get-tuple-element.38), channel_id=1, source_target_pairs={{0,64},{64,0},{1,65},{65,1},{2,66},{66,2},{3,67},{67,3},{4,68},{68... | collective-permute-start | bytes 282632 | tf_op jit(solution)/shard_map/ppermute | solution.py:430
  77.1 6.9 %copy-start.5 = (f32[1,2,184,128]{3,2,1,0:T(8,128)S(1)}, f32[1,2,184,128]{3,2,1,0:T(8,128)}, u32[]{:S(2)}) copy-start(f32[1,2,184,128]{3,2,1,0:T(8,128)} %copy-done.4) | copy-start | bytes 565252
  77.1 10.8 %collective-permute-start.3 = (bf16[1,2,184,128]{3,2,1,0:T(8,128)(2,1)S(1)}, bf16[1,2,184,128]{3,2,1,0:T(8,128)(2,1)S(1)}, u32[]{:S(2)}, u32[]{:S(2)}) collective-permute-start(bf16[1,2,184,128]{3,2,1,0:T(8,128)(2,1)S(1)} %waves.5), channel_id=1, source_target_pairs={{0,64},{64,0},{1,65},{65,1},{2,66},{66,2},{3,67},{67,3},{4,68},{68... | collective-permute-start | bytes 282632 | tf_op jit(solution)/shard_map/ppermute | solution.py:430
  78.4 4.8 %collective-permute-start.1 = (f32[8,128]{1,0:T(8,128)S(1)}, f32[8,128]{1,0:T(8,128)S(1)}, u32[]{:S(2)}, u32[]{:S(2)}) collective-permute-start(f32[8,128]{1,0:T(8,128)S(1)} %get-tuple-element.28._.refs_2_), channel_id=1, source_target_pairs={{0,192},{64,128},{128,64},{192,0},{1,193},{65,129},{129,65},{193,1... | collective-permute-start | bytes 12296 | tf_op jit(solution)/shard_map/ppermute | solution.py:469

commit v3 on v1

--- a/solution.py
+++ b/solution.py
@@ -43,11 +43,51 @@
     return pltpu.CompilerParams(vmem_limit_bytes=mib * MIB)
 
 
+def main_lanes(lon):
+    return lon // 128 * 128
+
+
+def packed_shape(cols, lon):
+    main = main_lanes(lon)
+    return cols + cols // (main // (lon - main)), main
+
+
+def fold_tails(tail_ref, lon):
+    main = main_lanes(lon)
+    width = lon - main
+    parts = main // width
+    rows = tail_ref.shape[0] // parts
+    low = lax.broadcasted_iota(jnp.int32, (rows, 128), 1) < width
+    total = None
+    for j in range(parts):
+        piece = jnp.where(low, tail_ref[j * rows : (j + 1) * rows, :], 0.0)
+        wide = jnp.concatenate([piece, jnp.zeros((rows, main - 128), F32)], axis=1)
+        wide = pltpu.roll(wide, j * width, 1) if j else wide
+        total = wide if total is None else total + wide
+    return total
+
+
+def unfold_tails(folded, tail_ref, lon):
+    main = main_lanes(lon)
+    width = lon - main
+    rows = folded.shape[0]
+    for j in range(main // width):
+        wide = pltpu.roll(folded, main - j * width, 1) if j else folded
+        tail_ref[j * rows : (j + 1) * rows, :] = wide[:, :128]
+
+
+def put_packed(box, field, at, tail_ref, lon):
+    main = main_lanes(lon)
+    size = field.shape[0]
+    box[at : at + size, :] = field[:, :main]
+    tail_ref[at : at + size, 0 : lon - main] = field[:, main:].astype(F32)
+
+
 def keep_of(mask):
     return mask.astype(F32).astype(BF16)
 
 
-def pack_kernel(half_ref, u_ref, v_ref, t_ref, m_ref, o_ref, fields, mask, sems):
+def pack_kernel(half_ref, u_ref, v_ref, t_ref, m_ref, o_ref, fields, mask, tails, sems):
     part = fields.shape[1]
     at = pl.ds((1 - half_ref[0]) * part, part)
     copies = [pltpu.make_async_copy(m_ref.at[0], mask, sems.at[3])]
@@ -59,8 +99,10 @@
         c.wait()
     size = part * fields.shape[2]
     keep = keep_of(mask[...])[None]
+    lon = mask.shape[1]
     for f in range(3):
-        o_ref[0, f * size : (f + 1) * size, :] = (fields[f] * keep).reshape(size, -1)
+        put_packed(o_ref.at[0], (fields[f] * keep).reshape(size, lon), f * size, tails, lon)
+    o_ref[0, 3 * size :, :] = fold_tails(tails, lon).astype(BF16)
 
 
 def pack(half, u, v, t, mask):
@@ -68,12 +110,13 @@
     part = samples // 2
     return pl.pallas_call(
         pack_kernel,
-        out_shape=jax.ShapeDtypeStruct((1, 3 * part * levels, lon), BF16),
+        out_shape=jax.ShapeDtypeStruct((1, *packed_shape(3 * part * levels, lon)), BF16),
         in_specs=[SMEM, HBM, HBM, HBM, HBM],
         out_specs=VMEM,
         scratch_shapes=[
             pltpu.VMEM((3, part, levels, lon), BF16),
             pltpu.VMEM((levels, lon), jnp.int32),
+            pltpu.VMEM((3 * part * levels, 128), F32),
             pltpu.SemaphoreType.DMA((4,)),
         ],
         compiler_params=params(60),
@@ -124,7 +167,7 @@
 def send_kernel(groups, half_ref, u_ref, v_ref, t_ref, m_ref, _, *rest):
     n = len(groups)
     far_refs, near_refs = rest[: n - 1], rest[n - 1 : 2 * n - 1]
-    us, vs, ts, masks, fars, nears, sems, out_sems = rest[2 * n - 1 :]
+    us, vs, ts, masks, fars, nears, tails, sems, out_sems = rest[2 * n - 1 :]
     rows, samples, levels, lon = vs.shape
     part = samples // 2
     size = part * levels
@@ -152,8 +195,13 @@
                     continue
                 ref = far_refs[g - 1] if k == 0 else near_refs[g]
                 for f, field in enumerate((ts, us, vs)):
-                    mine = field[j, pl.ds(where * part, part)] * keep[None]
-                    box[j, f * size : (f + 1) * size, :] = mine.reshape(size, lon)
+                    mine = (field[j, pl.ds(where * part, part)] * keep[None]).reshape(size, lon)
+                    if k:
+                        box[j, f * size : (f + 1) * size, :] = mine
+                    else:
+                        put_packed(box.at[j], mine, f * size, tails.at[j], lon)
+                if not k:
+                    box[j, 3 * size :, :] = fold_tails(tails.at[j], lon).astype(BF16)
                 c = pltpu.make_async_copy(box.at[j], ref.at[i], out_sems.at[j, k])
                 c.start()
                 done.append(c)
@@ -166,11 +214,13 @@
     part = samples // 2
     unit = 3 * part * levels
     n = len(groups)
+    wire = packed_shape(unit, lon)
     packed = [jax.ShapeDtypeStruct((len(g), unit, lon), BF16) for g in groups]
+    sent = [jax.ShapeDtypeStruct((len(g), *wire), BF16) for g in groups[1:]]
     return pl.pallas_call(
         lambda *refs: send_kernel(groups, *refs),
         out_shape=(
-            *packed[1:],
+            *sent,
             *packed,
         ),
         in_specs=[SMEM, HBM, HBM, HBM, HBM, ANY],
@@ -180,8 +230,9 @@
             pltpu.VMEM((rows, samples, levels, lon), BF16),
             pltpu.VMEM((rows, samples, levels, lon), BF16),
             pltpu.VMEM((rows, levels, lon), jnp.int32),
+            pltpu.VMEM((rows, *wire), BF16),
             pltpu.VMEM((rows, unit, lon), BF16),
-            pltpu.VMEM((rows, unit, lon), BF16),
+            pltpu.VMEM((rows, unit, 128), F32),
             pltpu.SemaphoreType.DMA((rows, 4)),
             pltpu.SemaphoreType.DMA((rows, 2)),
         ],
@@ -190,13 +241,22 @@
     )(half, u, v, t, mask, after)
 
 
-def wave_kernel(half_ref, table_ref, own_ref, got_ref, _, *o_refs, flips):
+def wave_kernel(half_ref, table_ref, own_ref, got_ref, _, *refs, flips):
+    o_refs, (mix, tails) = refs[:-2], refs[-2:]
     n = table_ref.shape[2] // 2
+    cols, lon = own_ref.shape[1:]
+    main = main_lanes(lon)
     scale = 2.0 / (MERIDIANS * MERIDIANS)
     for i in range(got_ref.shape[0]):
-        own, got = own_ref[i].astype(F32), got_ref[i].astype(F32)
-        for p, mixed in enumerate(((own - got).astype(BF16), (own + got).astype(BF16))):
-            x = jnp.concatenate([mixed, mixed[2 * mixed.shape[0] // 3 :]])
+        unfold_tails(got_ref[i, cols:].astype(F32), tails.at[i], lon)
+        for at, end in ((0, main), (main, lon)):
+            own = own_ref[i, :, at:end].astype(F32)
+            got = tails[i, :, 0 : lon - main] if at else got_ref[i, 0:cols].astype(F32)
+            for p, mixed in enumerate(((own - got).astype(BF16), (own + got).astype(BF16))):
+                mix[i, p, 0:cols, at:end] = mixed
+                mix[i, p, cols:, at:end] = mixed[2 * cols // 3 :]
+        for p in range(2):
+            x = mix[i, p]
             w = x.shape[0] // 2
             for flip, o_ref in zip(flips, o_refs):
                 table = table_ref[1 - half_ref[0] if flip else half_ref[0], p]
@@ -206,13 +266,17 @@
 
 
 def waves(half, table, own, got, after, *flips):
-    rows, cols, _ = got.shape
+    rows, cols, lon = own.shape
     shape = (rows, 2, PADDED, 2 * cols // 3)
     return pl.pallas_call(
         functools.partial(wave_kernel, flips=flips),
         out_shape=tuple(jax.ShapeDtypeStruct(shape, BF16 if f else F32) for f in flips),
         in_specs=[SMEM, VMEM, VMEM, VMEM, ANY],
         out_specs=(VMEM,) * len(flips),
+        scratch_shapes=[
+            pltpu.VMEM((rows, 2, 4 * cols // 3, lon), BF16),
+            pltpu.VMEM((rows, cols, 128), F32),
+        ],
         compiler_params=params(16),
         name="waves",
     )(half, table, own, got, after)

time: 87.4 us -> 85.6 us (0.979)
  waiting for transfers between devices: 33.3 us -> 31.3 us
    ppermute x7, waiting for transfers between devices: 30.4 us -> 28.4 us  [swap(): return lax.ppermute(x, 'lon', across)]
where the time goes in v3:
time: 85.6 us; the launch traced here: 85.2 us
  waiting for transfers between devices  31.3 us (37%)
  blocking collectives  26.2 us (31%)
  Pallas kernels  17.5 us (20%)
  starting transfers between devices  8.41 us (10%)
  local copies, waits for them, and re-layouts  1.1 us (1%)
    ppermute x7, waiting for transfers between devices, swap(): return lax.ppermute(x, 'lon', across)  28.4 us
    all_to_all x2, blocking collectives, all_of(): return lax.all_to_all(x, axes, split_axis=0, concat_axis=0, tiled=True)  26.2 us
    ppermute x7, starting transfers between devices, swap(): return lax.ppermute(x, 'lon', across)  7.26 us
    pallas_call x4, Pallas kernels, waves(): pl.pallas_call(functools.partial(wave_kernel, flips=flips), out_shape=tup...  5.77 us
    pallas_call x1, Pallas kernels, send(): pl.pallas_call(lambda *refs: send_kernel(groups, *refs), out_shape=(*sent...  3.37 us
    ppermute x1, waiting for transfers between devices, per_device(): lax.ppermute(near_half, ('lat', 'lon'), [(i, 3 - i) for i in range(4)])  2.87 us
    pallas_call x1, Pallas kernels, zonal(): pl.pallas_call(sums_kernel, out_shape=jax.ShapeDtypeStruct((2 * rows, sam...  2.81 us
    pallas_call x2, Pallas kernels, join(): pl.pallas_call(lambda *refs: join_kernel(rows[0], parts, *refs), out_shap...  2.21 us
  transfers between devices with their start and end apart: 8, of which 2 were waited for; matrix products, arithmetic and copies ran while one was open for 0% of the time, Pallas kernels for 10%

profile of v3, /device:TPU:6, one launch (start us, length us, event | category | flops | bytes accessed | tf_op | source)
XLA Modules:
  0.0 85.2 jit_solution(3087756015081270931)
XLA Ops:
  0.6 1.9 %pack.1._ = bf16[1,216,640]{2,1,0:T(8,128)(2,1)} custom-call(s32[1]{0:T(128)} %bitcast.1.half_ref.refs_0_, bf16[5,4,32,720]{3,2,1,0:T(8,128)(2,1)} %refs_1_.1, bf16[5,4,32,720]{3,2,1,0:T(8,128)(2,1)} %refs_2_.1, bf16[5,4,32,720]{3,2,1,0:T(8,128)(2,1)} %refs_3_.1, s32[5,32,720]{2,1,0:T(8,128)} %refs_4_.3), custom_call_target="tpu_custom_call" | custom-call | tf_op jit(solution)/shard_map/pack/pallas_call | solution.py:111
  2.6 2.8 %sums.1.refs_1_.refs_5_ = f32[10,128]{1,0:T(8,128)} custom-call(bf16[5,4,32,720]{3,2,1,0:T(8,128)(2,1)} %refs_2_.1, s32[5,32,720]{2,1,0:T(8,128)} %refs_4_.3, bf16[1,216,640]{2,1,0:T(8,128)(2,1)} %pack.1._), custom_call_target="tpu_custom_call" | custom-call | tf_op jit(solution)/shard_map/sums/pallas_call | solution.py:152
  5.4 3.4 %send.1 = (bf16[2,216,640]{2,1,0:T(8,128)(2,1)}, bf16[2,216,640]{2,1,0:T(8,128)(2,1)}, bf16[1,192,720]{2,1,0:T(8,128)(2,1)}, bf16[2,192,720]{2,1,0:T(8,128)(2,1)}, bf16[2,192,720]{2,1,0:T(8,128)(2,1)}) custom-call(s32[1]{0:T(128)} %bitcast.1.half_ref.refs_0_, bf16[5,4,32,720]{3,2,1,0:T(8,128)(2,1)} %refs_1_.1, bf16[5,4,32,720]{3,2,1,0:T(8,128)(2,1)} %refs_2_.1, ...), custom_call_target="tpu_custom_call" | custom-call | tf_op jit(solution)/shard_map/send/pallas_call | solution.py:220
  8.8 0.9 %collective-permute-start.5 = (bf16[2,216,640]{2,1,0:T(8,128)(2,1)}, bf16[2,216,640]{2,1,0:T(8,128)(2,1)}, u32[]{:S(2)}, u32[]{:S(2)}) collective-permute-start(bf16[2,216,640]{2,1,0:T(8,128)(2,1)} %get-tuple-element.33), channel_id=1, source_target_pairs={{0,64},{64,0},{1,65},{65,1},{2,66},{66,2},{3,67},{67,3},{4,68},{68... | collective-permute-start | bytes 1658888 | tf_op jit(solution)/shard_map/ppermute | solution.py:494
  9.7 1.2 %collective-permute-start.2 = (bf16[2,216,640]{2,1,0:T(8,128)(2,1)}, bf16[2,216,640]{2,1,0:T(8,128)(2,1)S(1)}, u32[]{:S(2)}, u32[]{:S(2)}) collective-permute-start(bf16[2,216,640]{2,1,0:T(8,128)(2,1)} %get-tuple-element.28), channel_id=1, source_target_pairs={{0,64},{64,0},{1,65},{65,1},{2,66},{66,2},{3,67},{67,3},{4,68},{68... | collective-permute-start | bytes 1658888 | tf_op jit(solution)/shard_map/ppermute | solution.py:494
  10.9 0.8 collective-permute-start.4
  11.7 1.2 %collective-permute-start = (f32[10,128]{1,0:T(8,128)S(1)}, f32[10,128]{1,0:T(8,128)S(1)}, u32[]{:S(2)}, u32[]{:S(2)}) collective-permute-start(f32[10,128]{1,0:T(8,128)S(1)} %copy-done.4), channel_id=1, source_target_pairs={{0,64},{64,0},{1,65},{65,1},{2,66},{66,2},{3,67},{67,3},{4,68},{68... | collective-permute-start | bytes 15368 | tf_op jit(solution)/shard_map/ppermute | solution.py:494
  12.9 28.4 %collective-permute-done.refs_2_ = f32[10,128]{1,0:T(8,128)S(1)} collective-permute-done((f32[10,128]{1,0:T(8,128)S(1)}, f32[10,128]{1,0:T(8,128)S(1)}, u32[]{:S(2)}, u32[]{:S(2)}) %collective-permute-start) | collective-permute-done | bytes 5152 | tf_op jit(solution)/shard_map/ppermute | solution.py:494
  41.4 9.9 %all_to_all.10.refs_1_ = f32[8,16,128]{2,1,0:T(8,128)S(1)} all-to-all(f32[8,16,128]{2,1,0:T(8,128)S(1)} %shard_map.102._), channel_id=1, replica_groups=mesh['lat'=2,'lon'=2,'lev_0'=8,'lev_1'=4,'lev_2'=2] {'lev_1','lev_2'}, dimensions={0} | all-to-all | bytes 131072 | tf_op jit(solution)/shard_map/all_to_all | solution.py:477
  51.3 0.5 shard_map.103
  51.8 16.3 %all_to_all.11.refs_2_ = f32[8,8,128]{2,1,0:T(8,128)S(1)} all-to-all(f32[8,8,128]{2,1,0:T(8,128)S(1)} %get-tuple-element.24._), channel_id=1, replica_groups=mesh['lat'=2,'lon'=2,'lev_0'=8,'lev_1'=4,'lev_2'=2] {'lev_0'}, dimensions={0} | all-to-all | bytes 65536 | tf_op jit(solution)/shard_map/all_to_all | solution.py:477
  68.2 1.1 %copy-done.2 = bf16[2,192,720]{2,1,0:T(8,128)(2,1)S(1)} copy-done((bf16[2,192,720]{2,1,0:T(8,128)(2,1)S(1)}, bf16[2,192,720]{2,1,0:T(8,128)(2,1)}, u32[]{:S(2)}) %copy-start.2) | copy-done | bytes 552984
  69.3 2.4 %waves.7 = (bf16[2,2,184,128]{3,2,1,0:T(8,128)(2,1)S(1)}, f32[2,2,184,128]{3,2,1,0:T(8,128)S(1)}) custom-call(s32[1]{0:T(128)} %bitcast.1.half_ref.refs_0_, bf16[2,2,368,720]{3,2,1,0:T(8,128)(2,1)S(1)} %copy-done, bf16[2,192,720]{2,1,0:T(8,128)(2,1)S(1)} %copy-done.2, bf16[2,216,640]{2,1,0:T(8,128)(2,1)} %collective-permute-done.5.got_ref, ...), custom_call_target="tpu_custom_call" | custom-call | tf_op jit(solution)/shard_map/waves/pallas_call | solution.py:271
  71.7 0.9 %collective-permute-start.7 = (bf16[2,2,184,128]{3,2,1,0:T(8,128)(2,1)S(1)}, bf16[2,2,184,128]{3,2,1,0:T(8,128)(2,1)S(1)}, u32[]{:S(2)}, u32[]{:S(2)}) collective-permute-start(bf16[2,2,184,128]{3,2,1,0:T(8,128)(2,1)S(1)} %get-tuple-element.36), channel_id=1, source_target_pairs={{0,64},{64,0},{1,65},{65,1},{2,66},{66,2},{3,67},{67,3},{4,68},{68... | collective-permute-start | bytes 565256 | tf_op jit(solution)/shard_map/ppermute | solution.py:494
  72.6 0.8 waves.5
  73.4 1.3 %collective-permute-start.3 = (bf16[2,2,184,128]{3,2,1,0:T(8,128)(2,1)S(1)}, bf16[2,2,184,128]{3,2,1,0:T(8,128)(2,1)S(1)}, u32[]{:S(2)}, u32[]{:S(2)}) collective-permute-start(bf16[2,2,184,128]{3,2,1,0:T(8,128)(2,1)S(1)} %waves.5), channel_id=1, source_target_pairs={{0,64},{64,0},{1,65},{65,1},{2,66},{66,2},{3,67},{67,3},{4,68},{68... | collective-permute-start | bytes 565256 | tf_op jit(solution)/shard_map/ppermute | solution.py:494
  74.7 1.8 %waves.6 = (bf16[1,2,184,128]{3,2,1,0:T(8,128)(2,1)S(1)}, f32[1,2,184,128]{3,2,1,0:T(8,128)S(1)}) custom-call(s32[1]{0:T(128)} %bitcast.1.half_ref.refs_0_, bf16[2,2,368,720]{3,2,1,0:T(8,128)(2,1)S(1)} %copy-done, bf16[1,192,720]{2,1,0:T(8,128)(2,1)S(1)} %copy-done.3, bf16[1,216,640]{2,1,0:T(8,128)(2,1)} %collective-permute-done.4.got_ref, ...), custom_call_target="tpu_custom_call" | custom-call | tf_op jit(solution)/shard_map/waves/pallas_call | solution.py:271
  76.5 0.9 %collective-permute-start.6 = (bf16[1,2,184,128]{3,2,1,0:T(8,128)(2,1)S(1)}, bf16[1,2,184,128]{3,2,1,0:T(8,128)(2,1)S(1)}, u32[]{:S(2)}, u32[]{:S(2)}) collective-permute-start(bf16[1,2,184,128]{3,2,1,0:T(8,128)(2,1)S(1)} %get-tuple-element.35), channel_id=1, source_target_pairs={{0,64},{64,0},{1,65},{65,1},{2,66},{66,2},{3,67},{67,3},{4,68},{68... | collective-permute-start | bytes 282632 | tf_op jit(solution)/shard_map/ppermute | solution.py:494
  77.4 1.1 %collective-permute-start.1 = (f32[8,128]{1,0:T(8,128)S(1)}, f32[8,128]{1,0:T(8,128)S(1)}, u32[]{:S(2)}, u32[]{:S(2)}) collective-permute-start(f32[8,128]{1,0:T(8,128)S(1)} %get-tuple-element.26._.refs_2_), channel_id=1, source_target_pairs={{0,192},{64,128},{128,64},{192,0},{1,193},{65,129},{129,65},{193,1... | collective-permute-start | bytes 12296 | tf_op jit(solution)/shard_map/ppermute | solution.py:533
  78.5 0.8 waves.4.refs_4_.refs_1_
  79.3 2.9 %collective-permute-done.1.refs_3_ = f32[8,128]{1,0:T(8,128)S(1)} collective-permute-done((f32[8,128]{1,0:T(8,128)S(1)}, f32[8,128]{1,0:T(8,128)S(1)}, u32[]{:S(2)}, u32[]{:S(2)}) %collective-permute-start.1) | collective-permute-done | bytes 4128 | tf_op jit(solution)/shard_map/ppermute | solution.py:533
  82.2 0.8 shard_map.105
  83.0 1.2 %join.2 = (f32[5,360,128]{2,1,0:T(8,128)}, f32[5,360,128]{2,1,0:T(8,128)}) custom-call(s32[1]{0:T(128)} %bitcast.1.half_ref.refs_0_, f32[1,2,184,128]{3,2,1,0:T(8,128)S(1)} %get-tuple-element.31.refs_1_, f32[2,2,184,128]{3,2,1,0:T(8,128)S(1)} %get-tuple-element.34.refs_2_, bf16[1,2,184,128]{3,2,1,0:T(8,128)(2,1)S(1)} %collective-permute-done.6.refs_3_, ...), custom_call_target="tpu_custom_call" | custom-call | tf_op jit(solution)/shard_map/join/pallas_call | solution.py:324
  84.2 1.0 %join.3 = (f32[5,360,128]{2,1,0:T(8,128)}, f32[5,360,128]{2,1,0:T(8,128)}) custom-call(s32[1]{0:T(128)} %bitcast.1.half_ref.refs_0_, f32[2,2,184,128]{3,2,1,0:T(8,128)S(1)} %waves.4.refs_4_.refs_1_, bf16[2,2,184,128]{3,2,1,0:T(8,128)(2,1)S(1)} %collective-permute-done.3.refs_2_, ...), custom_call_target="tpu_custom_call", output_to_operand_aliasing={{0}: (3, {}), {1}: (4, {})} | custom-call | tf_op jit(solution)/shard_map/join/pallas_call | solution.py:324
  (21 shorter events, 0.2 us)
Async XLA Ops:
  2.5 38.8 %copy-start.5 = (f32[5,4,32]{2,1,0:T(4,128)S(1)}, f32[5,4,32]{2,1,0:T(4,128)}, u32[]{:S(2)}) copy-start(f32[5,4,32]{2,1,0:T(4,128)} %refs_4_.2) | copy-start | bytes 7684
  2.6 38.8 %copy-start.6 = (f32[32]{0:T(128)S(1)}, f32[32]{0:T(128)}, u32[]{:S(2)}) copy-start(f32[32]{0:T(128)} %param.11) | copy-start | bytes 388
  5.4 6.4 %copy-start.4 = (f32[10,128]{1,0:T(8,128)S(1)}, f32[10,128]{1,0:T(8,128)}, u32[]{:S(2)}) copy-start(f32[10,128]{1,0:T(8,128)} %sums.1.refs_1_.refs_5_) | copy-start | bytes 15364
  5.4 62.8 %copy-start = (bf16[2,2,368,720]{3,2,1,0:T(8,128)(2,1)S(1)}, bf16[2,2,368,720]{3,2,1,0:T(8,128)(2,1)}, u32[]{:S(2)}) copy-start(bf16[2,2,368,720]{3,2,1,0:T(8,128)(2,1)} %constant.29.clone.table_ref) | copy-start | bytes 6359044
  8.8 63.8 %copy-start.1 = (bf16[2,192,720]{2,1,0:T(8,128)(2,1)S(1)}, bf16[2,192,720]{2,1,0:T(8,128)(2,1)}, u32[]{:S(2)}) copy-start(bf16[2,192,720]{2,1,0:T(8,128)(2,1)} %get-tuple-element.27.own_ref) | copy-start | bytes 1658884
  8.8 59.4 %collective-permute-start.5 = (bf16[2,216,640]{2,1,0:T(8,128)(2,1)}, bf16[2,216,640]{2,1,0:T(8,128)(2,1)}, u32[]{:S(2)}, u32[]{:S(2)}) collective-permute-start(bf16[2,216,640]{2,1,0:T(8,128)(2,1)} %get-tuple-element.33), channel_id=1, source_target_pairs={{0,64},{64,0},{1,65},{65,1},{2,66},{66,2},{3,67},{67,3},{4,68},{68... | collective-permute-start | bytes 1658888 | tf_op jit(solution)/shard_map/ppermute | solution.py:494
  9.7 62.9 %collective-permute-start.2 = (bf16[2,216,640]{2,1,0:T(8,128)(2,1)}, bf16[2,216,640]{2,1,0:T(8,128)(2,1)S(1)}, u32[]{:S(2)}, u32[]{:S(2)}) collective-permute-start(bf16[2,216,640]{2,1,0:T(8,128)(2,1)} %get-tuple-element.28), channel_id=1, source_target_pairs={{0,64},{64,0},{1,65},{65,1},{2,66},{66,2},{3,67},{67,3},{4,68},{68... | collective-permute-start | bytes 1658888 | tf_op jit(solution)/shard_map/ppermute | solution.py:494
  10.9 63.8 %collective-permute-start.4 = (bf16[1,216,640]{2,1,0:T(8,128)(2,1)}, bf16[1,216,640]{2,1,0:T(8,128)(2,1)}, u32[]{:S(2)}, u32[]{:S(2)}) collective-permute-start(bf16[1,216,640]{2,1,0:T(8,128)(2,1)} %pack.1._), channel_id=1, source_target_pairs={{0,64},{64,0},{1,65},{65,1},{2,66},{66,2},{3,67},{67,3},{4,68},{68... | collective-permute-start | bytes 829448 | tf_op jit(solution)/shard_map/ppermute | solution.py:494
  11.7 29.6 %collective-permute-start = (f32[10,128]{1,0:T(8,128)S(1)}, f32[10,128]{1,0:T(8,128)S(1)}, u32[]{:S(2)}, u32[]{:S(2)}) collective-permute-start(f32[10,128]{1,0:T(8,128)S(1)} %copy-done.4), channel_id=1, source_target_pairs={{0,64},{64,0},{1,65},{65,1},{2,66},{66,2},{3,67},{67,3},{4,68},{68... | collective-permute-start | bytes 15368 | tf_op jit(solution)/shard_map/ppermute | solution.py:494
  68.2 1.1 %copy-start.2 = (bf16[2,192,720]{2,1,0:T(8,128)(2,1)S(1)}, bf16[2,192,720]{2,1,0:T(8,128)(2,1)}, u32[]{:S(2)}) copy-start(bf16[2,192,720]{2,1,0:T(8,128)(2,1)} %get-tuple-element.32.own_ref) | copy-start | bytes 1658884
  71.7 3.0 %copy-start.3 = (bf16[1,192,720]{2,1,0:T(8,128)(2,1)S(1)}, bf16[1,192,720]{2,1,0:T(8,128)(2,1)}, u32[]{:S(2)}) copy-start(bf16[1,192,720]{2,1,0:T(8,128)(2,1)} %get-tuple-element.30.own_ref) | copy-start | bytes 829444
  71.7 11.3 %collective-permute-start.7 = (bf16[2,2,184,128]{3,2,1,0:T(8,128)(2,1)S(1)}, bf16[2,2,184,128]{3,2,1,0:T(8,128)(2,1)S(1)}, u32[]{:S(2)}, u32[]{:S(2)}) collective-permute-start(bf16[2,2,184,128]{3,2,1,0:T(8,128)(2,1)S(1)} %get-tuple-element.36), channel_id=1, source_target_pairs={{0,64},{64,0},{1,65},{65,1},{2,66},{66,2},{3,67},{67,3},{4,68},{68... | collective-permute-start | bytes 565256 | tf_op jit(solution)/shard_map/ppermute | solution.py:494
  73.4 10.8 %collective-permute-start.3 = (bf16[2,2,184,128]{3,2,1,0:T(8,128)(2,1)S(1)}, bf16[2,2,184,128]{3,2,1,0:T(8,128)(2,1)S(1)}, u32[]{:S(2)}, u32[]{:S(2)}) collective-permute-start(bf16[2,2,184,128]{3,2,1,0:T(8,128)(2,1)S(1)} %waves.5), channel_id=1, source_target_pairs={{0,64},{64,0},{1,65},{65,1},{2,66},{66,2},{3,67},{67,3},{4,68},{68... | collective-permute-start | bytes 565256 | tf_op jit(solution)/shard_map/ppermute | solution.py:494
  76.5 6.5 %collective-permute-start.6 = (bf16[1,2,184,128]{3,2,1,0:T(8,128)(2,1)S(1)}, bf16[1,2,184,128]{3,2,1,0:T(8,128)(2,1)S(1)}, u32[]{:S(2)}, u32[]{:S(2)}) collective-permute-start(bf16[1,2,184,128]{3,2,1,0:T(8,128)(2,1)S(1)} %get-tuple-element.35), channel_id=1, source_target_pairs={{0,64},{64,0},{1,65},{65,1},{2,66},{66,2},{3,67},{67,3},{4,68},{68... | collective-permute-start | bytes 282632 | tf_op jit(solution)/shard_map/ppermute | solution.py:494
  77.4 4.8 %collective-permute-start.1 = (f32[8,128]{1,0:T(8,128)S(1)}, f32[8,128]{1,0:T(8,128)S(1)}, u32[]{:S(2)}, u32[]{:S(2)}) collective-permute-start(f32[8,128]{1,0:T(8,128)S(1)} %get-tuple-element.26._.refs_2_), channel_id=1, source_target_pairs={{0,192},{64,128},{128,64},{192,0},{1,193},{65,129},{129,65},{193,1... | collective-permute-start | bytes 12296 | tf_op jit(solution)/shard_map/ppermute | solution.py:533

commit v4 on v3

--- a/solution.py
+++ b/solution.py
@@ -124,50 +124,10 @@
     )(half, u, v, t, mask)
 
 
-def sums_kernel(v_ref, m_ref, _, sums_ref, vs, masks, sems):
-    rows, samples, levels, lon = vs.shape
-    copies = [
-        (
-            pltpu.make_async_copy(m_ref.at[j], masks.at[j], sems.at[j, 0]),
-            pltpu.make_async_copy(v_ref.at[j], vs.at[j], sems.at[j, 1]),
-        )
-        for j in range(rows)
-    ]
-    for group in copies:
-        for c in group:
-            c.start()
-    ones = jnp.ones((8, lon), BF16)
-    for j in range(rows):
-        for c in copies[j]:
-            c.wait()
-        keep = keep_of(masks[j])
-        v = (vs[j] * keep[None]).reshape(samples * levels, lon)
-        sums_ref[j : j + 1, :] = lax.dot_general(ones, v, CONTRACT, preferred_element_type=F32)[0:1]
-        kept = lax.dot_general(ones, keep, CONTRACT, preferred_element_type=F32)[0:1]
-        sums_ref[rows + j : rows + j + 1, :] = jnp.concatenate([kept] * samples, axis=1)
-
-
-def zonal(v, mask, after):
-    rows, samples, levels, lon = v.shape
-    return pl.pallas_call(
-        sums_kernel,
-        out_shape=jax.ShapeDtypeStruct((2 * rows, samples * levels), F32),
-        in_specs=[HBM, HBM, ANY],
-        out_specs=VMEM,
-        scratch_shapes=[
-            pltpu.VMEM((rows, samples, levels, lon), BF16),
-            pltpu.VMEM((rows, levels, lon), jnp.int32),
-            pltpu.SemaphoreType.DMA((rows, 2)),
-        ],
-        compiler_params=params(60),
-        name="sums",
-    )(v, mask, after)
-
-
 def send_kernel(groups, half_ref, u_ref, v_ref, t_ref, m_ref, _, *rest):
     n = len(groups)
-    far_refs, near_refs = rest[: n - 1], rest[n - 1 : 2 * n - 1]
-    us, vs, ts, masks, fars, nears, tails, sems, out_sems = rest[2 * n - 1 :]
+    far_refs, near_refs, sums_ref = rest[: n - 1], rest[n - 1 : 2 * n - 1], rest[2 * n - 1]
+    us, vs, ts, masks, fars, nears, tails, sems, out_sems = rest[2 * n :]
     rows, samples, levels, lon = vs.shape
     part = samples // 2
     size = part * levels
@@ -184,12 +144,19 @@
         for c in group:
             c.start()
         copies.append(group)
+    ones = jnp.ones((8, lon), BF16)
     done = []
     for g, group in enumerate(groups):
         for i, j in enumerate(group):
             for c in copies[j]:
                 c.wait()
             keep = keep_of(masks[j])
+            v = (vs[j] * keep[None]).reshape(samples * levels, lon)
+            sums_ref[j : j + 1, :] = lax.dot_general(
+                ones, v, CONTRACT, preferred_element_type=F32
+            )[0:1]
+            kept = lax.dot_general(ones, keep, CONTRACT, preferred_element_type=F32)[0:1]
+            sums_ref[rows + j : rows + j + 1, :] = jnp.concatenate([kept] * samples, axis=1)
             for k, (where, box) in enumerate(((far, fars), (near, nears))):
                 if k == 0 and g == 0:
                     continue
@@ -222,9 +189,10 @@
         out_shape=(
             *sent,
             *packed,
+            jax.ShapeDtypeStruct((2 * rows, samples * levels), F32),
         ),
         in_specs=[SMEM, HBM, HBM, HBM, HBM, ANY],
-        out_specs=(HBM,) * (2 * n - 1),
+        out_specs=(HBM,) * (2 * n - 1) + (VMEM,),
         scratch_shapes=[
             pltpu.VMEM((rows, samples, levels, lon), BF16),
             pltpu.VMEM((rows, samples, levels, lon), BF16),
@@ -494,8 +462,7 @@
         return lax.ppermute(x, "lon", across)
 
     first = pack(half, u, v, t, mask)
-    sums = zonal(v, mask, first)
-    packed = send(half, u, v, t, mask, sums, GROUPS)
+    *packed, sums = send(half, u, v, t, mask, first, GROUPS)
     rest, own = packed[: len(GROUPS) - 1], packed[len(GROUPS) - 1 :]
     got = [swap(first)]
     by_lon = swap(sums)

time: 85.6 us -> 84.2 us (0.984)
  Pallas kernels: 17.5 us -> 15.4 us
    pallas_call x1 -> x0, Pallas kernels: 2.81 us -> none  [zonal(): pl.pallas_call(sums_kernel, out_shape=jax.ShapeDtypeStruct((2 * rows, sam...]
where the time goes in v4:
time: 84.2 us; the launch traced here: 83.9 us
  waiting for transfers between devices  31.3 us (37%)
  blocking collectives  26.2 us (31%)
  Pallas kernels  15.4 us (18%)
  starting transfers between devices  8.39 us (10%)
  local copies, waits for them, and re-layouts  1.79 us (2%)
    ppermute x7, waiting for transfers between devices, swap(): return lax.ppermute(x, 'lon', across)  28.4 us
    all_to_all x2, blocking collectives, all_of(): return lax.all_to_all(x, axes, split_axis=0, concat_axis=0, tiled=True)  26.2 us
    ppermute x7, starting transfers between devices, swap(): return lax.ppermute(x, 'lon', across)  7.26 us
    pallas_call x4, Pallas kernels, waves(): pl.pallas_call(functools.partial(wave_kernel, flips=flips), out_shape=tup...  5.77 us
    pallas_call x1, Pallas kernels, send(): pl.pallas_call(lambda *refs: send_kernel(groups, *refs), out_shape=(*sent...  4.14 us
    ppermute x1, waiting for transfers between devices, per_device(): lax.ppermute(near_half, ('lat', 'lon'), [(i, 3 - i) for i in range(4)])  2.89 us
    pallas_call x2, Pallas kernels, join(): pl.pallas_call(lambda *refs: join_kernel(rows[0], parts, *refs), out_shap...  2.22 us
    pallas_call x1, Pallas kernels, pack(): pl.pallas_call(pack_kernel, out_shape=jax.ShapeDtypeStruct((1, *packed_sh...  1.9 us
  transfers between devices with their start and end apart: 8, of which 2 were waited for; matrix products, arithmetic and copies ran while one was open for 0% of the time, Pallas kernels for 10%

profile of v4, /device:TPU:6, one launch (start us, length us, event | category | flops | bytes accessed | tf_op | source)
XLA Modules:
  0.0 83.9 jit_solution(12856935686138631813)
XLA Ops:
  0.6 1.9 %pack.1.refs_5_ = bf16[1,216,640]{2,1,0:T(8,128)(2,1)} custom-call(s32[1]{0:T(128)} %bitcast.1.half_ref.refs_0_, bf16[5,4,32,720]{3,2,1,0:T(8,128)(2,1)} %refs_1_.1, bf16[5,4,32,720]{3,2,1,0:T(8,128)(2,1)} %refs_2_.1, bf16[5,4,32,720]{3,2,1,0:T(8,128)(2,1)} %refs_3_.1, s32[5,32,720]{2,1,0:T(8,128)} %refs_4_.2), custom_call_target="tpu_custom_call" | custom-call | tf_op jit(solution)/shard_map/pack/pallas_call | solution.py:111
  2.6 4.1 %send.1 = (bf16[2,216,640]{2,1,0:T(8,128)(2,1)}, bf16[2,216,640]{2,1,0:T(8,128)(2,1)}, bf16[1,192,720]{2,1,0:T(8,128)(2,1)}, bf16[2,192,720]{2,1,0:T(8,128)(2,1)...) custom-call(s32[1]{0:T(128)} %bitcast.1.half_ref.refs_0_, bf16[5,4,32,720]{3,2,1,0:T(8,128)(2,1)} %refs_1_.1, ...), custom_call_target="tpu_custom_call" | custom-call | tf_op jit(solution)/shard_map/send/pallas_call | solution.py:187
  6.7 0.9 %collective-permute-start.5 = (bf16[2,216,640]{2,1,0:T(8,128)(2,1)}, bf16[2,216,640]{2,1,0:T(8,128)(2,1)}, u32[]{:S(2)}, u32[]{:S(2)}) collective-permute-start(bf16[2,216,640]{2,1,0:T(8,128)(2,1)} %get-tuple-element.35), channel_id=1, source_target_pairs={{0,64},{64,0},{1,65},{65,1},{2,66},{66,2},{3,67},{67,3},{4,68},{68... | collective-permute-start | bytes 1658888 | tf_op jit(solution)/shard_map/ppermute | solution.py:462
  7.6 1.2 %collective-permute-start.2 = (bf16[2,216,640]{2,1,0:T(8,128)(2,1)}, bf16[2,216,640]{2,1,0:T(8,128)(2,1)S(1)}, u32[]{:S(2)}, u32[]{:S(2)}) collective-permute-start(bf16[2,216,640]{2,1,0:T(8,128)(2,1)} %get-tuple-element.30), channel_id=1, source_target_pairs={{0,64},{64,0},{1,65},{65,1},{2,66},{66,2},{3,67},{67,3},{4,68},{68... | collective-permute-start | bytes 1658888 | tf_op jit(solution)/shard_map/ppermute | solution.py:462
  8.8 0.8 collective-permute-start.4
  9.7 1.2 %collective-permute-start = (f32[10,128]{1,0:T(8,128)}, f32[10,128]{1,0:T(8,128)S(1)}, u32[]{:S(2)}, u32[]{:S(2)}) collective-permute-start(f32[10,128]{1,0:T(8,128)} %get-tuple-element.24.refs_1_), channel_id=1, source_target_pairs={{0,64},{64,0},{1,65},{65,1},{2,66},{66,2},{3,67},{67,3},{4,68},{68... | collective-permute-start | bytes 15368 | tf_op jit(solution)/shard_map/ppermute | solution.py:462
  10.9 28.4 %collective-permute-done.refs_2_ = f32[10,128]{1,0:T(8,128)S(1)} collective-permute-done((f32[10,128]{1,0:T(8,128)}, f32[10,128]{1,0:T(8,128)S(1)}, u32[]{:S(2)}, u32[]{:S(2)}) %collective-permute-start) | collective-permute-done | bytes 5152 | tf_op jit(solution)/shard_map/ppermute | solution.py:462
  39.3 0.7 copy-done.5
  40.1 9.9 %all_to_all.10.refs_1_ = f32[8,16,128]{2,1,0:T(8,128)S(1)} all-to-all(f32[8,16,128]{2,1,0:T(8,128)S(1)} %shard_map.102._), channel_id=1, replica_groups=mesh['lat'=2,'lon'=2,'lev_0'=8,'lev_1'=4,'lev_2'=2] {'lev_1','lev_2'}, dimensions={0} | all-to-all | bytes 131072 | tf_op jit(solution)/shard_map/all_to_all | solution.py:445
  50.0 0.5 shard_map.103
  50.5 16.3 %all_to_all.11.refs_2_ = f32[8,8,128]{2,1,0:T(8,128)S(1)} all-to-all(f32[8,8,128]{2,1,0:T(8,128)S(1)} %get-tuple-element.26._), channel_id=1, replica_groups=mesh['lat'=2,'lon'=2,'lev_0'=8,'lev_1'=4,'lev_2'=2] {'lev_0'}, dimensions={0} | all-to-all | bytes 65536 | tf_op jit(solution)/shard_map/all_to_all | solution.py:445
  66.8 1.1 %copy-done.2 = bf16[2,192,720]{2,1,0:T(8,128)(2,1)S(1)} copy-done((bf16[2,192,720]{2,1,0:T(8,128)(2,1)S(1)}, bf16[2,192,720]{2,1,0:T(8,128)(2,1)}, u32[]{:S(2)}) %copy-start.2) | copy-done | bytes 552984
  67.9 2.4 %waves.7 = (bf16[2,2,184,128]{3,2,1,0:T(8,128)(2,1)S(1)}, f32[2,2,184,128]{3,2,1,0:T(8,128)S(1)}) custom-call(s32[1]{0:T(128)} %bitcast.1.half_ref.refs_0_, bf16[2,2,368,720]{3,2,1,0:T(8,128)(2,1)S(1)} %copy-done, bf16[2,192,720]{2,1,0:T(8,128)(2,1)S(1)} %copy-done.2, bf16[2,216,640]{2,1,0:T(8,128)(2,1)} %collective-permute-done.5.got_ref, ...), custom_call_target="tpu_custom_call" | custom-call | tf_op jit(solution)/shard_map/waves/pallas_call | solution.py:239
  70.3 0.9 %collective-permute-start.7 = (bf16[2,2,184,128]{3,2,1,0:T(8,128)(2,1)S(1)}, bf16[2,2,184,128]{3,2,1,0:T(8,128)(2,1)S(1)}, u32[]{:S(2)}, u32[]{:S(2)}) collective-permute-start(bf16[2,2,184,128]{3,2,1,0:T(8,128)(2,1)S(1)} %get-tuple-element.38), channel_id=1, source_target_pairs={{0,64},{64,0},{1,65},{65,1},{2,66},{66,2},{3,67},{67,3},{4,68},{68... | collective-permute-start | bytes 565256 | tf_op jit(solution)/shard_map/ppermute | solution.py:462
  71.3 0.8 waves.5
  72.1 1.3 %collective-permute-start.3 = (bf16[2,2,184,128]{3,2,1,0:T(8,128)(2,1)S(1)}, bf16[2,2,184,128]{3,2,1,0:T(8,128)(2,1)S(1)}, u32[]{:S(2)}, u32[]{:S(2)}) collective-permute-start(bf16[2,2,184,128]{3,2,1,0:T(8,128)(2,1)S(1)} %waves.5), channel_id=1, source_target_pairs={{0,64},{64,0},{1,65},{65,1},{2,66},{66,2},{3,67},{67,3},{4,68},{68... | collective-permute-start | bytes 565256 | tf_op jit(solution)/shard_map/ppermute | solution.py:462
  73.3 1.8 %waves.6 = (bf16[1,2,184,128]{3,2,1,0:T(8,128)(2,1)S(1)}, f32[1,2,184,128]{3,2,1,0:T(8,128)S(1)}) custom-call(s32[1]{0:T(128)} %bitcast.1.half_ref.refs_0_, bf16[2,2,368,720]{3,2,1,0:T(8,128)(2,1)S(1)} %copy-done, bf16[1,192,720]{2,1,0:T(8,128)(2,1)S(1)} %copy-done.3, bf16[1,216,640]{2,1,0:T(8,128)(2,1)} %collective-permute-done.4.got_ref, ...), custom_call_target="tpu_custom_call" | custom-call | tf_op jit(solution)/shard_map/waves/pallas_call | solution.py:239
  75.1 0.9 %collective-permute-start.6 = (bf16[1,2,184,128]{3,2,1,0:T(8,128)(2,1)S(1)}, bf16[1,2,184,128]{3,2,1,0:T(8,128)(2,1)S(1)}, u32[]{:S(2)}, u32[]{:S(2)}) collective-permute-start(bf16[1,2,184,128]{3,2,1,0:T(8,128)(2,1)S(1)} %get-tuple-element.37), channel_id=1, source_target_pairs={{0,64},{64,0},{1,65},{65,1},{2,66},{66,2},{3,67},{67,3},{4,68},{68... | collective-permute-start | bytes 282632 | tf_op jit(solution)/shard_map/ppermute | solution.py:462
  76.0 1.1 %collective-permute-start.1 = (f32[8,128]{1,0:T(8,128)S(1)}, f32[8,128]{1,0:T(8,128)S(1)}, u32[]{:S(2)}, u32[]{:S(2)}) collective-permute-start(f32[8,128]{1,0:T(8,128)S(1)} %get-tuple-element.28._.refs_2_), channel_id=1, source_target_pairs={{0,192},{64,128},{128,64},{192,0},{1,193},{65,129},{129,65},{193,1... | collective-permute-start | bytes 12296 | tf_op jit(solution)/shard_map/ppermute | solution.py:500
  77.2 0.8 waves.4.refs_4_.refs_1_
  78.0 2.9 %collective-permute-done.1.refs_3_ = f32[8,128]{1,0:T(8,128)S(1)} collective-permute-done((f32[8,128]{1,0:T(8,128)S(1)}, f32[8,128]{1,0:T(8,128)S(1)}, u32[]{:S(2)}, u32[]{:S(2)}) %collective-permute-start.1) | collective-permute-done | bytes 4128 | tf_op jit(solution)/shard_map/ppermute | solution.py:500
  80.9 0.8 shard_map.105
  81.7 1.2 %join.2 = (f32[5,360,128]{2,1,0:T(8,128)}, f32[5,360,128]{2,1,0:T(8,128)}) custom-call(s32[1]{0:T(128)} %bitcast.1.half_ref.refs_0_, f32[1,2,184,128]{3,2,1,0:T(8,128)S(1)} %get-tuple-element.33.refs_1_, f32[2,2,184,128]{3,2,1,0:T(8,128)S(1)} %get-tuple-element.36.refs_2_, bf16[1,2,184,128]{3,2,1,0:T(8,128)(2,1)S(1)} %collective-permute-done.6.refs_3_, ...), custom_call_target="tpu_custom_call" | custom-call | tf_op jit(solution)/shard_map/join/pallas_call | solution.py:292
  82.8 1.0 %join.3 = (f32[5,360,128]{2,1,0:T(8,128)}, f32[5,360,128]{2,1,0:T(8,128)}) custom-call(s32[1]{0:T(128)} %bitcast.1.half_ref.refs_0_, f32[2,2,184,128]{3,2,1,0:T(8,128)S(1)} %waves.4.refs_4_.refs_1_, bf16[2,2,184,128]{3,2,1,0:T(8,128)(2,1)S(1)} %collective-permute-done.3.refs_2_, ...), custom_call_target="tpu_custom_call", output_to_operand_aliasing={{0}: (3, {}), {1}: (4, {})} | custom-call | tf_op jit(solution)/shard_map/join/pallas_call | solution.py:292
  (20 shorter events, 0.2 us)
Async XLA Ops:
  2.5 36.7 %copy-start.4 = (f32[5,4,32]{2,1,0:T(4,128)S(1)}, f32[5,4,32]{2,1,0:T(4,128)}, u32[]{:S(2)}) copy-start(f32[5,4,32]{2,1,0:T(4,128)} %refs_4_.3) | copy-start | bytes 7684
  2.6 36.7 %copy-start.6 = (f32[32]{0:T(128)S(1)}, f32[32]{0:T(128)}, u32[]{:S(2)}) copy-start(f32[32]{0:T(128)} %param.11) | copy-start | bytes 388
  2.6 64.2 %copy-start = (bf16[2,2,368,720]{3,2,1,0:T(8,128)(2,1)S(1)}, bf16[2,2,368,720]{3,2,1,0:T(8,128)(2,1)}, u32[]{:S(2)}) copy-start(bf16[2,2,368,720]{3,2,1,0:T(8,128)(2,1)} %constant.29.clone.table_ref) | copy-start | bytes 6359044
  6.7 64.5 %copy-start.1 = (bf16[2,192,720]{2,1,0:T(8,128)(2,1)S(1)}, bf16[2,192,720]{2,1,0:T(8,128)(2,1)}, u32[]{:S(2)}) copy-start(bf16[2,192,720]{2,1,0:T(8,128)(2,1)} %get-tuple-element.29.own_ref) | copy-start | bytes 1658884
  6.7 60.1 %collective-permute-start.5 = (bf16[2,216,640]{2,1,0:T(8,128)(2,1)}, bf16[2,216,640]{2,1,0:T(8,128)(2,1)}, u32[]{:S(2)}, u32[]{:S(2)}) collective-permute-start(bf16[2,216,640]{2,1,0:T(8,128)(2,1)} %get-tuple-element.35), channel_id=1, source_target_pairs={{0,64},{64,0},{1,65},{65,1},{2,66},{66,2},{3,67},{67,3},{4,68},{68... | collective-permute-start | bytes 1658888 | tf_op jit(solution)/shard_map/ppermute | solution.py:462
  7.6 63.6 %collective-permute-start.2 = (bf16[2,216,640]{2,1,0:T(8,128)(2,1)}, bf16[2,216,640]{2,1,0:T(8,128)(2,1)S(1)}, u32[]{:S(2)}, u32[]{:S(2)}) collective-permute-start(bf16[2,216,640]{2,1,0:T(8,128)(2,1)} %get-tuple-element.30), channel_id=1, source_target_pairs={{0,64},{64,0},{1,65},{65,1},{2,66},{66,2},{3,67},{67,3},{4,68},{68... | collective-permute-start | bytes 1658888 | tf_op jit(solution)/shard_map/ppermute | solution.py:462
  8.8 64.5 %collective-permute-start.4 = (bf16[1,216,640]{2,1,0:T(8,128)(2,1)}, bf16[1,216,640]{2,1,0:T(8,128)(2,1)}, u32[]{:S(2)}, u32[]{:S(2)}) collective-permute-start(bf16[1,216,640]{2,1,0:T(8,128)(2,1)} %pack.1.refs_5_), channel_id=1, source_target_pairs={{0,64},{64,0},{1,65},{65,1},{2,66},{66,2},{3,67},{67,3},{4,68},{68... | collective-permute-start | bytes 829448 | tf_op jit(solution)/shard_map/ppermute | solution.py:462
  9.7 29.6 %collective-permute-start = (f32[10,128]{1,0:T(8,128)}, f32[10,128]{1,0:T(8,128)S(1)}, u32[]{:S(2)}, u32[]{:S(2)}) collective-permute-start(f32[10,128]{1,0:T(8,128)} %get-tuple-element.24.refs_1_), channel_id=1, source_target_pairs={{0,64},{64,0},{1,65},{65,1},{2,66},{66,2},{3,67},{67,3},{4,68},{68... | collective-permute-start | bytes 15368 | tf_op jit(solution)/shard_map/ppermute | solution.py:462
  39.3 0.7 copy-start.5
  66.8 1.1 %copy-start.2 = (bf16[2,192,720]{2,1,0:T(8,128)(2,1)S(1)}, bf16[2,192,720]{2,1,0:T(8,128)(2,1)}, u32[]{:S(2)}) copy-start(bf16[2,192,720]{2,1,0:T(8,128)(2,1)} %get-tuple-element.34.own_ref) | copy-start | bytes 1658884
  70.3 3.0 %copy-start.3 = (bf16[1,192,720]{2,1,0:T(8,128)(2,1)S(1)}, bf16[1,192,720]{2,1,0:T(8,128)(2,1)}, u32[]{:S(2)}) copy-start(bf16[1,192,720]{2,1,0:T(8,128)(2,1)} %get-tuple-element.32.own_ref) | copy-start | bytes 829444
  70.3 11.3 %collective-permute-start.7 = (bf16[2,2,184,128]{3,2,1,0:T(8,128)(2,1)S(1)}, bf16[2,2,184,128]{3,2,1,0:T(8,128)(2,1)S(1)}, u32[]{:S(2)}, u32[]{:S(2)}) collective-permute-start(bf16[2,2,184,128]{3,2,1,0:T(8,128)(2,1)S(1)} %get-tuple-element.38), channel_id=1, source_target_pairs={{0,64},{64,0},{1,65},{65,1},{2,66},{66,2},{3,67},{67,3},{4,68},{68... | collective-permute-start | bytes 565256 | tf_op jit(solution)/shard_map/ppermute | solution.py:462
  72.1 10.8 %collective-permute-start.3 = (bf16[2,2,184,128]{3,2,1,0:T(8,128)(2,1)S(1)}, bf16[2,2,184,128]{3,2,1,0:T(8,128)(2,1)S(1)}, u32[]{:S(2)}, u32[]{:S(2)}) collective-permute-start(bf16[2,2,184,128]{3,2,1,0:T(8,128)(2,1)S(1)} %waves.5), channel_id=1, source_target_pairs={{0,64},{64,0},{1,65},{65,1},{2,66},{66,2},{3,67},{67,3},{4,68},{68... | collective-permute-start | bytes 565256 | tf_op jit(solution)/shard_map/ppermute | solution.py:462
  75.1 6.5 %collective-permute-start.6 = (bf16[1,2,184,128]{3,2,1,0:T(8,128)(2,1)S(1)}, bf16[1,2,184,128]{3,2,1,0:T(8,128)(2,1)S(1)}, u32[]{:S(2)}, u32[]{:S(2)}) collective-permute-start(bf16[1,2,184,128]{3,2,1,0:T(8,128)(2,1)S(1)} %get-tuple-element.37), channel_id=1, source_target_pairs={{0,64},{64,0},{1,65},{65,1},{2,66},{66,2},{3,67},{67,3},{4,68},{68... | collective-permute-start | bytes 282632 | tf_op jit(solution)/shard_map/ppermute | solution.py:462
  76.0 4.8 %collective-permute-start.1 = (f32[8,128]{1,0:T(8,128)S(1)}, f32[8,128]{1,0:T(8,128)S(1)}, u32[]{:S(2)}, u32[]{:S(2)}) collective-permute-start(f32[8,128]{1,0:T(8,128)S(1)} %get-tuple-element.28._.refs_2_), channel_id=1, source_target_pairs={{0,192},{64,128},{128,64},{192,0},{1,193},{65,129},{129,65},{193,1... | collective-permute-start | bytes 12296 | tf_op jit(solution)/shard_map/ppermute | solution.py:500

commit v5 on v0

--- a/solution.py
+++ b/solution.py
@@ -43,11 +43,51 @@
     return pltpu.CompilerParams(vmem_limit_bytes=mib * MIB)
 
 
+def main_lanes(lon):
+    return lon // 128 * 128
+
+
+def packed_shape(cols, lon):
+    main = main_lanes(lon)
+    return cols + cols // (main // (lon - main)), main
+
+
+def fold_tails(tail_ref, lon):
+    main = main_lanes(lon)
+    width = lon - main
+    parts = main // width
+    rows = tail_ref.shape[0] // parts
+    low = lax.broadcasted_iota(jnp.int32, (rows, 128), 1) < width
+    total = None
+    for j in range(parts):
+        piece = jnp.where(low, tail_ref[j * rows : (j + 1) * rows, :], 0.0)
+        wide = jnp.concatenate([piece, jnp.zeros((rows, main - 128), F32)], axis=1)
+        wide = pltpu.roll(wide, j * width, 1) if j else wide
+        total = wide if total is None else total + wide
+    return total
+
+
+def unfold_tails(folded, tail_ref, lon):
+    main = main_lanes(lon)
+    width = lon - main
+    rows = folded.shape[0]
+    for j in range(main // width):
+        wide = pltpu.roll(folded, main - j * width, 1) if j else folded
+        tail_ref[j * rows : (j + 1) * rows, :] = wide[:, :128]
+
+
+def put_packed(box, field, at, tail_ref, lon):
+    main = main_lanes(lon)
+    size = field.shape[0]
+    box[at : at + size, :] = field[:, :main]
+    tail_ref[at : at + size, 0 : lon - main] = field[:, main:].astype(F32)
+
+
 def keep_of(mask):
     return mask.astype(F32).astype(BF16)
 
 
-def first_kernel(half_ref, u_ref, v_ref, t_ref, m_ref, o_ref, sums_ref, us, vs, ts, masks, sems):
+def first_kernel(half_ref, u_ref, v_ref, t_ref, m_ref, o_ref, sums_ref, us, vs, ts, masks, tails, sems):
     rows, samples, levels, lon = vs.shape
     part = samples // 2
     size = part * levels
@@ -75,15 +115,14 @@
         keep = keep_of(masks[j])
         v = (vs[j] * keep[None]).reshape(samples * levels, lon)
         sums_ref[j : j + 1, :] = lax.dot_general(ones, v, CONTRACT, preferred_element_type=F32)[0:1]
-        full = jnp.broadcast_to(keep[None], (samples, levels, lon)).reshape(samples * levels, lon)
-        sums_ref[rows + j : rows + j + 1, :] = lax.dot_general(
-            ones, full, CONTRACT, preferred_element_type=F32
-        )[0:1]
+        kept = lax.dot_general(ones, keep, CONTRACT, preferred_element_type=F32)[0:1]
+        sums_ref[rows + j : rows + j + 1, :] = jnp.concatenate([kept] * samples, axis=1)
     for c in extra:
         c.wait()
     keep = keep_of(masks[0])[None]
     for f, field in enumerate((ts[...], us[...], vs[0, at])):
-        o_ref[0, f * size : (f + 1) * size, :] = (field * keep).reshape(size, lon)
+        put_packed(o_ref.at[0], (field * keep).reshape(size, lon), f * size, tails, lon)
+    o_ref[0, 3 * size :, :] = fold_tails(tails, lon).astype(BF16)
 
 
 def first_part(half, u, v, t, mask):
@@ -92,7 +131,7 @@
     return pl.pallas_call(
         first_kernel,
         out_shape=(
-            jax.ShapeDtypeStruct((1, 3 * part * levels, lon), BF16),
+            jax.ShapeDtypeStruct((1, *packed_shape(3 * part * levels, lon)), BF16),
             jax.ShapeDtypeStruct((2 * rows, samples * levels), F32),
         ),
         in_specs=[SMEM, HBM, HBM, HBM, HBM],
@@ -102,6 +141,7 @@
             pltpu.VMEM((rows, samples, levels, lon), BF16),
             pltpu.VMEM((part, levels, lon), BF16),
             pltpu.VMEM((rows, levels, lon), jnp.int32),
+            pltpu.VMEM((3 * part * levels, 128), F32),
             pltpu.SemaphoreType.DMA((rows, 4)),
         ],
         compiler_params=params(60),
@@ -112,7 +152,7 @@
 def send_kernel(groups, half_ref, u_ref, v_ref, t_ref, m_ref, _, *rest):
     n = len(groups)
     far_refs, near_refs = rest[: n - 1], rest[n - 1 : 2 * n - 1]
-    us, vs, ts, masks, fars, nears, sems, out_sems = rest[2 * n - 1 :]
+    us, vs, ts, masks, fars, nears, tails, sems, out_sems = rest[2 * n - 1 :]
     rows, samples, levels, lon = vs.shape
     part = samples // 2
     size = part * levels
@@ -140,8 +180,13 @@
                     continue
                 ref = far_refs[g - 1] if k == 0 else near_refs[g]
                 for f, field in enumerate((ts, us, vs)):
-                    mine = field[j, pl.ds(where * part, part)] * keep[None]
-                    box[j, f * size : (f + 1) * size, :] = mine.reshape(size, lon)
+                    mine = (field[j, pl.ds(where * part, part)] * keep[None]).reshape(size, lon)
+                    if k:
+                        box[j, f * size : (f + 1) * size, :] = mine
+                    else:
+                        put_packed(box.at[j], mine, f * size, tails.at[j], lon)
+                if not k:
+                    box[j, 3 * size :, :] = fold_tails(tails.at[j], lon).astype(BF16)
                 c = pltpu.make_async_copy(box.at[j], ref.at[i], out_sems.at[j, k])
                 c.start()
                 done.append(c)
@@ -154,11 +199,13 @@
     part = samples // 2
     unit = 3 * part * levels
     n = len(groups)
+    wire = packed_shape(unit, lon)
     packed = [jax.ShapeDtypeStruct((len(g), unit, lon), BF16) for g in groups]
+    sent = [jax.ShapeDtypeStruct((len(g), *wire), BF16) for g in groups[1:]]
     return pl.pallas_call(
         lambda *refs: send_kernel(groups, *refs),
         out_shape=(
-            *packed[1:],
+            *sent,
             *packed,
         ),
         in_specs=[SMEM, HBM, HBM, HBM, HBM, ANY],
@@ -168,8 +215,9 @@
             pltpu.VMEM((rows, samples, levels, lon), BF16),
             pltpu.VMEM((rows, samples, levels, lon), BF16),
             pltpu.VMEM((rows, levels, lon), jnp.int32),
+            pltpu.VMEM((rows, *wire), BF16),
             pltpu.VMEM((rows, unit, lon), BF16),
-            pltpu.VMEM((rows, unit, lon), BF16),
+            pltpu.VMEM((rows, unit, 128), F32),
             pltpu.SemaphoreType.DMA((rows, 4)),
             pltpu.SemaphoreType.DMA((rows, 2)),
         ],
@@ -178,13 +226,22 @@
     )(half, u, v, t, mask, after)
 
 
-def wave_kernel(half_ref, table_ref, own_ref, got_ref, _, *o_refs, flips):
+def wave_kernel(half_ref, table_ref, own_ref, got_ref, _, *refs, flips):
+    o_refs, (mix, tails) = refs[:-2], refs[-2:]
     n = table_ref.shape[2] // 2
+    cols, lon = own_ref.shape[1:]
+    main = main_lanes(lon)
     scale = 2.0 / (MERIDIANS * MERIDIANS)
     for i in range(got_ref.shape[0]):
-        own, got = own_ref[i].astype(F32), got_ref[i].astype(F32)
-        for p, mixed in enumerate(((own - got).astype(BF16), (own + got).astype(BF16))):
-            x = jnp.concatenate([mixed, mixed[2 * mixed.shape[0] // 3 :]])
+        unfold_tails(got_ref[i, cols:].astype(F32), tails.at[i], lon)
+        for at, end in ((0, main), (main, lon)):
+            own = own_ref[i, :, at:end].astype(F32)
+            got = tails[i, :, 0 : lon - main] if at else got_ref[i, 0:cols].astype(F32)
+            for p, mixed in enumerate(((own - got).astype(BF16), (own + got).astype(BF16))):
+                mix[i, p, 0:cols, at:end] = mixed
+                mix[i, p, cols:, at:end] = mixed[2 * cols // 3 :]
+        for p in range(2):
+            x = mix[i, p]
             w = x.shape[0] // 2
             for flip, o_ref in zip(flips, o_refs):
                 table = table_ref[1 - half_ref[0] if flip else half_ref[0], p]
@@ -194,13 +251,17 @@
 
 
 def waves(half, table, own, got, after, *flips):
-    rows, cols, _ = got.shape
+    rows, cols, lon = own.shape
     shape = (rows, 2, PADDED, 2 * cols // 3)
     return pl.pallas_call(
         functools.partial(wave_kernel, flips=flips),
         out_shape=tuple(jax.ShapeDtypeStruct(shape, BF16 if f else F32) for f in flips),
         in_specs=[SMEM, VMEM, VMEM, VMEM, ANY],
         out_specs=(VMEM,) * len(flips),
+        scratch_shapes=[
+            pltpu.VMEM((rows, 2, 4 * cols // 3, lon), BF16),
+            pltpu.VMEM((rows, cols, 128), F32),
+        ],
         compiler_params=params(16),
         name="waves",
     )(half, table, own, got, after)

time: 85.7 us -> 84 us (0.980)
  waiting for transfers between devices: 33.3 us -> 31.3 us
    ppermute x7, waiting for transfers between devices: 30.4 us -> 28.4 us  [swap(): return lax.ppermute(x, 'lon', across)]
where the time goes in v5:
time: 84 us; the launch traced here: 83.7 us
  waiting for transfers between devices  31.3 us (37%)
  blocking collectives  26.2 us (31%)
  Pallas kernels  15.9 us (19%)
  starting transfers between devices  8.38 us (10%)
  local copies, waits for them, and re-layouts  1.1 us (1%)
    ppermute x7, waiting for transfers between devices, swap(): return lax.ppermute(x, 'lon', across)  28.4 us
    all_to_all x2, blocking collectives, all_of(): return lax.all_to_all(x, axes, split_axis=0, concat_axis=0, tiled=True)  26.2 us
    ppermute x7, starting transfers between devices, swap(): return lax.ppermute(x, 'lon', across)  7.26 us
    pallas_call x4, Pallas kernels, waves(): pl.pallas_call(functools.partial(wave_kernel, flips=flips), out_shape=tup...  5.79 us
    pallas_call x1, Pallas kernels, send(): pl.pallas_call(lambda *refs: send_kernel(groups, *refs), out_shape=(*sent...  3.37 us
    pallas_call x1, Pallas kernels, first_part(): pl.pallas_call(first_kernel, out_shape=(jax.ShapeDtypeStruct((1, *packed_...  3.14 us
    ppermute x1, waiting for transfers between devices, per_device(): lax.ppermute(near_half, ('lat', 'lon'), [(i, 3 - i) for i in range(4)])  2.89 us
    pallas_call x2, Pallas kernels, join(): pl.pallas_call(lambda *refs: join_kernel(rows[0], parts, *refs), out_shap...  2.21 us
  transfers between devices with their start and end apart: 8, of which 2 were waited for; matrix products, arithmetic and copies ran while one was open for 0% of the time, Pallas kernels for 10%

profile of v5, /device:TPU:6, one launch (start us, length us, event | category | flops | bytes accessed | tf_op | source)
XLA Modules:
  0.0 83.7 jit_solution(687342037125924008)
XLA Ops:
  0.6 3.1 %sums.1 = (bf16[1,216,640]{2,1,0:T(8,128)(2,1)}, f32[10,128]{1,0:T(8,128)}) custom-call(s32[1]{0:T(128)} %bitcast.1.half_ref.refs_0_, bf16[5,4,32,720]{3,2,1,0:T(8,128)(2,1)} %refs_1_.1, bf16[5,4,32,720]{3,2,1,0:T(8,128)(2,1)} %refs_2_.1, bf16[5,4,32,720]{3,2,1,0:T(8,128)(2,1)} %refs_3_.1, s32[5,32,720]{2,1,0:T(8,128)} %refs_4_.3), custom_call_target="tpu_custom_call" | custom-call | tf_op jit(solution)/shard_map/sums/pallas_call | solution.py:131
  3.8 3.4 %send.1 = (bf16[2,216,640]{2,1,0:T(8,128)(2,1)}, bf16[2,216,640]{2,1,0:T(8,128)(2,1)}, bf16[1,192,720]{2,1,0:T(8,128)(2,1)}, bf16[2,192,720]{2,1,0:T(8,128)(2,1)}, bf16[2,192,720]{2,1,0:T(8,128)(2,1)}) custom-call(s32[1]{0:T(128)} %bitcast.1.half_ref.refs_0_, bf16[5,4,32,720]{3,2,1,0:T(8,128)(2,1)} %refs_1_.1, bf16[5,4,32,720]{3,2,1,0:T(8,128)(2,1)} %refs_2_.1, ...), custom_call_target="tpu_custom_call" | custom-call | tf_op jit(solution)/shard_map/send/pallas_call | solution.py:205
  7.2 0.9 %collective-permute-start.5 = (bf16[2,216,640]{2,1,0:T(8,128)(2,1)}, bf16[2,216,640]{2,1,0:T(8,128)(2,1)}, u32[]{:S(2)}, u32[]{:S(2)}) collective-permute-start(bf16[2,216,640]{2,1,0:T(8,128)(2,1)} %get-tuple-element.37), channel_id=1, source_target_pairs={{0,64},{64,0},{1,65},{65,1},{2,66},{66,2},{3,67},{67,3},{4,68},{68... | collective-permute-start | bytes 1658888 | tf_op jit(solution)/shard_map/ppermute | solution.py:479
  8.1 1.2 %collective-permute-start.2 = (bf16[2,216,640]{2,1,0:T(8,128)(2,1)}, bf16[2,216,640]{2,1,0:T(8,128)(2,1)S(1)}, u32[]{:S(2)}, u32[]{:S(2)}) collective-permute-start(bf16[2,216,640]{2,1,0:T(8,128)(2,1)} %get-tuple-element.31), channel_id=1, source_target_pairs={{0,64},{64,0},{1,65},{65,1},{2,66},{66,2},{3,67},{67,3},{4,68},{68... | collective-permute-start | bytes 1658888 | tf_op jit(solution)/shard_map/ppermute | solution.py:479
  9.3 0.8 collective-permute-start.4
  10.2 1.2 %collective-permute-start = (f32[10,128]{1,0:T(8,128)S(1)}, f32[10,128]{1,0:T(8,128)S(1)}, u32[]{:S(2)}, u32[]{:S(2)}) collective-permute-start(f32[10,128]{1,0:T(8,128)S(1)} %copy-done.4), channel_id=1, source_target_pairs={{0,64},{64,0},{1,65},{65,1},{2,66},{66,2},{3,67},{67,3},{4,68},{68... | collective-permute-start | bytes 15368 | tf_op jit(solution)/shard_map/ppermute | solution.py:479
  11.4 28.4 %collective-permute-done.refs_2_ = f32[10,128]{1,0:T(8,128)S(1)} collective-permute-done((f32[10,128]{1,0:T(8,128)S(1)}, f32[10,128]{1,0:T(8,128)S(1)}, u32[]{:S(2)}, u32[]{:S(2)}) %collective-permute-start) | collective-permute-done | bytes 5152 | tf_op jit(solution)/shard_map/ppermute | solution.py:479
  39.8 0.1 shard_map.102._
  39.9 9.9 %all_to_all.10.refs_1_ = f32[8,16,128]{2,1,0:T(8,128)S(1)} all-to-all(f32[8,16,128]{2,1,0:T(8,128)S(1)} %shard_map.102._), channel_id=1, replica_groups=mesh['lat'=2,'lon'=2,'lev_0'=8,'lev_1'=4,'lev_2'=2] {'lev_1','lev_2'}, dimensions={0} | all-to-all | bytes 131072 | tf_op jit(solution)/shard_map/all_to_all | solution.py:462
  49.8 0.5 shard_map.103
  50.3 16.3 %all_to_all.11.refs_2_ = f32[8,8,128]{2,1,0:T(8,128)S(1)} all-to-all(f32[8,8,128]{2,1,0:T(8,128)S(1)} %get-tuple-element.27._), channel_id=1, replica_groups=mesh['lat'=2,'lon'=2,'lev_0'=8,'lev_1'=4,'lev_2'=2] {'lev_0'}, dimensions={0} | all-to-all | bytes 65536 | tf_op jit(solution)/shard_map/all_to_all | solution.py:462
  66.6 1.1 %copy-done.2 = bf16[2,192,720]{2,1,0:T(8,128)(2,1)S(1)} copy-done((bf16[2,192,720]{2,1,0:T(8,128)(2,1)S(1)}, bf16[2,192,720]{2,1,0:T(8,128)(2,1)}, u32[]{:S(2)}) %copy-start.2) | copy-done | bytes 552984
  67.7 2.4 %waves.7 = (bf16[2,2,184,128]{3,2,1,0:T(8,128)(2,1)S(1)}, f32[2,2,184,128]{3,2,1,0:T(8,128)S(1)}) custom-call(s32[1]{0:T(128)} %bitcast.1.half_ref.refs_0_, bf16[2,2,368,720]{3,2,1,0:T(8,128)(2,1)S(1)} %copy-done, bf16[2,192,720]{2,1,0:T(8,128)(2,1)S(1)} %copy-done.2, bf16[2,216,640]{2,1,0:T(8,128)(2,1)} %collective-permute-done.5.got_ref, ...), custom_call_target="tpu_custom_call" | custom-call | tf_op jit(solution)/shard_map/waves/pallas_call | solution.py:256
  70.1 0.9 %collective-permute-start.7 = (bf16[2,2,184,128]{3,2,1,0:T(8,128)(2,1)S(1)}, bf16[2,2,184,128]{3,2,1,0:T(8,128)(2,1)S(1)}, u32[]{:S(2)}, u32[]{:S(2)}) collective-permute-start(bf16[2,2,184,128]{3,2,1,0:T(8,128)(2,1)S(1)} %get-tuple-element.40), channel_id=1, source_target_pairs={{0,64},{64,0},{1,65},{65,1},{2,66},{66,2},{3,67},{67,3},{4,68},{68... | collective-permute-start | bytes 565256 | tf_op jit(solution)/shard_map/ppermute | solution.py:479
  71.1 0.8 waves.5
  71.9 1.3 %collective-permute-start.3 = (bf16[2,2,184,128]{3,2,1,0:T(8,128)(2,1)S(1)}, bf16[2,2,184,128]{3,2,1,0:T(8,128)(2,1)S(1)}, u32[]{:S(2)}, u32[]{:S(2)}) collective-permute-start(bf16[2,2,184,128]{3,2,1,0:T(8,128)(2,1)S(1)} %waves.5), channel_id=1, source_target_pairs={{0,64},{64,0},{1,65},{65,1},{2,66},{66,2},{3,67},{67,3},{4,68},{68... | collective-permute-start | bytes 565256 | tf_op jit(solution)/shard_map/ppermute | solution.py:479
  73.2 1.8 %waves.6 = (bf16[1,2,184,128]{3,2,1,0:T(8,128)(2,1)S(1)}, f32[1,2,184,128]{3,2,1,0:T(8,128)S(1)}) custom-call(s32[1]{0:T(128)} %bitcast.1.half_ref.refs_0_, bf16[2,2,368,720]{3,2,1,0:T(8,128)(2,1)S(1)} %copy-done, bf16[1,192,720]{2,1,0:T(8,128)(2,1)S(1)} %copy-done.3, bf16[1,216,640]{2,1,0:T(8,128)(2,1)} %collective-permute-done.4.got_ref, ...), custom_call_target="tpu_custom_call" | custom-call | tf_op jit(solution)/shard_map/waves/pallas_call | solution.py:256
  74.9 0.9 %collective-permute-start.6 = (bf16[1,2,184,128]{3,2,1,0:T(8,128)(2,1)S(1)}, bf16[1,2,184,128]{3,2,1,0:T(8,128)(2,1)S(1)}, u32[]{:S(2)}, u32[]{:S(2)}) collective-permute-start(bf16[1,2,184,128]{3,2,1,0:T(8,128)(2,1)S(1)} %get-tuple-element.39), channel_id=1, source_target_pairs={{0,64},{64,0},{1,65},{65,1},{2,66},{66,2},{3,67},{67,3},{4,68},{68... | collective-permute-start | bytes 282632 | tf_op jit(solution)/shard_map/ppermute | solution.py:479
  75.8 1.1 %collective-permute-start.1 = (f32[8,128]{1,0:T(8,128)S(1)}, f32[8,128]{1,0:T(8,128)S(1)}, u32[]{:S(2)}, u32[]{:S(2)}) collective-permute-start(f32[8,128]{1,0:T(8,128)S(1)} %get-tuple-element.29._.refs_2_), channel_id=1, source_target_pairs={{0,192},{64,128},{128,64},{192,0},{1,193},{65,129},{129,65},{193,1... | collective-permute-start | bytes 12296 | tf_op jit(solution)/shard_map/ppermute | solution.py:517
  77.0 0.8 waves.4.refs_4_.refs_1_
  77.8 2.9 %collective-permute-done.1.refs_3_ = f32[8,128]{1,0:T(8,128)S(1)} collective-permute-done((f32[8,128]{1,0:T(8,128)S(1)}, f32[8,128]{1,0:T(8,128)S(1)}, u32[]{:S(2)}, u32[]{:S(2)}) %collective-permute-start.1) | collective-permute-done | bytes 4128 | tf_op jit(solution)/shard_map/ppermute | solution.py:517
  80.7 0.8 shard_map.105
  81.5 1.2 %join.2 = (f32[5,360,128]{2,1,0:T(8,128)}, f32[5,360,128]{2,1,0:T(8,128)}) custom-call(s32[1]{0:T(128)} %bitcast.1.half_ref.refs_0_, f32[1,2,184,128]{3,2,1,0:T(8,128)S(1)} %get-tuple-element.35.refs_1_, f32[2,2,184,128]{3,2,1,0:T(8,128)S(1)} %get-tuple-element.38.refs_2_, bf16[1,2,184,128]{3,2,1,0:T(8,128)(2,1)S(1)} %collective-permute-done.6.refs_3_, ...), custom_call_target="tpu_custom_call" | custom-call | tf_op jit(solution)/shard_map/join/pallas_call | solution.py:309
  82.6 1.0 %join.3 = (f32[5,360,128]{2,1,0:T(8,128)}, f32[5,360,128]{2,1,0:T(8,128)}) custom-call(s32[1]{0:T(128)} %bitcast.1.half_ref.refs_0_, f32[2,2,184,128]{3,2,1,0:T(8,128)S(1)} %waves.4.refs_4_.refs_1_, bf16[2,2,184,128]{3,2,1,0:T(8,128)(2,1)S(1)} %collective-permute-done.3.refs_2_, ...), custom_call_target="tpu_custom_call", output_to_operand_aliasing={{0}: (3, {}), {1}: (4, {})} | custom-call | tf_op jit(solution)/shard_map/join/pallas_call | solution.py:309
  (20 shorter events, 0.1 us)
Async XLA Ops:
  3.8 6.4 %copy-start.4 = (f32[10,128]{1,0:T(8,128)S(1)}, f32[10,128]{1,0:T(8,128)}, u32[]{:S(2)}) copy-start(f32[10,128]{1,0:T(8,128)} %get-tuple-element.25.refs_1_.refs_5_) | copy-start | bytes 15364
  3.8 36.0 %copy-start.5 = (f32[5,4,32]{2,1,0:T(4,128)S(1)}, f32[5,4,32]{2,1,0:T(4,128)}, u32[]{:S(2)}) copy-start(f32[5,4,32]{2,1,0:T(4,128)} %refs_4_.2) | copy-start | bytes 7684
  3.8 36.0 %copy-start.6 = (f32[32]{0:T(128)S(1)}, f32[32]{0:T(128)}, u32[]{:S(2)}) copy-start(f32[32]{0:T(128)} %param.11) | copy-start | bytes 388
  3.8 62.8 %copy-start = (bf16[2,2,368,720]{3,2,1,0:T(8,128)(2,1)S(1)}, bf16[2,2,368,720]{3,2,1,0:T(8,128)(2,1)}, u32[]{:S(2)}) copy-start(bf16[2,2,368,720]{3,2,1,0:T(8,128)(2,1)} %constant.29.clone.table_ref) | copy-start | bytes 6359044
  7.2 63.8 %copy-start.1 = (bf16[2,192,720]{2,1,0:T(8,128)(2,1)S(1)}, bf16[2,192,720]{2,1,0:T(8,128)(2,1)}, u32[]{:S(2)}) copy-start(bf16[2,192,720]{2,1,0:T(8,128)(2,1)} %get-tuple-element.30.own_ref) | copy-start | bytes 1658884
  7.2 59.4 %collective-permute-start.5 = (bf16[2,216,640]{2,1,0:T(8,128)(2,1)}, bf16[2,216,640]{2,1,0:T(8,128)(2,1)}, u32[]{:S(2)}, u32[]{:S(2)}) collective-permute-start(bf16[2,216,640]{2,1,0:T(8,128)(2,1)} %get-tuple-element.37), channel_id=1, source_target_pairs={{0,64},{64,0},{1,65},{65,1},{2,66},{66,2},{3,67},{67,3},{4,68},{68... | collective-permute-start | bytes 1658888 | tf_op jit(solution)/shard_map/ppermute | solution.py:479
  8.1 62.9 %collective-permute-start.2 = (bf16[2,216,640]{2,1,0:T(8,128)(2,1)}, bf16[2,216,640]{2,1,0:T(8,128)(2,1)S(1)}, u32[]{:S(2)}, u32[]{:S(2)}) collective-permute-start(bf16[2,216,640]{2,1,0:T(8,128)(2,1)} %get-tuple-element.31), channel_id=1, source_target_pairs={{0,64},{64,0},{1,65},{65,1},{2,66},{66,2},{3,67},{67,3},{4,68},{68... | collective-permute-start | bytes 1658888 | tf_op jit(solution)/shard_map/ppermute | solution.py:479
  9.3 63.8 %collective-permute-start.4 = (bf16[1,216,640]{2,1,0:T(8,128)(2,1)}, bf16[1,216,640]{2,1,0:T(8,128)(2,1)}, u32[]{:S(2)}, u32[]{:S(2)}) collective-permute-start(bf16[1,216,640]{2,1,0:T(8,128)(2,1)} %get-tuple-element.34), channel_id=1, source_target_pairs={{0,64},{64,0},{1,65},{65,1},{2,66},{66,2},{3,67},{67,3},{4,68},{68... | collective-permute-start | bytes 829448 | tf_op jit(solution)/shard_map/ppermute | solution.py:479
  10.2 29.6 %collective-permute-start = (f32[10,128]{1,0:T(8,128)S(1)}, f32[10,128]{1,0:T(8,128)S(1)}, u32[]{:S(2)}, u32[]{:S(2)}) collective-permute-start(f32[10,128]{1,0:T(8,128)S(1)} %copy-done.4), channel_id=1, source_target_pairs={{0,64},{64,0},{1,65},{65,1},{2,66},{66,2},{3,67},{67,3},{4,68},{68... | collective-permute-start | bytes 15368 | tf_op jit(solution)/shard_map/ppermute | solution.py:479
  66.6 1.1 %copy-start.2 = (bf16[2,192,720]{2,1,0:T(8,128)(2,1)S(1)}, bf16[2,192,720]{2,1,0:T(8,128)(2,1)}, u32[]{:S(2)}) copy-start(bf16[2,192,720]{2,1,0:T(8,128)(2,1)} %get-tuple-element.36.own_ref) | copy-start | bytes 1658884
  70.1 3.0 %copy-start.3 = (bf16[1,192,720]{2,1,0:T(8,128)(2,1)S(1)}, bf16[1,192,720]{2,1,0:T(8,128)(2,1)}, u32[]{:S(2)}) copy-start(bf16[1,192,720]{2,1,0:T(8,128)(2,1)} %get-tuple-element.33.own_ref) | copy-start | bytes 829444
  70.1 11.3 %collective-permute-start.7 = (bf16[2,2,184,128]{3,2,1,0:T(8,128)(2,1)S(1)}, bf16[2,2,184,128]{3,2,1,0:T(8,128)(2,1)S(1)}, u32[]{:S(2)}, u32[]{:S(2)}) collective-permute-start(bf16[2,2,184,128]{3,2,1,0:T(8,128)(2,1)S(1)} %get-tuple-element.40), channel_id=1, source_target_pairs={{0,64},{64,0},{1,65},{65,1},{2,66},{66,2},{3,67},{67,3},{4,68},{68... | collective-permute-start | bytes 565256 | tf_op jit(solution)/shard_map/ppermute | solution.py:479
  71.9 10.8 %collective-permute-start.3 = (bf16[2,2,184,128]{3,2,1,0:T(8,128)(2,1)S(1)}, bf16[2,2,184,128]{3,2,1,0:T(8,128)(2,1)S(1)}, u32[]{:S(2)}, u32[]{:S(2)}) collective-permute-start(bf16[2,2,184,128]{3,2,1,0:T(8,128)(2,1)S(1)} %waves.5), channel_id=1, source_target_pairs={{0,64},{64,0},{1,65},{65,1},{2,66},{66,2},{3,67},{67,3},{4,68},{68... | collective-permute-start | bytes 565256 | tf_op jit(solution)/shard_map/ppermute | solution.py:479
  74.9 6.5 %collective-permute-start.6 = (bf16[1,2,184,128]{3,2,1,0:T(8,128)(2,1)S(1)}, bf16[1,2,184,128]{3,2,1,0:T(8,128)(2,1)S(1)}, u32[]{:S(2)}, u32[]{:S(2)}) collective-permute-start(bf16[1,2,184,128]{3,2,1,0:T(8,128)(2,1)S(1)} %get-tuple-element.39), channel_id=1, source_target_pairs={{0,64},{64,0},{1,65},{65,1},{2,66},{66,2},{3,67},{67,3},{4,68},{68... | collective-permute-start | bytes 282632 | tf_op jit(solution)/shard_map/ppermute | solution.py:479
  75.8 4.8 %collective-permute-start.1 = (f32[8,128]{1,0:T(8,128)S(1)}, f32[8,128]{1,0:T(8,128)S(1)}, u32[]{:S(2)}, u32[]{:S(2)}) collective-permute-start(f32[8,128]{1,0:T(8,128)S(1)} %get-tuple-element.29._.refs_2_), channel_id=1, source_target_pairs={{0,192},{64,128},{128,64},{192,0},{1,193},{65,129},{129,65},{193,1... | collective-permute-start | bytes 12296 | tf_op jit(solution)/shard_map/ppermute | solution.py:517

commit v6 on v5

--- a/solution.py
+++ b/solution.py
@@ -87,7 +87,7 @@
     return mask.astype(F32).astype(BF16)
 
 
-def first_kernel(half_ref, u_ref, v_ref, t_ref, m_ref, o_ref, sums_ref, us, vs, ts, masks, tails, sems):
+def first_kernel(half_ref, u_ref, v_ref, t_ref, m_ref, o_ref, sums_ref, us, vs, ts, masks, tails, box, sems, out_sem):
     rows, samples, levels, lon = vs.shape
     part = samples // 2
     size = part * levels
@@ -108,21 +108,25 @@
     for group in (copies[0], extra, *copies[1:]):
         for c in group:
             c.start()
+    for c in (*copies[0], *extra):
+        c.wait()
+    keep = keep_of(masks[0])[None]
+    for f, field in enumerate((ts[...], us[...], vs[0, at])):
+        put_packed(box, (field * keep).reshape(size, lon), f * size, tails, lon)
+    box[3 * size :, :] = fold_tails(tails, lon).astype(BF16)
+    out = pltpu.make_async_copy(box, o_ref.at[0], out_sem)
+    out.start()
     ones = jnp.ones((8, lon), BF16)
     for j in range(rows):
-        for c in copies[j]:
-            c.wait()
+        if j:
+            for c in copies[j]:
+                c.wait()
         keep = keep_of(masks[j])
         v = (vs[j] * keep[None]).reshape(samples * levels, lon)
         sums_ref[j : j + 1, :] = lax.dot_general(ones, v, CONTRACT, preferred_element_type=F32)[0:1]
         kept = lax.dot_general(ones, keep, CONTRACT, preferred_element_type=F32)[0:1]
         sums_ref[rows + j : rows + j + 1, :] = jnp.concatenate([kept] * samples, axis=1)
-    for c in extra:
-        c.wait()
-    keep = keep_of(masks[0])[None]
-    for f, field in enumerate((ts[...], us[...], vs[0, at])):
-        put_packed(o_ref.at[0], (field * keep).reshape(size, lon), f * size, tails, lon)
-    o_ref[0, 3 * size :, :] = fold_tails(tails, lon).astype(BF16)
+    out.wait()
 
 
 def first_part(half, u, v, t, mask):
@@ -135,14 +139,16 @@
             jax.ShapeDtypeStruct((2 * rows, samples * levels), F32),
         ),
         in_specs=[SMEM, HBM, HBM, HBM, HBM],
-        out_specs=(VMEM, VMEM),
+        out_specs=(HBM, VMEM),
         scratch_shapes=[
             pltpu.VMEM((part, levels, lon), BF16),
             pltpu.VMEM((rows, samples, levels, lon), BF16),
             pltpu.VMEM((part, levels, lon), BF16),
             pltpu.VMEM((rows, levels, lon), jnp.int32),
             pltpu.VMEM((3 * part * levels, 128), F32),
+            pltpu.VMEM(packed_shape(3 * part * levels, lon), BF16),
             pltpu.SemaphoreType.DMA((rows, 4)),
+            pltpu.SemaphoreType.DMA,
         ],
         compiler_params=params(60),
         name="sums",

time: 84 us -> 83.9 us (level)
  no operation moved by 1% of the time
where the time goes in v6:
time: 83.9 us; the launch traced here: 83.6 us
  waiting for transfers between devices  31.3 us (37%)
  blocking collectives  26.2 us (31%)
  Pallas kernels  15.8 us (19%)
  starting transfers between devices  8.39 us (10%)
  local copies, waits for them, and re-layouts  1.1 us (1%)
    ppermute x7, waiting for transfers between devices, swap(): return lax.ppermute(x, 'lon', across)  28.4 us
    all_to_all x2, blocking collectives, all_of(): return lax.all_to_all(x, axes, split_axis=0, concat_axis=0, tiled=True)  26.2 us
    ppermute x7, starting transfers between devices, swap(): return lax.ppermute(x, 'lon', across)  7.26 us
    pallas_call x4, Pallas kernels, waves(): pl.pallas_call(functools.partial(wave_kernel, flips=flips), out_shape=tup...  5.78 us
    pallas_call x1, Pallas kernels, send(): pl.pallas_call(lambda *refs: send_kernel(groups, *refs), out_shape=(*sent...  3.37 us
    pallas_call x1, Pallas kernels, first_part(): pl.pallas_call(first_kernel, out_shape=(jax.ShapeDtypeStruct((1, *packed_...  3.02 us
    ppermute x1, waiting for transfers between devices, per_device(): lax.ppermute(near_half, ('lat', 'lon'), [(i, 3 - i) for i in range(4)])  2.88 us
    pallas_call x2, Pallas kernels, join(): pl.pallas_call(lambda *refs: join_kernel(rows[0], parts, *refs), out_shap...  2.21 us
  transfers between devices with their start and end apart: 8, of which 2 were waited for; matrix products, arithmetic and copies ran while one was open for 0% of the time, Pallas kernels for 10%

profile of v6, /device:TPU:6, one launch (start us, length us, event | category | flops | bytes accessed | tf_op | source)
XLA Modules:
  0.0 83.6 jit_solution(10538778577190751825)
XLA Ops:
  0.6 3.0 %sums.1 = (bf16[1,216,640]{2,1,0:T(8,128)(2,1)}, f32[10,128]{1,0:T(8,128)}) custom-call(s32[1]{0:T(128)} %bitcast.1.half_ref.refs_0_, bf16[5,4,32,720]{3,2,1,0:T(8,128)(2,1)} %refs_1_.1, bf16[5,4,32,720]{3,2,1,0:T(8,128)(2,1)} %refs_2_.1, bf16[5,4,32,720]{3,2,1,0:T(8,128)(2,1)} %refs_3_.1, s32[5,32,720]{2,1,0:T(8,128)} %refs_4_.3), custom_call_target="tpu_custom_call" | custom-call | tf_op jit(solution)/shard_map/sums/pallas_call | solution.py:135
  3.7 3.4 %send.1 = (bf16[2,216,640]{2,1,0:T(8,128)(2,1)}, bf16[2,216,640]{2,1,0:T(8,128)(2,1)}, bf16[1,192,720]{2,1,0:T(8,128)(2,1)}, bf16[2,192,720]{2,1,0:T(8,128)(2,1)}, bf16[2,192,720]{2,1,0:T(8,128)(2,1)}) custom-call(s32[1]{0:T(128)} %bitcast.1.half_ref.refs_0_, bf16[5,4,32,720]{3,2,1,0:T(8,128)(2,1)} %refs_1_.1, bf16[5,4,32,720]{3,2,1,0:T(8,128)(2,1)} %refs_2_.1, ...), custom_call_target="tpu_custom_call" | custom-call | tf_op jit(solution)/shard_map/send/pallas_call | solution.py:211
  7.1 0.9 %collective-permute-start.5 = (bf16[2,216,640]{2,1,0:T(8,128)(2,1)}, bf16[2,216,640]{2,1,0:T(8,128)(2,1)}, u32[]{:S(2)}, u32[]{:S(2)}) collective-permute-start(bf16[2,216,640]{2,1,0:T(8,128)(2,1)} %get-tuple-element.37), channel_id=1, source_target_pairs={{0,64},{64,0},{1,65},{65,1},{2,66},{66,2},{3,67},{67,3},{4,68},{68... | collective-permute-start | bytes 1658888 | tf_op jit(solution)/shard_map/ppermute | solution.py:485
  8.0 1.2 %collective-permute-start.2 = (bf16[2,216,640]{2,1,0:T(8,128)(2,1)}, bf16[2,216,640]{2,1,0:T(8,128)(2,1)S(1)}, u32[]{:S(2)}, u32[]{:S(2)}) collective-permute-start(bf16[2,216,640]{2,1,0:T(8,128)(2,1)} %get-tuple-element.31), channel_id=1, source_target_pairs={{0,64},{64,0},{1,65},{65,1},{2,66},{66,2},{3,67},{67,3},{4,68},{68... | collective-permute-start | bytes 1658888 | tf_op jit(solution)/shard_map/ppermute | solution.py:485
  9.2 0.8 collective-permute-start.4
  10.0 1.2 %collective-permute-start = (f32[10,128]{1,0:T(8,128)S(1)}, f32[10,128]{1,0:T(8,128)S(1)}, u32[]{:S(2)}, u32[]{:S(2)}) collective-permute-start(f32[10,128]{1,0:T(8,128)S(1)} %copy-done.4), channel_id=1, source_target_pairs={{0,64},{64,0},{1,65},{65,1},{2,66},{66,2},{3,67},{67,3},{4,68},{68... | collective-permute-start | bytes 15368 | tf_op jit(solution)/shard_map/ppermute | solution.py:485
  11.2 28.4 %collective-permute-done.refs_2_ = f32[10,128]{1,0:T(8,128)S(1)} collective-permute-done((f32[10,128]{1,0:T(8,128)S(1)}, f32[10,128]{1,0:T(8,128)S(1)}, u32[]{:S(2)}, u32[]{:S(2)}) %collective-permute-start) | collective-permute-done | bytes 5152 | tf_op jit(solution)/shard_map/ppermute | solution.py:485
  39.6 0.1 shard_map.102._
  39.8 9.9 %all_to_all.10.refs_1_ = f32[8,16,128]{2,1,0:T(8,128)S(1)} all-to-all(f32[8,16,128]{2,1,0:T(8,128)S(1)} %shard_map.102._), channel_id=1, replica_groups=mesh['lat'=2,'lon'=2,'lev_0'=8,'lev_1'=4,'lev_2'=2] {'lev_1','lev_2'}, dimensions={0} | all-to-all | bytes 131072 | tf_op jit(solution)/shard_map/all_to_all | solution.py:468
  49.6 0.5 shard_map.103
  50.1 16.3 %all_to_all.11.refs_2_ = f32[8,8,128]{2,1,0:T(8,128)S(1)} all-to-all(f32[8,8,128]{2,1,0:T(8,128)S(1)} %get-tuple-element.27._), channel_id=1, replica_groups=mesh['lat'=2,'lon'=2,'lev_0'=8,'lev_1'=4,'lev_2'=2] {'lev_0'}, dimensions={0} | all-to-all | bytes 65536 | tf_op jit(solution)/shard_map/all_to_all | solution.py:468
  66.5 1.1 %copy-done.2 = bf16[2,192,720]{2,1,0:T(8,128)(2,1)S(1)} copy-done((bf16[2,192,720]{2,1,0:T(8,128)(2,1)S(1)}, bf16[2,192,720]{2,1,0:T(8,128)(2,1)}, u32[]{:S(2)}) %copy-start.2) | copy-done | bytes 552984
  67.6 2.4 %waves.7 = (bf16[2,2,184,128]{3,2,1,0:T(8,128)(2,1)S(1)}, f32[2,2,184,128]{3,2,1,0:T(8,128)S(1)}) custom-call(s32[1]{0:T(128)} %bitcast.1.half_ref.refs_0_, bf16[2,2,368,720]{3,2,1,0:T(8,128)(2,1)S(1)} %copy-done, bf16[2,192,720]{2,1,0:T(8,128)(2,1)S(1)} %copy-done.2, bf16[2,216,640]{2,1,0:T(8,128)(2,1)} %collective-permute-done.5.got_ref, ...), custom_call_target="tpu_custom_call" | custom-call | tf_op jit(solution)/shard_map/waves/pallas_call | solution.py:262
  70.0 0.9 %collective-permute-start.7 = (bf16[2,2,184,128]{3,2,1,0:T(8,128)(2,1)S(1)}, bf16[2,2,184,128]{3,2,1,0:T(8,128)(2,1)S(1)}, u32[]{:S(2)}, u32[]{:S(2)}) collective-permute-start(bf16[2,2,184,128]{3,2,1,0:T(8,128)(2,1)S(1)} %get-tuple-element.40), channel_id=1, source_target_pairs={{0,64},{64,0},{1,65},{65,1},{2,66},{66,2},{3,67},{67,3},{4,68},{68... | collective-permute-start | bytes 565256 | tf_op jit(solution)/shard_map/ppermute | solution.py:485
  70.9 0.8 waves.5
  71.7 1.3 %collective-permute-start.3 = (bf16[2,2,184,128]{3,2,1,0:T(8,128)(2,1)S(1)}, bf16[2,2,184,128]{3,2,1,0:T(8,128)(2,1)S(1)}, u32[]{:S(2)}, u32[]{:S(2)}) collective-permute-start(bf16[2,2,184,128]{3,2,1,0:T(8,128)(2,1)S(1)} %waves.5), channel_id=1, source_target_pairs={{0,64},{64,0},{1,65},{65,1},{2,66},{66,2},{3,67},{67,3},{4,68},{68... | collective-permute-start | bytes 565256 | tf_op jit(solution)/shard_map/ppermute | solution.py:485
  73.0 1.8 %waves.6 = (bf16[1,2,184,128]{3,2,1,0:T(8,128)(2,1)S(1)}, f32[1,2,184,128]{3,2,1,0:T(8,128)S(1)}) custom-call(s32[1]{0:T(128)} %bitcast.1.half_ref.refs_0_, bf16[2,2,368,720]{3,2,1,0:T(8,128)(2,1)S(1)} %copy-done, bf16[1,192,720]{2,1,0:T(8,128)(2,1)S(1)} %copy-done.3, bf16[1,216,640]{2,1,0:T(8,128)(2,1)} %collective-permute-done.4.got_ref, ...), custom_call_target="tpu_custom_call" | custom-call | tf_op jit(solution)/shard_map/waves/pallas_call | solution.py:262
  74.8 0.9 %collective-permute-start.6 = (bf16[1,2,184,128]{3,2,1,0:T(8,128)(2,1)S(1)}, bf16[1,2,184,128]{3,2,1,0:T(8,128)(2,1)S(1)}, u32[]{:S(2)}, u32[]{:S(2)}) collective-permute-start(bf16[1,2,184,128]{3,2,1,0:T(8,128)(2,1)S(1)} %get-tuple-element.39), channel_id=1, source_target_pairs={{0,64},{64,0},{1,65},{65,1},{2,66},{66,2},{3,67},{67,3},{4,68},{68... | collective-permute-start | bytes 282632 | tf_op jit(solution)/shard_map/ppermute | solution.py:485
  75.7 1.1 %collective-permute-start.1 = (f32[8,128]{1,0:T(8,128)S(1)}, f32[8,128]{1,0:T(8,128)S(1)}, u32[]{:S(2)}, u32[]{:S(2)}) collective-permute-start(f32[8,128]{1,0:T(8,128)S(1)} %get-tuple-element.29._.refs_2_), channel_id=1, source_target_pairs={{0,192},{64,128},{128,64},{192,0},{1,193},{65,129},{129,65},{193,1... | collective-permute-start | bytes 12296 | tf_op jit(solution)/shard_map/ppermute | solution.py:523
  76.8 0.8 waves.4.refs_4_.refs_1_
  77.6 2.9 %collective-permute-done.1.refs_3_ = f32[8,128]{1,0:T(8,128)S(1)} collective-permute-done((f32[8,128]{1,0:T(8,128)S(1)}, f32[8,128]{1,0:T(8,128)S(1)}, u32[]{:S(2)}, u32[]{:S(2)}) %collective-permute-start.1) | collective-permute-done | bytes 4128 | tf_op jit(solution)/shard_map/ppermute | solution.py:523
  80.5 0.8 shard_map.105
  81.3 1.2 %join.2 = (f32[5,360,128]{2,1,0:T(8,128)}, f32[5,360,128]{2,1,0:T(8,128)}) custom-call(s32[1]{0:T(128)} %bitcast.1.half_ref.refs_0_, f32[1,2,184,128]{3,2,1,0:T(8,128)S(1)} %get-tuple-element.35.refs_1_, f32[2,2,184,128]{3,2,1,0:T(8,128)S(1)} %get-tuple-element.38.refs_2_, bf16[1,2,184,128]{3,2,1,0:T(8,128)(2,1)S(1)} %collective-permute-done.6.refs_3_, ...), custom_call_target="tpu_custom_call" | custom-call | tf_op jit(solution)/shard_map/join/pallas_call | solution.py:315
  82.5 1.0 %join.3 = (f32[5,360,128]{2,1,0:T(8,128)}, f32[5,360,128]{2,1,0:T(8,128)}) custom-call(s32[1]{0:T(128)} %bitcast.1.half_ref.refs_0_, f32[2,2,184,128]{3,2,1,0:T(8,128)S(1)} %waves.4.refs_4_.refs_1_, bf16[2,2,184,128]{3,2,1,0:T(8,128)(2,1)S(1)} %collective-permute-done.3.refs_2_, ...), custom_call_target="tpu_custom_call", output_to_operand_aliasing={{0}: (3, {}), {1}: (4, {})} | custom-call | tf_op jit(solution)/shard_map/join/pallas_call | solution.py:315
  (20 shorter events, 0.1 us)
Async XLA Ops:
  3.7 6.4 %copy-start.4 = (f32[10,128]{1,0:T(8,128)S(1)}, f32[10,128]{1,0:T(8,128)}, u32[]{:S(2)}) copy-start(f32[10,128]{1,0:T(8,128)} %get-tuple-element.25.refs_1_.refs_5_) | copy-start | bytes 15364
  3.7 36.0 %copy-start.5 = (f32[5,4,32]{2,1,0:T(4,128)S(1)}, f32[5,4,32]{2,1,0:T(4,128)}, u32[]{:S(2)}) copy-start(f32[5,4,32]{2,1,0:T(4,128)} %refs_4_.2) | copy-start | bytes 7684
  3.7 36.0 %copy-start.6 = (f32[32]{0:T(128)S(1)}, f32[32]{0:T(128)}, u32[]{:S(2)}) copy-start(f32[32]{0:T(128)} %param.11) | copy-start | bytes 388
  3.7 62.8 %copy-start = (bf16[2,2,368,720]{3,2,1,0:T(8,128)(2,1)S(1)}, bf16[2,2,368,720]{3,2,1,0:T(8,128)(2,1)}, u32[]{:S(2)}) copy-start(bf16[2,2,368,720]{3,2,1,0:T(8,128)(2,1)} %constant.29.clone.table_ref) | copy-start | bytes 6359044
  7.1 63.8 %copy-start.1 = (bf16[2,192,720]{2,1,0:T(8,128)(2,1)S(1)}, bf16[2,192,720]{2,1,0:T(8,128)(2,1)}, u32[]{:S(2)}) copy-start(bf16[2,192,720]{2,1,0:T(8,128)(2,1)} %get-tuple-element.30.own_ref) | copy-start | bytes 1658884
  7.1 59.4 %collective-permute-start.5 = (bf16[2,216,640]{2,1,0:T(8,128)(2,1)}, bf16[2,216,640]{2,1,0:T(8,128)(2,1)}, u32[]{:S(2)}, u32[]{:S(2)}) collective-permute-start(bf16[2,216,640]{2,1,0:T(8,128)(2,1)} %get-tuple-element.37), channel_id=1, source_target_pairs={{0,64},{64,0},{1,65},{65,1},{2,66},{66,2},{3,67},{67,3},{4,68},{68... | collective-permute-start | bytes 1658888 | tf_op jit(solution)/shard_map/ppermute | solution.py:485
  8.0 62.9 %collective-permute-start.2 = (bf16[2,216,640]{2,1,0:T(8,128)(2,1)}, bf16[2,216,640]{2,1,0:T(8,128)(2,1)S(1)}, u32[]{:S(2)}, u32[]{:S(2)}) collective-permute-start(bf16[2,216,640]{2,1,0:T(8,128)(2,1)} %get-tuple-element.31), channel_id=1, source_target_pairs={{0,64},{64,0},{1,65},{65,1},{2,66},{66,2},{3,67},{67,3},{4,68},{68... | collective-permute-start | bytes 1658888 | tf_op jit(solution)/shard_map/ppermute | solution.py:485
  9.2 63.8 %collective-permute-start.4 = (bf16[1,216,640]{2,1,0:T(8,128)(2,1)}, bf16[1,216,640]{2,1,0:T(8,128)(2,1)}, u32[]{:S(2)}, u32[]{:S(2)}) collective-permute-start(bf16[1,216,640]{2,1,0:T(8,128)(2,1)} %get-tuple-element.34), channel_id=1, source_target_pairs={{0,64},{64,0},{1,65},{65,1},{2,66},{66,2},{3,67},{67,3},{4,68},{68... | collective-permute-start | bytes 829448 | tf_op jit(solution)/shard_map/ppermute | solution.py:485
  10.0 29.6 %collective-permute-start = (f32[10,128]{1,0:T(8,128)S(1)}, f32[10,128]{1,0:T(8,128)S(1)}, u32[]{:S(2)}, u32[]{:S(2)}) collective-permute-start(f32[10,128]{1,0:T(8,128)S(1)} %copy-done.4), channel_id=1, source_target_pairs={{0,64},{64,0},{1,65},{65,1},{2,66},{66,2},{3,67},{67,3},{4,68},{68... | collective-permute-start | bytes 15368 | tf_op jit(solution)/shard_map/ppermute | solution.py:485
  66.5 1.1 %copy-start.2 = (bf16[2,192,720]{2,1,0:T(8,128)(2,1)S(1)}, bf16[2,192,720]{2,1,0:T(8,128)(2,1)}, u32[]{:S(2)}) copy-start(bf16[2,192,720]{2,1,0:T(8,128)(2,1)} %get-tuple-element.36.own_ref) | copy-start | bytes 1658884
  70.0 3.0 %copy-start.3 = (bf16[1,192,720]{2,1,0:T(8,128)(2,1)S(1)}, bf16[1,192,720]{2,1,0:T(8,128)(2,1)}, u32[]{:S(2)}) copy-start(bf16[1,192,720]{2,1,0:T(8,128)(2,1)} %get-tuple-element.33.own_ref) | copy-start | bytes 829444
  70.0 11.3 %collective-permute-start.7 = (bf16[2,2,184,128]{3,2,1,0:T(8,128)(2,1)S(1)}, bf16[2,2,184,128]{3,2,1,0:T(8,128)(2,1)S(1)}, u32[]{:S(2)}, u32[]{:S(2)}) collective-permute-start(bf16[2,2,184,128]{3,2,1,0:T(8,128)(2,1)S(1)} %get-tuple-element.40), channel_id=1, source_target_pairs={{0,64},{64,0},{1,65},{65,1},{2,66},{66,2},{3,67},{67,3},{4,68},{68... | collective-permute-start | bytes 565256 | tf_op jit(solution)/shard_map/ppermute | solution.py:485
  71.7 10.8 %collective-permute-start.3 = (bf16[2,2,184,128]{3,2,1,0:T(8,128)(2,1)S(1)}, bf16[2,2,184,128]{3,2,1,0:T(8,128)(2,1)S(1)}, u32[]{:S(2)}, u32[]{:S(2)}) collective-permute-start(bf16[2,2,184,128]{3,2,1,0:T(8,128)(2,1)S(1)} %waves.5), channel_id=1, source_target_pairs={{0,64},{64,0},{1,65},{65,1},{2,66},{66,2},{3,67},{67,3},{4,68},{68... | collective-permute-start | bytes 565256 | tf_op jit(solution)/shard_map/ppermute | solution.py:485
  74.8 6.5 %collective-permute-start.6 = (bf16[1,2,184,128]{3,2,1,0:T(8,128)(2,1)S(1)}, bf16[1,2,184,128]{3,2,1,0:T(8,128)(2,1)S(1)}, u32[]{:S(2)}, u32[]{:S(2)}) collective-permute-start(bf16[1,2,184,128]{3,2,1,0:T(8,128)(2,1)S(1)} %get-tuple-element.39), channel_id=1, source_target_pairs={{0,64},{64,0},{1,65},{65,1},{2,66},{66,2},{3,67},{67,3},{4,68},{68... | collective-permute-start | bytes 282632 | tf_op jit(solution)/shard_map/ppermute | solution.py:485
  75.7 4.8 %collective-permute-start.1 = (f32[8,128]{1,0:T(8,128)S(1)}, f32[8,128]{1,0:T(8,128)S(1)}, u32[]{:S(2)}, u32[]{:S(2)}) collective-permute-start(f32[8,128]{1,0:T(8,128)S(1)} %get-tuple-element.29._.refs_2_), channel_id=1, source_target_pairs={{0,192},{64,128},{128,64},{192,0},{1,193},{65,129},{129,65},{193,1... | collective-permute-start | bytes 12296 | tf_op jit(solution)/shard_map/ppermute | solution.py:523
